TPU v7x, 32 devices: a whole 2x2x4 slice. The times are simulated.
32 devices in a mesh: front: 8 (over z, y), row: 2 (over core), col: 2 (over x).
Axes of the slice: x: 2, y: 2, z: 4, core: 2. Of those that a mesh axis runs over, the one named last changes fastest.
Arguments:
- bounds: int32 [8], P('front'), may hold values from 3072 to 5120, as said below
- block_map: int32 [8, 40], P('front', 'row'), may hold values from 0 to 383, as said below
- pivot_inverse: bfloat16 [8, 1024, 1024], P('front', 'col', 'row'), may hold values from -0.1875 to 0.1875
- upper_block: bfloat16 [8, 1024, 5120], P('front', 'row', 'col'), may hold values from -0.078125 to 0.078125
- lower_block: bfloat16 [8, 5120, 1024], P('front', 'row', 'col'), may hold values from -0.1875 to 0.1875
- trailing_block: bfloat16 [8, 5120, 5120], P('front', 'row', 'col'), may hold values from -0.078125 to 0.078125
- sketch: bfloat16 [5120, 512], P('col'), may hold values from -6 to 6
- basis: bfloat16 [8, 6144, 512], P('front', 'row'), may hold values from -0.078125 to 0.078125
Outputs:
- coefficients: float32 [8, 512, 512], P('front', None, 'col')
- residual: float32 [8, 6144, 512], P('front', 'row', 'col')
Inputs may be any that keep to these rules, and one draw needn't show every extreme that they name: `bounds`: each is a multiple of 128; some front has exactly 5120. `block_map`: entries for blocks at or beyond a front's boundary are ignored. Within one front all entries are distinct. Owner (g, r) holds parent blocks g * 48 + r * 24 to g * 48 + (r + 1) * 24 - 1; an entry held by the device at index r of row names a block of an owner with the same r. Among the 20 entries held by one device, at most 3 name blocks of one owner, and some device has exactly 3 for some owner.
All inputs are finite; a program needn't handle non-finite values.
Results may differ from a plain program's by a relative error of at most 0.0042.
Values may be sent and summed in bfloat16 or wider, within the bound.
No kernel may reach another device: no remote copies, remote signals or barrier semaphores. Data moves between devices by JAX's collectives and lax.ppermute only.
A program may use at most 128 MiB of HBM per device.

v0:
```python
import jax
import jax.numpy as jnp
from jax import lax
from jax.sharding import PartitionSpec as P

BLOCK = 128


def extend_add(blocks, targets, live_rows, per_device):
    dest_count = lax.axis_size("front")
    row_count = lax.axis_size("row")
    capacity = (blocks.shape[0] + dest_count - 1) // dest_count
    block_height = blocks.shape[1]
    lane_width = blocks.shape[2]
    destination = targets // (row_count * per_device)
    local_block = targets % per_device
    dest_hits = (
        destination[:, None] == jnp.arange(dest_count, dtype=jnp.int32)[None, :]
    ) & live_rows[:, None]
    dest_counts = dest_hits.astype(jnp.int32)
    earlier = jnp.cumsum(dest_counts, axis=0) - dest_counts
    slot_rank = jnp.sum(earlier * dest_counts, axis=1)
    slot_index = destination * capacity + slot_rank
    chosen = (
        slot_index[None, :] == jnp.arange(dest_count * capacity, dtype=jnp.int32)[:, None]
    ) & live_rows[None, :]
    outgoing = jnp.einsum(
        "ps,sbw->pbw", chosen.astype(jnp.float32), blocks, precision=lax.Precision.HIGHEST
    )
    slot_tags = jnp.where(
        jnp.any(chosen, axis=1),
        jnp.sum(jnp.where(chosen, local_block[None, :], 0), axis=1),
        per_device,
    )
    incoming, incoming_tags = (
        lax.all_to_all(
            outgoing.reshape(dest_count, capacity, block_height, lane_width),
            "front",
            split_axis=0,
            concat_axis=0,
            tiled=True,
        ),
        lax.all_to_all(
            slot_tags.reshape(dest_count, capacity),
            "front",
            split_axis=0,
            concat_axis=0,
            tiled=True,
        ),
    )
    incoming = incoming.reshape(-1, block_height, lane_width)
    incoming_tags = incoming_tags.reshape(-1)
    owner_hits = (
        jnp.arange(per_device, dtype=jnp.int32)[:, None] == incoming_tags[None, :]
    ).astype(jnp.float32)
    return jnp.einsum("qs,sbw->qbw", owner_hits, incoming, precision=lax.Precision.HIGHEST)


def body(bounds, block_map, pivot_inverse, upper_block, lower_block, trailing_block, sketch, basis):
    row_index = lax.axis_index("row")
    col_index = lax.axis_index("col")
    col_width = sketch.shape[0]
    block_rows = block_map.shape[1]
    col_positions = col_index * col_width + jnp.arange(col_width, dtype=jnp.int32)
    block_starts = (row_index * block_rows + jnp.arange(block_rows, dtype=jnp.int32)) * BLOCK
    boundary = bounds[0]
    masked = sketch * (col_positions < boundary).astype(jnp.bfloat16)[:, None]
    upper_term = jnp.dot(upper_block[0], masked, preferred_element_type=jnp.float32)
    pivot_cols = lax.psum_scatter(upper_term, "col", scatter_dimension=1, tiled=True).astype(
        jnp.bfloat16
    )
    pivot_rows = lax.all_gather(pivot_cols, "col", axis=1, tiled=True)
    solved = lax.psum(
        jnp.dot(pivot_inverse[0], pivot_rows, preferred_element_type=jnp.float32), "row"
    ).astype(jnp.bfloat16)
    combined = jnp.dot(trailing_block[0], masked, preferred_element_type=jnp.float32) - jnp.dot(
        lower_block[0], solved, preferred_element_type=jnp.float32
    )
    combined = lax.psum_scatter(combined, "col", scatter_dimension=1, tiled=True)
    sketched = combined.reshape(block_rows, BLOCK, combined.shape[1])
    alive_rows = block_starts < boundary
    per_device = basis.shape[1] // BLOCK
    parent = extend_add(sketched, block_map.reshape(-1), alive_rows, per_device)
    sketch_rows = parent.reshape(-1, parent.shape[2])
    local_basis = basis[0]
    coeff_part = lax.dot_general(
        local_basis,
        sketch_rows.astype(jnp.bfloat16),
        (((0,), (0,)), ((), ())),
        preferred_element_type=jnp.float32,
    )
    coefficients = lax.psum(coeff_part, "row")
    residual = sketch_rows - jnp.dot(
        local_basis, coefficients.astype(jnp.bfloat16), preferred_element_type=jnp.float32
    )
    return (coefficients[None], residual[None])


def solution(mesh):
    placed = (
        P("front"),
        P("front", "row"),
        P("front", "col", "row"),
        P("front", "row", "col"),
        P("front", "row", "col"),
        P("front", "row", "col"),
        P("col", None),
        P("front", "row", None),
    )
    return jax.shard_map(
        body,
        mesh=mesh,
        in_specs=placed,
        out_specs=(P("front", None, "col"), P("front", "row", "col")),
        check_vma=False,
    )
```

profile of v0, /device:TPU:0, one launch (start us, length us, event | category | flops | bytes accessed | tf_op | source)
XLA Modules:
  0.0 259.1 jit_solution(1622142507018784711)
XLA Ops:
  7.2 0.0 copy-start
  7.2 0.0 reduce-scatter.3.cloned.1.call-start
  8.0 5.6 %fusion.17 = f32[512,512]{0,1:T(8,128)} fusion(bf16[1,512,2560]{2,1,0:T(8,128)(2,1)} %param.11, bf16[2560,512]{1,0:T(8,128)(2,1)} %param.14, bf16[2560]{0:T(1024)(128)(2,1)S(1)} %fusion.36), kind=kOutput, calls=%fused_computation.19 | convolution fusion | flops 1343488000 | bytes 6296576 | tf_op jit(solution)/shard_map/dot_general | solution.py:68
  13.6 0.0 reduce-scatter.3.cloned.1.call-update
  13.7 0.0 reduce-scatter.5.cloned.1.call-start
  13.7 13.2 %fusion = f32[512,2560]{1,0:T(8,128)} fusion(bf16[1,2560,2560]{2,1,0:T(8,128)(2,1)} %param.13, bf16[2560,512]{1,0:T(8,128)(2,1)} %param.14, bf16[2560]{0:T(1024)(128)(2,1)S(1)} %fusion.36), kind=kOutput, calls=%fused_computation | convolution fusion | flops 6712197120 | bytes 20976640 | tf_op jit(solution)/shard_map/dot_general | solution.py:76
  26.9 10.0 %reduce-scatter.3.cloned.1.call-done = f32[512,256]{0,1:T(8,128)} async-done(((f32[512,512]{0,1:T(8,128)}), f32[512,256]{0,1:T(8,128)}) %reduce-scatter.3.cloned.1.call-update) | async-done | bytes 524304 | tf_op jit(solution)/shard_map/reduce_scatter | solution.py:69
  36.9 1.1 convert_element_type.29
  38.0 8.5 %all_gather.3 = bf16[512,512]{0,1:T(8,128)(2,1)S(1)} all-gather(bf16[512,256]{0,1:T(8,128)(2,1)S(1)} %convert_element_type.29), channel_id=1, replica_groups=mesh['front'=8,'row'=2,'col'=2] {'col'}, dimensions={1}, use_global_device_ids=true | all-gather | bytes 786432 | tf_op jit(solution)/shard_map/all_gather | solution.py:72
  46.5 2.5 convolution_bitcast_fusion.1
  49.0 7.2 %all-reduce.4 = bf16[512,512]{0,1:T(8,128)(2,1)} all-reduce(f32[512,512]{0,1:T(8,128)} %convolution_bitcast_fusion.1), channel_id=1, replica_groups=mesh['front'=8,'row'=2,'col'=2] {'row'}, use_global_device_ids=true, to_apply=%region_5.6 | all-reduce | flops 262144 | bytes 1572864 | tf_op jit(solution)/shard_map/psum | solution.py:73
  56.3 7.3 %subtract_bitcast_fusion = f32[2560,512]{0,1:T(8,128)} fusion(f32[512,2560]{1,0:T(8,128)} %fusion, bf16[1,2560,512]{2,1,0:T(8,128)(2,1)} %param.12, bf16[512,512]{0,1:T(8,128)(2,1)} %all-reduce.4), kind=kOutput, calls=%fused_computation.2 | convolution fusion | flops 1343488000 | bytes 13631488 | tf_op jit(solution)/shard_map/dot_general | solution.py:76
  63.6 0.0 copy-start.1
  63.6 0.0 reduce-scatter.5.cloned.1.call-update
  63.6 0.6 copy-done.1
  64.2 0.1 fusion.33
  64.4 0.2 select_reduce_fusion.1
  64.6 0.1 fusion.35
  64.7 0.1 select_reduce_fusion
  64.8 0.7 select_n.44
  65.4 5.5 %all-to-all-start = ((s32[8,1,3]{2,1,0:T(1,128)}), s32[8,1,3]{2,1,0:T(1,128)S(1)}, u32[]{:S(2)}, u32[]{:S(2)}) async-start(s32[8,1,3]{2,1,0:T(1,128)} %bitcast.6), calls=%async_computation | async-start | bytes 8192 | tf_op jit(solution)/shard_map/all_to_all | solution.py:43
  71.0 58.6 %reduce-scatter.5.cloned.1.call-done = f32[2560,256]{0,1:T(8,128)} async-done(((f32[2560,512]{0,1:T(8,128)}), f32[2560,256]{0,1:T(8,128)}) %reduce-scatter.5.cloned.1.call-update) | async-done | bytes 2621456 | tf_op jit(solution)/shard_map/reduce_scatter | solution.py:79
  129.6 3.2 %copy.33 = f32[2560,256]{1,0:T(8,128)} copy(f32[2560,256]{0,1:T(8,128)} %reduce-scatter.5.cloned.1.call-done) | data formatting | bytes 5242880 | tf_op jit(solution)/shard_map/reduce_scatter | solution.py:79
  132.8 4.7 %fusion.7 = f32[8,3,128,256]{3,0,2,1:T(8,128)S(1)} fusion(f32[20,128,256]{2,1,0:T(8,128)} %bitcast.74, s32[8,3]{0,1:T(4,128)S(1)} %multiply_add_fusion, s32[20]{0:T(128)S(1)} %get-tuple-element.13, pred[20]{0:T(512)(128)(4,1)S(1)} %multiply_compare_fusion), kind=kOutput, calls=%fused_computation.9 | convolution fusion | flops 188744640 | bytes 5767364 | tf_op jit(solution)/shard_map/ps,sbw->pbw/dot_general | solution.py:27
  137.5 2.6 %copy.35 = f32[8,3,128,256]{3,2,1,0:T(8,128)} copy(f32[8,3,128,256]{3,0,2,1:T(8,128)S(1)} %fusion.7) | data formatting | bytes 6291456 | tf_op jit(solution)/shard_map/ps,sbw->pbw/dot_general | solution.py:27
  140.1 0.0 all-to-all-done
  140.1 5.5 %all-to-all-start.1 = ((f32[8,3,128,256]{3,2,1,0:T(8,128)}), f32[8,3,128,256]{3,2,1,0:T(8,128)}, u32[]{:S(2)}, u32[]{:S(2)}) async-start(f32[8,3,128,256]{3,2,1,0:T(8,128)} %copy.35), calls=%async_computation.3 | async-start | bytes 6291456 | tf_op jit(solution)/shard_map/all_to_all | solution.py:36
  145.7 0.0 all-reduce.3.cloned.1.call-start
  145.7 0.5 broadcast.130
  146.2 0.7 reduce.3
  146.9 0.1 eq.70
  147.0 69.3 %all-to-all-done.1 = f32[8,3,128,256]{3,2,1,0:T(8,128)} async-done(((f32[8,3,128,256]{3,2,1,0:T(8,128)}), f32[8,3,128,256]{3,2,1,0:T(8,128)}, u32[]{:S(2)}, u32[]{:S(2)}) %all-to-all-start.1) | async-done | bytes 3145760 | tf_op jit(solution)/shard_map/all_to_all | solution.py:36
  216.3 6.8 %fusion.48 = (bf16[24,128,256]{2,0,1:T(8,128)(2,1)S(1)}, f32[24,128,256]{2,0,1:T(8,128)}) fusion(f32[24,128,256]{2,1,0:T(8,128)} %bitcast.19, s32[24]{0:T(128)S(1)} %eq.70), kind=kOutput, calls=%fused_computation.58 | convolution fusion | flops 227279424 | bytes 7864416 | tf_op jit(solution)/shard_map/qs,sbw->qbw/dot_general | solution.py:56
  223.1 0.3 copy.37
  223.5 0.0 copy-done
  223.5 1.8 fusion.24
  225.3 0.0 all-reduce.3.cloned.1.call-update
  225.3 4.6 %copy.38 = f32[24,128,256]{2,1,0:T(8,128)} copy(f32[24,128,256]{2,0,1:T(8,128)} %get-tuple-element.15) | data formatting | bytes 6291456 | tf_op jit(solution)/shard_map/qs,sbw->qbw/dot_general | solution.py:56
  229.9 3.6 %copy.39 = f32[3072,256]{0,1:T(8,128)} copy(f32[3072,256]{1,0:T(8,128)} %bitcast.75) | data formatting | bytes 6291456 | tf_op jit(solution)/shard_map/reshape | solution.py:84
  233.5 8.7 %all-reduce.3.cloned.1.call-done = f32[512,256]{0,1:T(8,128)} async-done(((f32[512,256]{0,1:T(8,128)}), f32[512,256]{0,1:T(8,128)}) %all-reduce.3.cloned.1.call-update) | async-done | bytes 524304 | tf_op jit(solution)/shard_map/psum | solution.py:92
  242.2 2.0 copy.40
  244.3 4.7 %fusion.3 = f32[1,3072,256]{1,2,0:T(8,128)} fusion(f32[3072,256]{0,1:T(8,128)} %copy.39, bf16[1,3072,512]{2,1,0:T(8,128)(2,1)S(1)} %copy-done, f32[512,256]{0,1:T(8,128)} %all-reduce.3.cloned.1.call-done), kind=kOutput, calls=%fused_computation.5 | convolution fusion | flops 806223872 | bytes 9961472 | tf_op jit(solution)/shard_map/dot_general | solution.py:93
  249.0 3.5 %copy.41 = f32[1,3072,256]{2,1,0:T(8,128)} copy(f32[1,3072,256]{1,2,0:T(8,128)} %fusion.3) | data formatting | bytes 6291456
  (7 shorter events, 0.1 us)
Async XLA Ops:
  7.2 216.3 %copy-start = (bf16[1,3072,512]{2,1,0:T(8,128)(2,1)S(1)}, bf16[1,3072,512]{2,1,0:T(8,128)(2,1)}, u32[]{:S(2)}) copy-start(bf16[1,3072,512]{2,1,0:T(8,128)(2,1)} %param.15) | copy-start | bytes 9437188
  7.2 29.7 %reduce-scatter.3.cloned.1.call-start = ((), (), s32[]{:S(2)}) async-start(), calls=%async_computation.4 | async-start | bytes 1572864 | tf_op jit(solution)/shard_map/reduce_scatter | solution.py:69
  13.7 115.9 %reduce-scatter.5.cloned.1.call-start = ((), (), s32[]{:S(2)}) async-start(), calls=%async_computation.5 | async-start | bytes 7864320 | tf_op jit(solution)/shard_map/reduce_scatter | solution.py:79
  63.6 0.7 copy-start.1
  65.4 74.7 %all-to-all-start = ((s32[8,1,3]{2,1,0:T(1,128)}), s32[8,1,3]{2,1,0:T(1,128)S(1)}, u32[]{:S(2)}, u32[]{:S(2)}) async-start(s32[8,1,3]{2,1,0:T(1,128)} %bitcast.6), calls=%async_computation | async-start | bytes 8192 | tf_op jit(solution)/shard_map/all_to_all | solution.py:43
  140.1 76.2 %all-to-all-start.1 = ((f32[8,3,128,256]{3,2,1,0:T(8,128)}), f32[8,3,128,256]{3,2,1,0:T(8,128)}, u32[]{:S(2)}, u32[]{:S(2)}) async-start(f32[8,3,128,256]{3,2,1,0:T(8,128)} %copy.35), calls=%async_computation.3 | async-start | bytes 6291456 | tf_op jit(solution)/shard_map/all_to_all | solution.py:36
  145.7 96.5 %all-reduce.3.cloned.1.call-start = ((), (), s32[]{:S(2)}) async-start(), calls=%async_computation.6 | async-start | bytes 1048576 | tf_op jit(solution)/shard_map/psum | solution.py:92
Sparse Core Ops, SparseCore 0:
  13.8 23.0 reduce-scatter.2
  63.7 65.8 reduce-scatter.4
  225.5 16.7 all-reduce.2
where the time goes:
time: 260 us; the launch traced here: 259 us
  waiting for transfers between devices  147 us (57%)
  matrix products  46.7 us (18%)
  local copies, waits for them, and re-layouts  21.8 us (8%)
  blocking collectives  15.8 us (6%)
  between operations  14.6 us (6%)
  starting transfers between devices  11.2 us (4%)
    all_to_all x1, waiting for transfers between devices, extend_add(): lax.all_to_all(outgoing.reshape(dest_count, capacity, block_height, lane_...  69.3 us
    reduce_scatter x1, waiting for transfers between devices, body(): lax.psum_scatter(combined, 'col', scatter_dimension=1, tiled=True)  58.6 us
    dot_general x1, matrix products, body(): jnp.dot(trailing_block[0], masked, preferred_element_type=jnp.float32)  13.2 us
    reduce_scatter x1, waiting for transfers between devices, body(): lax.psum_scatter(upper_term, 'col', scatter_dimension=1, tiled=True)  9.97 us
    psum x1, waiting for transfers between devices, body(): coefficients = lax.psum(coeff_part, 'row')  8.74 us
    all_gather x1, blocking collectives, body(): pivot_rows = lax.all_gather(pivot_cols, 'col', axis=1, tiled=True)  8.54 us
    dot_general x1, matrix products, body(): jnp.dot(lower_block[0], solved, preferred_element_type=jnp.float32)  7.31 us
    psum x1, blocking collectives, body(): lax.psum(jnp.dot(pivot_inverse[0], pivot_rows, preferred_element_type=jnp...  7.25 us
  transfers between devices with their start and end apart: 5, of which 4 were waited for; matrix products, arithmetic and copies ran while one was open for 13% of the time, Pallas kernels for 0%

commit v1 on v0

v1 whole, which is shorter than its diff:
```python
import functools

import jax
import jax.numpy as jnp
from jax import lax
from jax.experimental import pallas as pl
from jax.experimental.pallas import tpu as pltpu
from jax.sharding import PartitionSpec as P


BLOCK = 128
TAG_ROWS = 16
F32 = jnp.float32
BF16 = jnp.bfloat16
VMEM = pl.BlockSpec(memory_space=pltpu.VMEM)
SMEM = pl.BlockSpec(memory_space=pltpu.SMEM)
MIB = 1024 * 1024
PIVOT_LIMIT = 16 * MIB
TRAILING_LIMIT = 46 * MIB


def dot(a, b):
    return jnp.dot(a, b, preferred_element_type=F32)


def mask_halves(bound, first, col, sketch_ref, out_ref):
    depth, width = sketch_ref.shape
    half = width // 2
    limit = bound - first * depth
    at = lax.broadcasted_iota(jnp.int32, (depth, half), 0)
    for side in range(2):
        pick = col if side == 0 else 1 - col
        value = sketch_ref[:, pl.ds(pl.multiple_of(pick * half, half), half)]
        out_ref[:, side * half : (side + 1) * half] = jnp.where(at < limit, value.astype(F32), 0.0).astype(BF16)


def plan_kernel(row_count, per_device, cap, fronts, ids_ref, bound_ref, map_ref, source_ref, tag_ref, count_ref):
    me, row = ids_ref[0], ids_ref[1]
    blocks = map_ref.shape[0]
    slots = fronts * cap
    for i in range(fronts):
        count_ref[i] = 0
    for i in range(slots):
        source_ref[i] = 0
        tag_ref[i] = per_device

    def one(j, carry):
        value = map_ref[j]

        @pl.when((row * blocks + j) * BLOCK < bound_ref[0])
        def _():
            turn = lax.bitwise_xor(value // (row_count * per_device), me)
            rank = count_ref[turn]
            count_ref[turn] = rank + 1
            source_ref[turn * cap + rank] = j
            tag_ref[turn * cap + rank] = value % per_device

        return carry

    lax.fori_loop(0, blocks, one, 0)


def pivot_kernel(ids_ref, bound_ref, upper_ref, sketch_ref, own_ref, other_ref, kept_own_ref, kept_other_ref, masked_ref, sum_ref):
    step, steps = pl.program_id(0), pl.num_programs(0)
    half = sketch_ref.shape[1] // 2
    mask_halves(bound_ref[0], ids_ref[2] * steps + step, ids_ref[2], sketch_ref, masked_ref)
    value = dot(upper_ref[...], masked_ref[...])

    @pl.when(step == 0)
    def _():
        sum_ref[...] = value

    @pl.when(step > 0)
    def _():
        sum_ref[...] += value

    @pl.when(step == steps - 1)
    def _():
        kept_own_ref[...] = sum_ref[:, :half]
        own_ref[...] = sum_ref[:, :half].astype(BF16)
        kept_other_ref[...] = sum_ref[:, half:]
        other_ref[...] = sum_ref[:, half:].astype(BF16)


def trailing_kernel(trailing_ref, masked_ref, own_ref, other_ref):
    value = dot(trailing_ref[...], masked_ref[...])
    half = masked_ref.shape[1] // 2
    own_ref[...] = value[:, :half]
    other_ref[...] = value[:, half:]


def solve_kernel(inverse_ref, kept_ref, got_ref, out_ref):
    rows = (kept_ref[...] + got_ref[...].astype(F32)).astype(BF16)
    out_ref[...] = dot(inverse_ref[...], rows)


def schur_kernel(part_ref, got_ref, lower_ref, trailing_ref, out_ref):
    solved = (part_ref[...] + got_ref[...]).astype(BF16)
    height = lower_ref.shape[0]
    step = 4 * BLOCK if height % (4 * BLOCK) == 0 else BLOCK
    for start in range(0, height, step):
        rows = slice(start, start + step)
        out_ref[rows, :] = (trailing_ref[rows, :] - dot(lower_ref[rows, :], solved)).astype(out_ref.dtype)


def packed_schur_kernel(groups, cap, source_ref, part_ref, got_ref, lower_ref, trailing_ref, *rest):
    outs, sum_ref = rest[:-1], rest[-1]
    schur_kernel(part_ref, got_ref, lower_ref, trailing_ref, sum_ref)
    for out, turns in zip(outs, groups):
        for i, turn in enumerate(turns):
            for s in range(cap):
                at = pl.multiple_of(source_ref[turn * cap + s] * BLOCK, BLOCK)
                start = (i * cap + s) * BLOCK
                out[start : start + BLOCK, :] = sum_ref[pl.ds(at, BLOCK), :]


def add_kernel(turns, cap, source_ref, tag_ref, own_ref, got_ref, *outs):
    size = cap * BLOCK
    width = own_ref.shape[1]
    index = lax.broadcasted_iota(jnp.int32, (TAG_ROWS, width), 0)
    for i, (turn, out) in enumerate(zip(turns, outs)):
        tags = jnp.zeros((TAG_ROWS, width), F32)
        for s in range(cap):
            at = pl.multiple_of(source_ref[turn * cap + s] * BLOCK, BLOCK)
            start = i * size + s * BLOCK
            value = own_ref[pl.ds(at, BLOCK), :] + got_ref[start : start + BLOCK, :].astype(F32)
            out[s * BLOCK : (s + 1) * BLOCK, :] = value.astype(BF16)
            tags = jnp.where(index == s, tag_ref[turn * cap + s].astype(F32), tags)
        out[size:, :] = tags.astype(BF16)


def add_pieces(per_device, cap, pieces, parent_ref):
    size = cap * BLOCK
    for piece in pieces:
        tile = piece[size : size + TAG_ROWS, :BLOCK].astype(F32)
        index = lax.broadcasted_iota(jnp.int32, tile.shape, 0)
        for s in range(cap):
            tag = jnp.max(jnp.where(index == s, tile, 0.0)).astype(jnp.int32)

            @pl.when(tag < per_device)
            def _():
                at = pl.ds(pl.multiple_of(tag * BLOCK, BLOCK), BLOCK)
                parent_ref[at, :] += piece[s * BLOCK : (s + 1) * BLOCK, :].astype(F32)


def early_kernel(per_device, cap, *refs):
    pieces, parent_ref = refs[:-1], refs[-1]
    parent_ref[...] = jnp.zeros_like(parent_ref)
    add_pieces(per_device, cap, pieces, parent_ref)


def late_kernel(per_device, cap, *refs):
    flipped_ref, pieces, (parent_ref, coeff_ref) = refs[0], refs[2:-2], refs[-2:]
    add_pieces(per_device, cap, pieces, parent_ref)
    coeff_ref[...] = dot(flipped_ref[...], parent_ref[...].astype(BF16))


def flip_kernel(basis_ref, out_ref):
    out_ref[...] = basis_ref[...].T


def residual_kernel(basis_ref, parent_ref, part_ref, got_ref, coeff_ref, out_ref):
    total = part_ref[...] + got_ref[...]

    @pl.when(pl.program_id(0) == 0)
    def _():
        coeff_ref[...] = total

    out_ref[...] = parent_ref[...] - dot(basis_ref[...], total.astype(BF16))


def swap(x, axis, turn=1):
    n = lax.axis_size(axis)
    return lax.ppermute(x, axis, [(i, i ^ turn) for i in range(n)])


def order_of(fronts):
    turns = []
    bit = fronts // 2
    while bit:
        turns += list(range(bit, 2 * bit))
        bit //= 2
    turns.append(0)
    cuts = [0, fronts // 8, fronts // 4, fronts // 2, fronts]
    return turns, [turns[a:b] for a, b in zip(cuts, cuts[1:])]


def call(kernel, operands, specs, outs, out_specs, flops, scratch=(), limit=None, **kw):
    space = 0
    for x in (*operands, *outs, *scratch):
        space += x.size * x.dtype.itemsize if hasattr(x, "size") else 0
    moved = sum(x.size * x.dtype.itemsize for x in (*operands, *outs))
    semantics = {"dimension_semantics": ("arbitrary",)} if "grid" in kw else {}
    return pl.pallas_call(
        kernel,
        out_shape=tuple(outs),
        in_specs=specs,
        out_specs=tuple(out_specs),
        scratch_shapes=[pltpu.VMEM(x.shape, x.dtype) if isinstance(x, jax.ShapeDtypeStruct) else x for x in scratch],
        compiler_params=pltpu.CompilerParams(vmem_limit_bytes=int(limit or space + 3 * MIB), **semantics),
        cost_estimate=pl.CostEstimate(flops=int(flops), bytes_accessed=int(moved), transcendentals=0),
        **kw,
    )(*operands)


def shape(rows, columns, dtype):
    return jax.ShapeDtypeStruct((rows, columns), dtype)


def program(bounds, block_map, pivot_inverse, upper_block, lower_block, trailing_block, sketch, basis):
    fronts, row_count = lax.axis_size("front"), lax.axis_size("row")
    assert fronts & (fronts - 1) == 0
    blocks = block_map.shape[1]
    per_device = basis.shape[1] // BLOCK
    cap = -(-blocks // fronts)
    depth, width = sketch.shape
    half = width // 2
    slots = fronts * cap
    size = cap * BLOCK
    ids = jnp.stack([lax.axis_index("front"), lax.axis_index("row"), lax.axis_index("col")]).astype(jnp.int32)
    inverse, upper, lower, trailing, basis = pivot_inverse[0], upper_block[0], lower_block[0], trailing_block[0], basis[0]
    height, _ = lower.shape
    tall = upper.shape[0]
    turns, groups = order_of(fronts)

    steps = 5 if depth % (5 * BLOCK) == 0 else 1
    part = depth // steps
    send_own, send_other, kept_own, kept_other, masked = call(
        pivot_kernel,
        (ids, bounds, upper, sketch),
        [
            SMEM,
            SMEM,
            pl.BlockSpec((tall, part), lambda k: (0, k)),
            pl.BlockSpec((part, width), lambda k: (k, 0)),
        ],
        (shape(tall, half, BF16),) * 2 + (shape(tall, half, F32),) * 2 + (shape(depth, width, BF16),),
        [pl.BlockSpec((tall, half), lambda k: (0, 0))] * 4 + [pl.BlockSpec((part, width), lambda k: (k, 0))],
        2 * upper.size * width,
        scratch=(shape(tall, width, F32),),
        limit=PIVOT_LIMIT,
        grid=(steps,),
    )
    got_other = swap(send_own, "col")
    got_own = swap(send_other, "col")

    source, tags = call(
        functools.partial(plan_kernel, row_count, per_device, cap, fronts),
        (ids, bounds, block_map.reshape(-1)),
        [SMEM] * 3,
        (jax.ShapeDtypeStruct((slots,), jnp.int32),) * 2,
        [SMEM] * 2,
        1e6,
        scratch=(pltpu.SMEM((fronts,), jnp.int32),),
    )

    tile = 4 * BLOCK if height % (4 * BLOCK) == 0 else BLOCK
    trail_own, trail_other = call(
        trailing_kernel,
        (trailing, masked),
        [pl.BlockSpec((tile, depth), lambda i: (i, 0)), pl.BlockSpec((depth, width), lambda i: (0, 0))],
        (shape(height, half, F32),) * 2,
        [pl.BlockSpec((tile, half), lambda i: (i, 0))] * 2,
        2 * trailing.size * width,
        limit=TRAILING_LIMIT,
        grid=(height // tile,),
    )

    def solve(kept, got):
        return call(solve_kernel, (inverse, kept, got), [VMEM] * 3, (shape(inverse.shape[0], half, F32),), [VMEM], 2 * inverse.size * half)[0]

    part_other = solve(kept_other, got_other)
    row_other = swap(part_other, "row")
    part_own = solve(kept_own, got_own)
    row_own = swap(part_own, "row")
    sums = call(
        functools.partial(packed_schur_kernel, groups, cap),
        (source, part_other, row_other, lower, trail_other),
        [SMEM] + [VMEM] * 4,
        tuple(shape(len(t) * size, half, BF16) for t in groups),
        [VMEM] * len(groups),
        2 * lower.size * half,
        scratch=(shape(height, half, BF16),),
    )
    arrived = [swap(x, "col") for x in sums]
    own = call(
        schur_kernel,
        (part_own, row_own, lower, trail_own),
        [VMEM] * 4,
        (shape(height, half, F32),),
        [VMEM],
        2 * lower.size * half,
    )[0]

    pieces = {}
    for g, members in enumerate(groups):
        made = call(
            functools.partial(add_kernel, members, cap),
            (source, tags, own, arrived[g]),
            [SMEM, SMEM, VMEM, VMEM],
            (shape(size + TAG_ROWS, half, BF16),) * len(members),
            [VMEM] * len(members),
            1e9,
        )
        for turn, piece in zip(members, made):
            pieces[turn] = swap(piece, "front", turn) if turn else piece

    rank = basis.shape[1]
    rows = per_device * BLOCK
    flipped = call(flip_kernel, (basis,), [VMEM], (shape(rank, rows, BF16),), [VMEM], 1e9)[0]
    late = groups[2]
    early = [t for t in turns if t not in late]
    parent = call(
        functools.partial(early_kernel, per_device, cap),
        [pieces[t] for t in early],
        [VMEM] * len(early),
        (shape(rows, half, F32),),
        [VMEM],
        1e9,
    )[0]
    parent, coeff = call(
        functools.partial(late_kernel, per_device, cap),
        [flipped, parent] + [pieces[t] for t in late],
        [VMEM] * (2 + len(late)),
        (shape(rows, half, F32), shape(rank, half, F32)),
        [VMEM] * 2,
        2 * basis.size * half,
        input_output_aliases={1: 0},
    )
    got = swap(coeff, "row")
    steps = 4 if per_device % 4 == 0 else 1
    tall = rows // steps
    coefficients, residual = call(
        residual_kernel,
        (basis, parent, coeff, got),
        [
            pl.BlockSpec((tall, rank), lambda i: (i, 0)),
            pl.BlockSpec((tall, half), lambda i: (i, 0)),
            pl.BlockSpec((rank, half), lambda i: (0, 0)),
            pl.BlockSpec((rank, half), lambda i: (0, 0)),
        ],
        (shape(rank, half, F32), shape(rows, half, F32)),
        [pl.BlockSpec((rank, half), lambda i: (0, 0)), pl.BlockSpec((tall, half), lambda i: (i, 0))],
        2 * basis.size * half,
        grid=(steps,),
        limit=20 * MIB,
    )
    return coefficients[None], residual[None]


def solution(mesh):
    placed = (
        P("front"),
        P("front", "row"),
        P("front", "col", "row"),
        P("front", "row", "col"),
        P("front", "row", "col"),
        P("front", "row", "col"),
        P("col", None),
        P("front", "row", None),
    )
    return jax.shard_map(
        program,
        mesh=mesh,
        in_specs=placed,
        out_specs=(P("front", None, "col"), P("front", "row", "col")),
        check_vma=False,
    )
```

time: 260 us -> 103 us (0.40)
  waiting for transfers between devices: 147 us -> 44.6 us
  matrix products: 46.7 us -> 0 us
  Pallas kernels: 0 us -> 29.1 us
  local copies, waits for them, and re-layouts: 21.8 us -> 3.5 us
  blocking collectives: 15.8 us -> 0 us
  between operations: 14.6 us -> 1.48 us
  starting transfers between devices: 11.2 us -> 24.1 us
    all_to_all x2 -> x0, waiting for transfers between devices: 69.3 us -> none  [the longest x1 69.3 us: extend_add(): lax.all_to_all(outgoing.reshape(dest_count, capacity, block_height, lane_...]
    reduce_scatter x2 -> x0, waiting for transfers between devices: 68.6 us -> none  [the longest x1 58.6 us: body(): lax.psum_scatter(combined, 'col', scatter_dimension=1, tiled=True)]
    dot_general x8 -> x0, matrix products: 46.7 us -> none  [the longest x1 13.2 us: body(): jnp.dot(trailing_block[0], masked, preferred_element_type=jnp.float32)]
    ppermute x0 -> x16, waiting for transfers between devices: none -> 44.6 us  [swap(): return lax.ppermute(x, axis, [(i, i ^ turn) for i in range(n)])]
    pallas_call x0 -> x15, Pallas kernels: none -> 29.1 us  [call(): pl.pallas_call(kernel, out_shape=tuple(outs), in_specs=specs, out_specs=t...]
    ppermute x0 -> x16, starting transfers between devices: none -> 24.1 us  [swap(): return lax.ppermute(x, axis, [(i, i ^ turn) for i in range(n)])]
    all_to_all x2 -> x0, starting transfers between devices: 11.1 us -> none  [the longest x1 5.53 us: extend_add(): lax.all_to_all(outgoing.reshape(dest_count, capacity, block_height, lane_...]
    psum x1 -> x0, waiting for transfers between devices: 8.74 us -> none  [body(): coefficients = lax.psum(coeff_part, 'row')]
  transfers between devices with their start and end apart: 5 -> 16, of which waited for: 4 -> 8; matrix products, arithmetic and copies ran while one was open for 13% -> 0% of each run, Pallas kernels for 0% -> 20%
where the time goes in v1:
time: 103 us
  waiting for transfers between devices  44.6 us (43%)
  Pallas kernels  29.1 us (28%)
  starting transfers between devices  24.1 us (23%)
  local copies, waits for them, and re-layouts  3.5 us (3%)
  between operations  1.48 us (1%)
    ppermute x16, waiting for transfers between devices, swap(): return lax.ppermute(x, axis, [(i, i ^ turn) for i in range(n)])  44.6 us
    pallas_call x15, Pallas kernels, call(): pl.pallas_call(kernel, out_shape=tuple(outs), in_specs=specs, out_specs=t...  29.1 us
    ppermute x16, starting transfers between devices, swap(): return lax.ppermute(x, axis, [(i, i ^ turn) for i in range(n)])  24.1 us
    unnamed x12, local copies, waits for them, and re-layouts  3.5 us
  transfers between devices with their start and end apart: 16, of which 8 were waited for; matrix products, arithmetic and copies ran while one was open for 0% of the time, Pallas kernels for 20%

profile of v1, /device:TPU:0, one launch (start us, length us, event | category | flops | bytes accessed | tf_op | source)
XLA Modules:
  0.0 102.8 jit_solution(11702552028450817533)
XLA Ops:
  1.3 0.1 pad_add_fusion.ids_ref
  1.4 0.0 copy-start.2
  1.4 1.7 %copy-done.2 = bf16[1,512,2560]{2,1,0:T(8,128)(2,1)S(1)} copy-done((bf16[1,512,2560]{2,1,0:T(8,128)(2,1)S(1)}, bf16[1,512,2560]{2,1,0:T(8,128)(2,1)}, u32[]{:S(2)}) %copy-start.2) | copy-done | bytes 2621464
  3.1 0.0 copy-start.3
  3.1 1.7 %copy-done.3 = bf16[2560,512]{1,0:T(8,128)(2,1)S(1)} copy-done((bf16[2560,512]{1,0:T(8,128)(2,1)S(1)}, bf16[2560,512]{1,0:T(8,128)(2,1)}, u32[]{:S(2)}) %copy-start.3) | copy-done | bytes 2621464
  4.8 0.0 copy-start.4
  4.8 3.7 %shard_map.97 = (bf16[512,256]{1,0:T(8,128)(2,1)S(1)}, bf16[512,256]{1,0:T(8,128)(2,1)S(1)}, f32[512,256]{1,0:T(8,128)S(1)}, f32[512,256]{1,0:T(8,128)S(1)}, bf16[2560,512]{1,0:T(8,128)(2,1)S(1)}) custom-call(s32[3]{0:T(128)S(1)} %pad_add_fusion.ids_ref, s32[1]{0:T(128)S(6)} %copy.12.bound_ref, bf16[512,2560]{1,0:T(8,128)(2,1)S(1)} %bitcast.15, ...), custom_call_target="tpu_custom_call" | custom-call | flops 1342177280 | bytes 9437200 | tf_op jit(solution)/shard_map/pallas_call | solution.py:194
  8.5 3.0 %collective-permute-start.2 = (bf16[512,256]{1,0:T(8,128)(2,1)S(1)}, bf16[512,256]{1,0:T(8,128)(2,1)S(1)}, u32[]{:S(2)}, u32[]{:S(2)}) collective-permute-start(bf16[512,256]{1,0:T(8,128)(2,1)S(1)} %get-tuple-element.32), channel_id=1, source_target_pairs={{0,1},{1,0},{2,3},{3,2},{4,5},{5,4},{6,7},{7,6},{8,9},{9,8},{10,11... | collective-permute-start | bytes 786440 | tf_op jit(solution)/shard_map/ppermute | solution.py:174
  11.6 0.1 collective-permute-start
  11.7 7.1 %collective-permute-done.2.got_ref = bf16[512,256]{1,0:T(8,128)(2,1)S(1)} collective-permute-done((bf16[512,256]{1,0:T(8,128)(2,1)S(1)}, bf16[512,256]{1,0:T(8,128)(2,1)S(1)}, u32[]{:S(2)}, u32[]{:S(2)}) %collective-permute-start.2) | collective-permute-done | bytes 262176 | tf_op jit(solution)/shard_map/ppermute | solution.py:174
  18.7 0.0 copy-done.4
  18.7 0.3 shard_map.101.part_ref
  19.1 0.1 collective-permute-start.3
  19.1 0.0 copy-start.5
  19.2 0.0 copy-start.1
  19.2 10.0 %shard_map.99 = (f32[2560,256]{1,0:T(8,128)S(1)}, f32[2560,256]{1,0:T(8,128)S(1)}) custom-call(bf16[2560,2560]{1,0:T(8,128)(2,1)} %bitcast.19, bf16[2560,512]{1,0:T(8,128)(2,1)S(1)} %get-tuple-element.29.masked_ref), custom_call_target="tpu_custom_call" | custom-call | flops 6710886400 | bytes 20971520 | tf_op jit(solution)/shard_map/pallas_call | solution.py:194
  29.1 0.0 copy-done.5
  29.1 1.7 %shard_map.96 = (s32[24]{0:T(128)S(1)}, s32[24]{0:T(128)S(1)}) custom-call(s32[3]{0:T(128)S(1)} %pad_add_fusion.ids_ref, s32[1]{0:T(128)S(6)} %copy.12.bound_ref, s32[20]{0:T(128)S(1)} %bitcast.18), custom_call_target="tpu_custom_call" | custom-call | flops 1000000 | bytes 288 | tf_op jit(solution)/shard_map/pallas_call | solution.py:194
  30.8 0.0 collective-permute-done.got_ref
  30.9 0.3 shard_map.98.part_ref
  31.2 0.5 collective-permute-start.1
  31.7 0.0 collective-permute-done.3.got_ref
  31.7 0.0 copy-done.1
  31.7 1.5 %shard_map.102 = (bf16[384,256]{1,0:T(8,128)(2,1)S(1)}, bf16[384,256]{1,0:T(8,128)(2,1)S(1)}, bf16[768,256]{1,0:T(8,128)(2,1)S(1)}, bf16[1536,256]{1,0:T(8,128)(2,1)S(1)}) custom-call(s32[24]{0:T(128)S(1)} %get-tuple-element.25.source_ref, f32[512,256]{1,0:T(8,128)S(1)} %shard_map.101.part_ref, f32[512,256]{1,0:T(8,128)S(1)} %collective-permute-done.3.got_ref, ...), custom_call_target="tpu_custom_call" | custom-call | flops 671088640 | bytes 7864416 | tf_op jit(solution)/shard_map/pallas_call | solution.py:194
  33.2 2.1 %collective-permute-start.8 = (bf16[1536,256]{1,0:T(8,128)(2,1)S(1)}, bf16[1536,256]{1,0:T(8,128)(2,1)S(1)}, u32[]{:S(2)}, u32[]{:S(2)}) collective-permute-start(bf16[1536,256]{1,0:T(8,128)(2,1)S(1)} %get-tuple-element.36), channel_id=1, source_target_pairs={{0,1},{1,0},{2,3},{3,2},{4,5},{5,4},{6,7},{7,6},{8,9},{9,8},{10,11... | collective-permute-start | bytes 2359304 | tf_op jit(solution)/shard_map/ppermute | solution.py:174
  35.3 0.1 collective-permute-start.6
  35.4 1.9 %collective-permute-start.4 = (bf16[384,256]{1,0:T(8,128)(2,1)S(1)}, bf16[384,256]{1,0:T(8,128)(2,1)S(1)}, u32[]{:S(2)}, u32[]{:S(2)}) collective-permute-start(bf16[384,256]{1,0:T(8,128)(2,1)S(1)} %get-tuple-element.34), channel_id=1, source_target_pairs={{0,1},{1,0},{2,3},{3,2},{4,5},{5,4},{6,7},{7,6},{8,9},{9,8},{10,11... | collective-permute-start | bytes 589832 | tf_op jit(solution)/shard_map/ppermute | solution.py:174
  37.3 0.1 collective-permute-start.12
  37.4 0.0 collective-permute-done.1.got_ref
  37.4 0.9 shard_map.100.own_ref
  38.3 19.6 %collective-permute-done.6.got_ref = bf16[384,256]{1,0:T(8,128)(2,1)S(1)} collective-permute-done((bf16[384,256]{1,0:T(8,128)(2,1)S(1)}, bf16[384,256]{1,0:T(8,128)(2,1)S(1)}, u32[]{:S(2)}, u32[]{:S(2)}) %collective-permute-start.6) | collective-permute-done | bytes 196640 | tf_op jit(solution)/shard_map/ppermute | solution.py:174
  57.9 0.6 shard_map.104
  58.5 4.1 %collective-permute-start.7 = (bf16[400,256]{1,0:T(8,128)(2,1)S(1)}, bf16[400,256]{1,0:T(8,128)(2,1)S(1)}, u32[]{:S(2)}, u32[]{:S(2)}) collective-permute-start(bf16[400,256]{1,0:T(8,128)(2,1)S(1)} %shard_map.104), channel_id=1, source_target_pairs={{0,20},{4,16},{8,28},{12,24},{16,4},{20,0},{24,12},{28,8},{1,21},{... | collective-permute-start | bytes 614408 | tf_op jit(solution)/shard_map/ppermute | solution.py:174
  62.6 0.0 collective-permute-done.4.got_ref
  62.6 0.6 shard_map.103
  63.2 2.7 %collective-permute-start.5 = (bf16[400,256]{1,0:T(8,128)(2,1)S(1)}, bf16[400,256]{1,0:T(8,128)(2,1)S(1)}, u32[]{:S(2)}, u32[]{:S(2)}) collective-permute-start(bf16[400,256]{1,0:T(8,128)(2,1)S(1)} %shard_map.103), channel_id=1, source_target_pairs={{0,16},{4,20},{8,24},{12,28},{16,0},{20,4},{24,8},{28,12},{1,17},{... | collective-permute-start | bytes 614408 | tf_op jit(solution)/shard_map/ppermute | solution.py:174
  65.9 0.0 collective-permute-done.8.got_ref
  65.9 0.7 shard_map.105
  66.6 0.0 copy-start
  66.6 2.6 %collective-permute-start.10 = (bf16[400,256]{1,0:T(8,128)(2,1)S(1)}, bf16[400,256]{1,0:T(8,128)(2,1)S(1)}, u32[]{:S(2)}, u32[]{:S(2)}) collective-permute-start(bf16[400,256]{1,0:T(8,128)(2,1)S(1)} %get-tuple-element.38), channel_id=1, source_target_pairs={{0,12},{4,8},{8,4},{12,0},{16,28},{20,24},{24,20},{28,16},{1,13},{... | collective-permute-start | bytes 614408 | tf_op jit(solution)/shard_map/ppermute | solution.py:174
  69.2 0.5 collective-permute-start.11
  69.7 0.2 collective-permute-done.12.got_ref
  69.9 1.8 %collective-permute-start.9 = (bf16[400,256]{1,0:T(8,128)(2,1)S(1)}, bf16[400,256]{1,0:T(8,128)(2,1)S(1)}, u32[]{:S(2)}, u32[]{:S(2)}) collective-permute-start(bf16[400,256]{1,0:T(8,128)(2,1)S(1)} %get-tuple-element.37), channel_id=1, source_target_pairs={{0,8},{4,12},{8,0},{12,4},{16,24},{20,28},{24,16},{28,20},{1,9},{5... | collective-permute-start | bytes 614408 | tf_op jit(solution)/shard_map/ppermute | solution.py:174
  71.7 0.6 shard_map.107
  72.3 3.8 %collective-permute-done.7.refs_1_ = bf16[400,256]{1,0:T(8,128)(2,1)S(1)} collective-permute-done((bf16[400,256]{1,0:T(8,128)(2,1)S(1)}, bf16[400,256]{1,0:T(8,128)(2,1)S(1)}, u32[]{:S(2)}, u32[]{:S(2)}) %collective-permute-start.7) | collective-permute-done | bytes 204832 | tf_op jit(solution)/shard_map/ppermute | solution.py:174
  76.1 2.8 %collective-permute-start.13 = (bf16[400,256]{1,0:T(8,128)(2,1)S(1)}, bf16[400,256]{1,0:T(8,128)(2,1)S(1)}, u32[]{:S(2)}, u32[]{:S(2)}) collective-permute-start(bf16[400,256]{1,0:T(8,128)(2,1)S(1)} %get-tuple-element.42), channel_id=1, source_target_pairs={{0,24},{4,28},{8,16},{12,20},{16,8},{20,12},{24,0},{28,4},{1,25},{... | collective-permute-start | bytes 614408 | tf_op jit(solution)/shard_map/ppermute | solution.py:174
  78.9 2.8 %collective-permute-done.5.refs_0_ = bf16[400,256]{1,0:T(8,128)(2,1)S(1)} collective-permute-done((bf16[400,256]{1,0:T(8,128)(2,1)S(1)}, bf16[400,256]{1,0:T(8,128)(2,1)S(1)}, u32[]{:S(2)}, u32[]{:S(2)}) %collective-permute-start.5) | collective-permute-done | bytes 204832 | tf_op jit(solution)/shard_map/ppermute | solution.py:174
  81.7 1.6 %collective-permute-start.14 = (bf16[400,256]{1,0:T(8,128)(2,1)S(1)}, bf16[400,256]{1,0:T(8,128)(2,1)S(1)}, u32[]{:S(2)}, u32[]{:S(2)}) collective-permute-start(bf16[400,256]{1,0:T(8,128)(2,1)S(1)} %get-tuple-element.43), channel_id=1, source_target_pairs={{0,28},{4,24},{8,20},{12,16},{16,12},{20,8},{24,4},{28,0},{1,29},{... | collective-permute-start | bytes 614408 | tf_op jit(solution)/shard_map/ppermute | solution.py:174
  83.3 0.0 copy-done
  83.3 0.9 shard_map.95.refs_0_
  84.2 3.7 %collective-permute-done.10.refs_3_ = bf16[400,256]{1,0:T(8,128)(2,1)S(1)} collective-permute-done((bf16[400,256]{1,0:T(8,128)(2,1)S(1)}, bf16[400,256]{1,0:T(8,128)(2,1)S(1)}, u32[]{:S(2)}, u32[]{:S(2)}) %collective-permute-start.10) | collective-permute-done | bytes 204832 | tf_op jit(solution)/shard_map/ppermute | solution.py:174
  87.9 0.0 collective-permute-done.11.refs_4_
  87.9 5.5 %collective-permute-done.9.refs_2_ = bf16[400,256]{1,0:T(8,128)(2,1)S(1)} collective-permute-done((bf16[400,256]{1,0:T(8,128)(2,1)S(1)}, bf16[400,256]{1,0:T(8,128)(2,1)S(1)}, u32[]{:S(2)}, u32[]{:S(2)}) %collective-permute-start.9) | collective-permute-done | bytes 204832 | tf_op jit(solution)/shard_map/ppermute | solution.py:174
  93.4 2.5 %shard_map.106.refs_1_ = f32[3072,256]{1,0:T(8,128)S(1)} custom-call(bf16[400,256]{1,0:T(8,128)(2,1)S(1)} %collective-permute-done.5.refs_0_, bf16[400,256]{1,0:T(8,128)(2,1)S(1)} %collective-permute-done.7.refs_1_, bf16[400,256]{1,0:T(8,128)(2,1)S(1)} %collective-permute-done.9.refs_2_, bf16[400,256]{1,0:T(8,128)(2,1)S(1)} %collective-permute-done.10.refs_3_, ...), custom_call_target="tpu_custom_call" | custom-call | flops 1000000000 | bytes 4374528 | tf_op jit(solution)/shard_map/pallas_call | solution.py:194
  95.9 0.0 collective-permute-done.13.refs_2_
  95.9 0.0 collective-permute-done.14.refs_3_
  95.9 1.8 %shard_map.108 = (f32[3072,256]{1,0:T(8,128)S(1)}, f32[512,256]{1,0:T(8,128)S(1)}) custom-call(bf16[512,3072]{1,0:T(8,128)(2,1)S(1)} %shard_map.95.refs_0_, f32[3072,256]{1,0:T(8,128)S(1)} %shard_map.106.refs_1_, bf16[400,256]{1,0:T(8,128)(2,1)S(1)} %collective-permute-done.13.refs_2_, ...), custom_call_target="tpu_custom_call", output_to_operand_aliasing={{0}: (1, {})} | custom-call | flops 805306368 | bytes 10371072 | tf_op jit(solution)/shard_map/pallas_call | solution.py:194
  97.7 0.1 collective-permute-start.15
  97.8 1.9 %collective-permute-done.15.got_ref = f32[512,256]{1,0:T(8,128)S(1)} collective-permute-done((f32[512,256]{1,0:T(8,128)S(1)}, f32[512,256]{1,0:T(8,128)S(1)}, u32[]{:S(2)}, u32[]{:S(2)}) %collective-permute-start.15) | collective-permute-done | bytes 524320 | tf_op jit(solution)/shard_map/ppermute | solution.py:174
  99.7 3.1 %shard_map.109 = (f32[512,256]{1,0:T(8,128)}, f32[3072,256]{1,0:T(8,128)}) custom-call(bf16[3072,512]{1,0:T(8,128)(2,1)S(1)} %bitcast.12, f32[3072,256]{1,0:T(8,128)S(1)} %get-tuple-element.44.parent_ref, f32[512,256]{1,0:T(8,128)S(1)} %get-tuple-element.45.part_ref, f32[512,256]{1,0:T(8,128)S(1)} %collective-permute-done.15.got_ref), custom_call_target="tpu_custom_call" | custom-call | flops 805306368 | bytes 11010048 | tf_op jit(solution)/shard_map/pallas_call | solution.py:194
Async XLA Ops:
  1.4 1.7 %copy-start.2 = (bf16[1,512,2560]{2,1,0:T(8,128)(2,1)S(1)}, bf16[1,512,2560]{2,1,0:T(8,128)(2,1)}, u32[]{:S(2)}) copy-start(bf16[1,512,2560]{2,1,0:T(8,128)(2,1)} %param.11) | copy-start | bytes 7864324
  3.1 1.7 %copy-start.3 = (bf16[2560,512]{1,0:T(8,128)(2,1)S(1)}, bf16[2560,512]{1,0:T(8,128)(2,1)}, u32[]{:S(2)}) copy-start(bf16[2560,512]{1,0:T(8,128)(2,1)} %sketch_ref.1) | copy-start | bytes 7864324
  4.8 13.9 %copy-start.4 = (bf16[1,512,512]{2,1,0:T(8,128)(2,1)S(1)}, bf16[1,512,512]{2,1,0:T(8,128)(2,1)}, u32[]{:S(2)}) copy-start(bf16[1,512,512]{2,1,0:T(8,128)(2,1)} %param.10) | copy-start | bytes 1572868
  8.5 10.2 %collective-permute-start.2 = (bf16[512,256]{1,0:T(8,128)(2,1)S(1)}, bf16[512,256]{1,0:T(8,128)(2,1)S(1)}, u32[]{:S(2)}, u32[]{:S(2)}) collective-permute-start(bf16[512,256]{1,0:T(8,128)(2,1)S(1)} %get-tuple-element.32), channel_id=1, source_target_pairs={{0,1},{1,0},{2,3},{3,2},{4,5},{5,4},{6,7},{7,6},{8,9},{9,8},{10,11... | collective-permute-start | bytes 786440 | tf_op jit(solution)/shard_map/ppermute | solution.py:174
  11.6 19.3 %collective-permute-start = (bf16[512,256]{1,0:T(8,128)(2,1)S(1)}, bf16[512,256]{1,0:T(8,128)(2,1)S(1)}, u32[]{:S(2)}, u32[]{:S(2)}) collective-permute-start(bf16[512,256]{1,0:T(8,128)(2,1)S(1)} %get-tuple-element.28), channel_id=1, source_target_pairs={{0,1},{1,0},{2,3},{3,2},{4,5},{5,4},{6,7},{7,6},{8,9},{9,8},{10,11... | collective-permute-start | bytes 786440 | tf_op jit(solution)/shard_map/ppermute | solution.py:174
  19.1 12.6 %collective-permute-start.3 = (f32[512,256]{1,0:T(8,128)S(1)}, f32[512,256]{1,0:T(8,128)S(1)}, u32[]{:S(2)}, u32[]{:S(2)}) collective-permute-start(f32[512,256]{1,0:T(8,128)S(1)} %shard_map.101.part_ref), channel_id=1, source_target_pairs={{0,2},{2,0},{1,3},{3,1},{4,6},{6,4},{5,7},{7,5},{8,10},{10,8},{9,1... | collective-permute-start | bytes 1572872 | tf_op jit(solution)/shard_map/ppermute | solution.py:174
  19.1 10.0 %copy-start.5 = (s32[1,20]{1,0:T(1,128)S(1)}, s32[1,20]{1,0:T(1,128)}, u32[]{:S(2)}) copy-start(s32[1,20]{1,0:T(1,128)} %param.9) | copy-start | bytes 244
  19.2 12.6 %copy-start.1 = (bf16[1,2560,512]{2,1,0:T(8,128)(2,1)S(1)}, bf16[1,2560,512]{2,1,0:T(8,128)(2,1)}, u32[]{:S(2)}) copy-start(bf16[1,2560,512]{2,1,0:T(8,128)(2,1)} %param.12) | copy-start | bytes 7864324
  31.2 6.3 %collective-permute-start.1 = (f32[512,256]{1,0:T(8,128)S(1)}, f32[512,256]{1,0:T(8,128)S(1)}, u32[]{:S(2)}, u32[]{:S(2)}) collective-permute-start(f32[512,256]{1,0:T(8,128)S(1)} %shard_map.98.part_ref), channel_id=1, source_target_pairs={{0,2},{2,0},{1,3},{3,1},{4,6},{6,4},{5,7},{7,5},{8,10},{10,8},{9,1... | collective-permute-start | bytes 1572872 | tf_op jit(solution)/shard_map/ppermute | solution.py:174
  33.2 32.7 %collective-permute-start.8 = (bf16[1536,256]{1,0:T(8,128)(2,1)S(1)}, bf16[1536,256]{1,0:T(8,128)(2,1)S(1)}, u32[]{:S(2)}, u32[]{:S(2)}) collective-permute-start(bf16[1536,256]{1,0:T(8,128)(2,1)S(1)} %get-tuple-element.36), channel_id=1, source_target_pairs={{0,1},{1,0},{2,3},{3,2},{4,5},{5,4},{6,7},{7,6},{8,9},{9,8},{10,11... | collective-permute-start | bytes 2359304 | tf_op jit(solution)/shard_map/ppermute | solution.py:174
  35.3 22.6 %collective-permute-start.6 = (bf16[384,256]{1,0:T(8,128)(2,1)S(1)}, bf16[384,256]{1,0:T(8,128)(2,1)S(1)}, u32[]{:S(2)}, u32[]{:S(2)}) collective-permute-start(bf16[384,256]{1,0:T(8,128)(2,1)S(1)} %get-tuple-element.35), channel_id=1, source_target_pairs={{0,1},{1,0},{2,3},{3,2},{4,5},{5,4},{6,7},{7,6},{8,9},{9,8},{10,11... | collective-permute-start | bytes 589832 | tf_op jit(solution)/shard_map/ppermute | solution.py:174
  35.4 27.2 %collective-permute-start.4 = (bf16[384,256]{1,0:T(8,128)(2,1)S(1)}, bf16[384,256]{1,0:T(8,128)(2,1)S(1)}, u32[]{:S(2)}, u32[]{:S(2)}) collective-permute-start(bf16[384,256]{1,0:T(8,128)(2,1)S(1)} %get-tuple-element.34), channel_id=1, source_target_pairs={{0,1},{1,0},{2,3},{3,2},{4,5},{5,4},{6,7},{7,6},{8,9},{9,8},{10,11... | collective-permute-start | bytes 589832 | tf_op jit(solution)/shard_map/ppermute | solution.py:174
  37.3 32.6 %collective-permute-start.12 = (bf16[768,256]{1,0:T(8,128)(2,1)S(1)}, bf16[768,256]{1,0:T(8,128)(2,1)S(1)}, u32[]{:S(2)}, u32[]{:S(2)}) collective-permute-start(bf16[768,256]{1,0:T(8,128)(2,1)S(1)} %get-tuple-element.41), channel_id=1, source_target_pairs={{0,1},{1,0},{2,3},{3,2},{4,5},{5,4},{6,7},{7,6},{8,9},{9,8},{10,11... | collective-permute-start | bytes 1179656 | tf_op jit(solution)/shard_map/ppermute | solution.py:174
  58.5 17.6 %collective-permute-start.7 = (bf16[400,256]{1,0:T(8,128)(2,1)S(1)}, bf16[400,256]{1,0:T(8,128)(2,1)S(1)}, u32[]{:S(2)}, u32[]{:S(2)}) collective-permute-start(bf16[400,256]{1,0:T(8,128)(2,1)S(1)} %shard_map.104), channel_id=1, source_target_pairs={{0,20},{4,16},{8,28},{12,24},{16,4},{20,0},{24,12},{28,8},{1,21},{... | collective-permute-start | bytes 614408 | tf_op jit(solution)/shard_map/ppermute | solution.py:174
  63.2 18.5 %collective-permute-start.5 = (bf16[400,256]{1,0:T(8,128)(2,1)S(1)}, bf16[400,256]{1,0:T(8,128)(2,1)S(1)}, u32[]{:S(2)}, u32[]{:S(2)}) collective-permute-start(bf16[400,256]{1,0:T(8,128)(2,1)S(1)} %shard_map.103), channel_id=1, source_target_pairs={{0,16},{4,20},{8,24},{12,28},{16,0},{20,4},{24,8},{28,12},{1,17},{... | collective-permute-start | bytes 614408 | tf_op jit(solution)/shard_map/ppermute | solution.py:174
  66.6 16.7 %copy-start = (bf16[1,3072,512]{2,1,0:T(8,128)(2,1)S(1)}, bf16[1,3072,512]{2,1,0:T(8,128)(2,1)}, u32[]{:S(2)}) copy-start(bf16[1,3072,512]{2,1,0:T(8,128)(2,1)} %param.15) | copy-start | bytes 9437188
  66.6 21.3 %collective-permute-start.10 = (bf16[400,256]{1,0:T(8,128)(2,1)S(1)}, bf16[400,256]{1,0:T(8,128)(2,1)S(1)}, u32[]{:S(2)}, u32[]{:S(2)}) collective-permute-start(bf16[400,256]{1,0:T(8,128)(2,1)S(1)} %get-tuple-element.38), channel_id=1, source_target_pairs={{0,12},{4,8},{8,4},{12,0},{16,28},{20,24},{24,20},{28,16},{1,13},{... | collective-permute-start | bytes 614408 | tf_op jit(solution)/shard_map/ppermute | solution.py:174
  69.2 18.7 %collective-permute-start.11 = (bf16[400,256]{1,0:T(8,128)(2,1)S(1)}, bf16[400,256]{1,0:T(8,128)(2,1)S(1)}, u32[]{:S(2)}, u32[]{:S(2)}) collective-permute-start(bf16[400,256]{1,0:T(8,128)(2,1)S(1)} %get-tuple-element.39), channel_id=1, source_target_pairs={{0,4},{4,0},{8,12},{12,8},{16,20},{20,16},{24,28},{28,24},{1,5},{5... | collective-permute-start | bytes 614408 | tf_op jit(solution)/shard_map/ppermute | solution.py:174
  69.9 23.5 %collective-permute-start.9 = (bf16[400,256]{1,0:T(8,128)(2,1)S(1)}, bf16[400,256]{1,0:T(8,128)(2,1)S(1)}, u32[]{:S(2)}, u32[]{:S(2)}) collective-permute-start(bf16[400,256]{1,0:T(8,128)(2,1)S(1)} %get-tuple-element.37), channel_id=1, source_target_pairs={{0,8},{4,12},{8,0},{12,4},{16,24},{20,28},{24,16},{28,20},{1,9},{5... | collective-permute-start | bytes 614408 | tf_op jit(solution)/shard_map/ppermute | solution.py:174
  76.1 19.8 %collective-permute-start.13 = (bf16[400,256]{1,0:T(8,128)(2,1)S(1)}, bf16[400,256]{1,0:T(8,128)(2,1)S(1)}, u32[]{:S(2)}, u32[]{:S(2)}) collective-permute-start(bf16[400,256]{1,0:T(8,128)(2,1)S(1)} %get-tuple-element.42), channel_id=1, source_target_pairs={{0,24},{4,28},{8,16},{12,20},{16,8},{20,12},{24,0},{28,4},{1,25},{... | collective-permute-start | bytes 614408 | tf_op jit(solution)/shard_map/ppermute | solution.py:174
  81.7 14.2 %collective-permute-start.14 = (bf16[400,256]{1,0:T(8,128)(2,1)S(1)}, bf16[400,256]{1,0:T(8,128)(2,1)S(1)}, u32[]{:S(2)}, u32[]{:S(2)}) collective-permute-start(bf16[400,256]{1,0:T(8,128)(2,1)S(1)} %get-tuple-element.43), channel_id=1, source_target_pairs={{0,28},{4,24},{8,20},{12,16},{16,12},{20,8},{24,4},{28,0},{1,29},{... | collective-permute-start | bytes 614408 | tf_op jit(solution)/shard_map/ppermute | solution.py:174
  97.7 2.0 %collective-permute-start.15 = (f32[512,256]{1,0:T(8,128)S(1)}, f32[512,256]{1,0:T(8,128)S(1)}, u32[]{:S(2)}, u32[]{:S(2)}) collective-permute-start(f32[512,256]{1,0:T(8,128)S(1)} %get-tuple-element.45.part_ref), channel_id=1, source_target_pairs={{0,2},{2,0},{1,3},{3,1},{4,6},{6,4},{5,7},{7,5},{8,10},{10,8},{9,1... | collective-permute-start | bytes 1572872 | tf_op jit(solution)/shard_map/ppermute | solution.py:174

commit v2 on v1

v2 whole, which is shorter than its diff:
```python
import functools

import jax
import jax.numpy as jnp
from jax import lax
from jax.experimental import pallas as pl
from jax.experimental.pallas import tpu as pltpu
from jax.sharding import PartitionSpec as P


BLOCK = 128
TAG_ROWS = 8
F32 = jnp.float32
BF16 = jnp.bfloat16
VMEM = pl.BlockSpec(memory_space=pltpu.VMEM)
SMEM = pl.BlockSpec(memory_space=pltpu.SMEM)
MIB = 1024 * 1024
TRAILING_LIMIT = 22 * MIB
ANY = pl.BlockSpec(memory_space=pl.ANY)


def dot(a, b):
    return jnp.dot(a, b, preferred_element_type=F32)


def pivot_kernel(
    sizes, ids_ref, bound_ref, map_ref, upper_hbm, sketch_hbm,
    own_ref, other_ref, kept_own_ref, kept_other_ref, masked_ref, order_ref, offset_ref, tag_ref,
    upper_ref, sketch_ref, sum_ref, upper_sem, sketch_sem, count_ref, rank_ref,
):
    depth, width = sketch_ref.shape
    half = width // 2
    parts = upper_sem.shape[0]
    part = depth // parts
    copies = []
    for k in range(parts):
        at = pl.ds(k * part, part)
        copies.append(
            (
                pltpu.make_async_copy(upper_hbm.at[:, at], upper_ref.at[:, at], upper_sem.at[k]),
                pltpu.make_async_copy(sketch_hbm.at[at, :], sketch_ref.at[at, :], sketch_sem.at[k]),
            )
        )
        for copy in copies[-1]:
            copy.start()
    plan(*sizes, ids_ref, bound_ref, map_ref, order_ref, offset_ref, tag_ref, count_ref, rank_ref)
    col = ids_ref[2]
    for k in range(parts):
        for copy in copies[k]:
            copy.wait()
        for start in range(k * part, (k + 1) * part, BLOCK):
            rows = slice(start, start + BLOCK)
            keep = jnp.where(col * depth + start < bound_ref[0], 1.0, 0.0).astype(F32)
            keep = jnp.full((BLOCK, half), keep, F32).astype(BF16)
            for side in range(2):
                pick = col if side == 0 else 1 - col
                value = sketch_ref[rows, pl.ds(pl.multiple_of(pick * half, half), half)]
                masked_ref[rows, side * half : (side + 1) * half] = value * keep
        first = (parts + 1) // 2
        if k == first - 1:
            at = slice(0, first * part)
            sum_ref[...] = dot(upper_ref[:, at], masked_ref[at, :])
        if k == parts - 1 and parts > 1:
            at = slice(first * part, depth)
            sum_ref[...] += dot(upper_ref[:, at], masked_ref[at, :])
    kept_own_ref[...] = sum_ref[:, :half]
    own_ref[...] = sum_ref[:, :half].astype(BF16)
    kept_other_ref[...] = sum_ref[:, half:]
    other_ref[...] = sum_ref[:, half:].astype(BF16)


def trailing_kernel(trailing_ref, masked_ref, own_ref, other_ref):
    value = dot(trailing_ref[...], masked_ref[...])
    half = masked_ref.shape[1] // 2
    own_ref[...] = value[:, :half]
    other_ref[...] = value[:, half:]


def solve_kernel(inverse_ref, kept_ref, got_ref, out_ref):
    rows = (kept_ref[...] + got_ref[...].astype(F32)).astype(BF16)
    out_ref[...] = dot(inverse_ref[...], rows)


def schur_kernel(part_ref, got_ref, lower_ref, trailing_ref, out_ref):
    solved = (part_ref[...] + got_ref[...]).astype(BF16)
    height = lower_ref.shape[0]
    step = 4 * BLOCK if height % (4 * BLOCK) == 0 else BLOCK
    for start in range(0, height, step):
        rows = slice(start, start + step)
        out_ref[rows, :] = (trailing_ref[rows, :] - dot(lower_ref[rows, :], solved)).astype(out_ref.dtype)


def packed_schur_kernel(cuts, order_ref, part_ref, got_ref, lower_ref, trailing_ref, *rest):
    outs, sum_ref = rest[:-1], rest[-1]
    schur_kernel(part_ref, got_ref, lower_ref, trailing_ref, sum_ref)
    for out, first in zip(outs, cuts):
        for p in range(out.shape[0] // BLOCK):
            at = pl.multiple_of(order_ref[first + p] * BLOCK, BLOCK)
            out[p * BLOCK : (p + 1) * BLOCK, :] = sum_ref[pl.ds(at, BLOCK), :]


def add_kernel(keys, cap, first, count, fresh, order_ref, offset_ref, tag_ref, own_ref, *refs):
    refs = list(refs)
    got_ref = refs.pop(0) if count else None
    if not fresh:
        refs.pop(0)
    sum_ref, outs = refs[0], refs[1:]
    for p in range(count):
        at = pl.multiple_of(order_ref[first + p] * BLOCK, BLOCK)
        value = own_ref[pl.ds(at, BLOCK), :] + got_ref[p * BLOCK : (p + 1) * BLOCK, :].astype(F32)
        sum_ref[(first + p) * BLOCK : (first + p + 1) * BLOCK, :] = value.astype(BF16)
    size = cap * BLOCK
    last = sum_ref.shape[0] // BLOCK - 1
    index = lax.broadcasted_iota(jnp.int32, (TAG_ROWS, sum_ref.shape[1]), 0)
    for key, out in zip(keys, outs):
        tags = jnp.zeros(index.shape, F32)
        for s in range(cap):
            at = pl.multiple_of(jnp.minimum(offset_ref[key] + s, last) * BLOCK, BLOCK)
            out[s * BLOCK : (s + 1) * BLOCK, :] = sum_ref[pl.ds(at, BLOCK), :]
            tags = jnp.where(index == s, tag_ref[key * cap + s].astype(F32), tags)
        out[size:, :] = tags.astype(BF16)


def add_pieces(per_device, cap, pieces, parent_ref):
    size = cap * BLOCK
    for piece in pieces:
        tile = piece[size : size + TAG_ROWS, :BLOCK].astype(F32)
        index = lax.broadcasted_iota(jnp.int32, tile.shape, 0)
        for s in range(cap):
            tag = jnp.max(jnp.where(index == s, tile, 0.0)).astype(jnp.int32)

            @pl.when(tag < per_device)
            def _():
                at = pl.ds(pl.multiple_of(tag * BLOCK, BLOCK), BLOCK)
                parent_ref[at, :] += piece[s * BLOCK : (s + 1) * BLOCK, :].astype(F32)


def early_kernel(per_device, cap, fresh, *refs):
    pieces, parent_ref = refs[: -1 if fresh else -2], refs[-1]
    if fresh:
        parent_ref[...] = jnp.zeros_like(parent_ref)
    add_pieces(per_device, cap, pieces, parent_ref)


def late_kernel(per_device, cap, *refs):
    flipped_ref, pieces, (parent_ref, coeff_ref) = refs[0], refs[2:-2], refs[-2:]
    add_pieces(per_device, cap, pieces, parent_ref)
    coeff_ref[...] = dot(flipped_ref[...], parent_ref[...].astype(BF16))


def flip_kernel(basis_ref, out_ref):
    out_ref[...] = basis_ref[...].T


def residual_kernel(basis_ref, parent_ref, part_ref, got_ref, coeff_hbm, out_hbm, coeff_ref, out_ref, coeff_sem, out_sem):
    total = part_ref[...] + got_ref[...]
    coeff_ref[...] = total
    copies = [pltpu.make_async_copy(coeff_ref, coeff_hbm, coeff_sem)]
    copies[0].start()
    total = total.astype(BF16)
    parts = out_sem.shape[0]
    part = out_ref.shape[0] // parts
    for k in range(parts):
        rows = slice(k * part, (k + 1) * part)
        out_ref[rows, :] = parent_ref[rows, :] - dot(basis_ref[rows, :], total)
        at = pl.ds(k * part, part)
        copies.append(pltpu.make_async_copy(out_ref.at[at, :], out_hbm.at[at, :], out_sem.at[k]))
        copies[-1].start()
    for copy in copies:
        copy.wait()


def swap(x, axis, turn=1):
    n = lax.axis_size(axis)
    return lax.ppermute(x, axis, [(i, i ^ turn) for i in range(n)])


def order_of(fronts):
    cuts = [0, fronts // 8, fronts // 4, fronts // 2, 3 * fronts // 4, fronts]
    return [list(range(a, b)) for a, b in zip(cuts, cuts[1:])]


def plan(row_count, per_device, cap, fronts, ids_ref, bound_ref, map_ref, order_ref, offset_ref, tag_ref, count_ref, rank_ref):
    me, row = ids_ref[0], ids_ref[1]
    blocks = map_ref.shape[0]
    for i in range(fronts):
        count_ref[i] = 0
    for i in range(fronts * cap):
        tag_ref[i] = per_device
    for i in range(blocks):
        order_ref[i] = 0

    def each_live(one):
        def step(j, carry):
            @pl.when((row * blocks + j) * BLOCK < bound_ref[0])
            def _():
                value = map_ref[j]
                one(j, value, fronts - 1 - lax.bitwise_xor(lax.div(value, row_count * per_device), me))

            return carry

        lax.fori_loop(0, blocks, step, 0)

    def count(j, value, key):
        rank = count_ref[key]
        count_ref[key] = rank + 1
        rank_ref[j] = rank
        tag_ref[key * cap + rank] = lax.rem(value, per_device)

    def place(j, value, key):
        order_ref[offset_ref[key] + rank_ref[j]] = j

    each_live(count)
    start = jnp.int32(0)
    for i in range(fronts):
        offset_ref[i] = start
        start = start + count_ref[i]
    each_live(place)


def call(kernel, operands, specs, outs, out_specs, flops, scratch=(), limit=None, **kw):
    space = 0
    for x in (*operands, *outs, *scratch):
        space += x.size * x.dtype.itemsize if hasattr(x, "size") else 0
    moved = sum(x.size * x.dtype.itemsize for x in (*operands, *outs))
    semantics = {"dimension_semantics": ("arbitrary",)} if "grid" in kw else {}
    return pl.pallas_call(
        kernel,
        out_shape=tuple(outs),
        in_specs=specs,
        out_specs=tuple(out_specs),
        scratch_shapes=[pltpu.VMEM(x.shape, x.dtype) if isinstance(x, jax.ShapeDtypeStruct) else x for x in scratch],
        compiler_params=pltpu.CompilerParams(vmem_limit_bytes=int(limit or space + 3 * MIB), **semantics),
        cost_estimate=pl.CostEstimate(flops=int(flops), bytes_accessed=int(moved), transcendentals=0),
        **kw,
    )(*operands)


def in_hbm(x):
    return pltpu.with_memory_space_constraint(x, pltpu.HBM)


def shape(rows, columns, dtype):
    return jax.ShapeDtypeStruct((rows, columns), dtype)


def program(bounds, block_map, pivot_inverse, upper_block, lower_block, trailing_block, sketch, basis):
    fronts, row_count = lax.axis_size("front"), lax.axis_size("row")
    assert fronts & (fronts - 1) == 0
    blocks = block_map.shape[1]
    per_device = basis.shape[1] // BLOCK
    cap = -(-blocks // fronts)
    depth, width = sketch.shape
    half = width // 2
    size = cap * BLOCK
    ids = jnp.stack([lax.axis_index("front"), lax.axis_index("row"), lax.axis_index("col")]).astype(jnp.int32)
    inverse, upper, lower, trailing, basis = pivot_inverse[0], upper_block[0], lower_block[0], trailing_block[0], basis[0]
    height, _ = lower.shape
    tall = upper.shape[0]
    groups = order_of(fronts)

    steps = 5 if depth % (5 * BLOCK) == 0 else 1
    send_own, send_other, kept_own, kept_other, masked, order, offset, tags = call(
        functools.partial(pivot_kernel, (row_count, per_device, cap, fronts)),
        (ids, bounds, block_map.reshape(-1), in_hbm(upper), in_hbm(sketch)),
        [SMEM, SMEM, SMEM, ANY, ANY],
        (shape(tall, half, BF16),) * 2
        + (shape(tall, half, F32),) * 2
        + (shape(depth, width, BF16),)
        + tuple(jax.ShapeDtypeStruct((n,), jnp.int32) for n in (blocks, fronts, fronts * cap)),
        [VMEM] * 5 + [SMEM] * 3,
        2 * upper.size * width,
        scratch=(
            shape(tall, depth, BF16),
            shape(depth, width, BF16),
            shape(tall, width, F32),
            pltpu.SemaphoreType.DMA((steps,)),
            pltpu.SemaphoreType.DMA((steps,)),
            pltpu.SMEM((fronts,), jnp.int32),
            pltpu.SMEM((blocks,), jnp.int32),
        ),
    )
    got_other = swap(send_own, "col")
    got_own = swap(send_other, "col")

    tile = 4 * BLOCK if height % (4 * BLOCK) == 0 else BLOCK
    trail_own, trail_other = call(
        trailing_kernel,
        (in_hbm(trailing), masked),
        [pl.BlockSpec((tile, depth), lambda i: (i, 0)), pl.BlockSpec((depth, width), lambda i: (0, 0))],
        (shape(height, half, F32),) * 2,
        [pl.BlockSpec((tile, half), lambda i: (i, 0))] * 2,
        2 * trailing.size * width,
        limit=TRAILING_LIMIT,
        grid=(height // tile,),
    )

    def solve(kept, got):
        return call(solve_kernel, (inverse, kept, got), [VMEM] * 3, (shape(inverse.shape[0], half, F32),), [VMEM], 2 * inverse.size * half)[0]

    part_other = solve(kept_other, got_other)
    row_other = swap(part_other, "row")
    part_own = solve(kept_own, got_own)
    row_own = swap(part_own, "row")
    cuts = [0] + [min(cap * (g[-1] + 1), blocks) for g in groups]
    counts = [b - a for a, b in zip(cuts, cuts[1:])]
    sums = call(
        functools.partial(packed_schur_kernel, [a for a, n in zip(cuts, counts) if n]),
        (order, part_other, row_other, lower, trail_other),
        [SMEM] + [VMEM] * 4,
        tuple(shape(n * BLOCK, half, BF16) for n in counts if n),
        [VMEM] * sum(n > 0 for n in counts),
        2 * lower.size * half,
        scratch=(shape(height, half, BF16),),
    )
    arrived = [swap(x, "col") for x in sums]
    own = call(
        schur_kernel,
        (part_own, row_own, lower, trail_own),
        [VMEM] * 4,
        (shape(height, half, F32),),
        [VMEM],
        2 * lower.size * half,
    )[0]

    pieces = {}
    total = None
    for g, keys in enumerate(groups):
        operands = [order, offset, tags, own]
        if counts[g]:
            operands.append(arrived[g])
        if g:
            operands.append(total)
        total, *made = call(
            functools.partial(add_kernel, keys, cap, cuts[g], counts[g], g == 0),
            operands,
            [SMEM] * 3 + [VMEM] * (len(operands) - 3),
            (shape(blocks * BLOCK, half, BF16),) + (shape(size + TAG_ROWS, half, BF16),) * len(keys),
            [VMEM] * (1 + len(keys)),
            1e9,
            **({"input_output_aliases": {len(operands) - 1: 0}} if g else {}),
        )
        for key, piece in zip(keys, made):
            turn = fronts - 1 - key
            pieces[key] = swap(piece, "front", turn) if turn else piece

    rank = basis.shape[1]
    rows = per_device * BLOCK
    flipped = call(flip_kernel, (basis,), [VMEM], (shape(rank, rows, BF16),), [VMEM], 1e9)[0]
    waves = [[fronts - 1] + groups[0] + groups[1], groups[2], [k for g in groups[3:] for k in g if k < fronts - 1]]
    parent = call(
        functools.partial(early_kernel, per_device, cap, True),
        [pieces[k] for k in waves[0]],
        [VMEM] * len(waves[0]),
        (shape(rows, half, F32),),
        [VMEM],
        1e9,
    )[0]
    parent = call(
        functools.partial(early_kernel, per_device, cap, False),
        [pieces[k] for k in waves[1]] + [parent],
        [VMEM] * (1 + len(waves[1])),
        (shape(rows, half, F32),),
        [VMEM],
        1e9,
        input_output_aliases={len(waves[1]): 0},
    )[0]
    parent, coeff = call(
        functools.partial(late_kernel, per_device, cap),
        [flipped, parent] + [pieces[k] for k in waves[2]],
        [VMEM] * (2 + len(waves[2])),
        (shape(rows, half, F32), shape(rank, half, F32)),
        [VMEM] * 2,
        2 * basis.size * half,
        input_output_aliases={1: 0},
    )
    got = swap(coeff, "row")
    steps = 6 if per_device % 6 == 0 else 1
    coefficients, residual = call(
        residual_kernel,
        (basis, parent, coeff, got),
        [VMEM] * 4,
        (shape(rank, half, F32), shape(rows, half, F32)),
        [ANY] * 2,
        2 * basis.size * half,
        scratch=(
            shape(rank, half, F32),
            shape(rows, half, F32),
            pltpu.SemaphoreType.DMA,
            pltpu.SemaphoreType.DMA((steps,)),
        ),
    )
    return coefficients[None], residual[None]


def solution(mesh):
    placed = (
        P("front"),
        P("front", "row"),
        P("front", "col", "row"),
        P("front", "row", "col"),
        P("front", "row", "col"),
        P("front", "row", "col"),
        P("col", None),
        P("front", "row", None),
    )

    def step(*args):
        sharded = jax.shard_map(
            program,
            mesh=mesh,
            in_specs=placed,
            out_specs=(P("front", None, "col"), P("front", "row", "col")),
            check_vma=False,
        )
        return sharded(*args)

    return step
```

time: 103 us -> 112 us (1.087)
  starting transfers between devices: 24.1 us -> 40.2 us
  waiting for transfers between devices: 44.6 us -> 41.5 us
  local copies, waits for them, and re-layouts: 3.5 us -> 0.67 us
  Pallas kernels: 29.1 us -> 27.6 us
    ppermute x16 -> x17, starting transfers between devices: 24.1 us -> 40.2 us  [swap(): return lax.ppermute(x, axis, [(i, i ^ turn) for i in range(n)])]
    ppermute x16 -> x17, waiting for transfers between devices: 44.6 us -> 41.5 us  [swap(): return lax.ppermute(x, axis, [(i, i ^ turn) for i in range(n)])]
    unnamed x12 -> x8, local copies, waits for them, and re-layouts: 3.5 us -> 0.67 us
    pallas_call x15 -> x16, Pallas kernels: 29.1 us -> 27.6 us  [call(): pl.pallas_call(kernel, out_shape=tuple(outs), in_specs=specs, out_specs=t...]
  transfers between devices with their start and end apart: 16 -> 17, of which waited for: 8 -> 9; matrix products, arithmetic and copies ran while one was open for 0% -> 0% of each run, Pallas kernels for 20% -> 17%
where the time goes in v2:
time: 112 us
  waiting for transfers between devices  41.5 us (37%)
  starting transfers between devices  40.2 us (36%)
  Pallas kernels  27.6 us (25%)
  between operations  1.49 us (1%)
    ppermute x17, waiting for transfers between devices, swap(): return lax.ppermute(x, axis, [(i, i ^ turn) for i in range(n)])  41.5 us
    ppermute x17, starting transfers between devices, swap(): return lax.ppermute(x, axis, [(i, i ^ turn) for i in range(n)])  40.2 us
    pallas_call x16, Pallas kernels, call(): pl.pallas_call(kernel, out_shape=tuple(outs), in_specs=specs, out_specs=t...  27.6 us
  transfers between devices with their start and end apart: 17, of which 9 were waited for; matrix products, arithmetic and copies ran while one was open for 0% of the time, Pallas kernels for 17%

profile of v2, /device:TPU:0, one launch (start us, length us, event | category | flops | bytes accessed | tf_op | source)
XLA Modules:
  0.0 111.5 jit_solution(11929018988073234521)
XLA Ops:
  1.3 0.1 pad_add_fusion.ids_ref
  1.4 0.0 copy-start.3
  1.4 0.7 copy-done.3
  2.0 0.0 copy-start.2
  2.0 4.1 %shard_map.96 = (bf16[512,256]{1,0:T(8,128)(2,1)S(1)}, bf16[512,256]{1,0:T(8,128)(2,1)S(1)}, f32[512,256]{1,0:T(8,128)S(1)}, f32[512,256]{1,0:T(8,128)S(1)}, bf1...) custom-call(s32[3]{0:T(128)S(1)} %pad_add_fusion.ids_ref, s32[1]{0:T(128)S(6)} %copy.22.bound_ref, ...), custom_call_target="tpu_custom_call" | custom-call | flops 1342177280 | bytes 9437488 | tf_op jit(solution)/shard_map/pallas_call | solution.py:227
  6.1 3.0 %collective-permute-start.2 = (bf16[512,256]{1,0:T(8,128)(2,1)S(1)}, bf16[512,256]{1,0:T(8,128)(2,1)S(1)}, u32[]{:S(2)}, u32[]{:S(2)}) collective-permute-start(bf16[512,256]{1,0:T(8,128)(2,1)S(1)} %get-tuple-element.41), channel_id=1, source_target_pairs={{0,1},{1,0},{2,3},{3,2},{4,5},{5,4},{6,7},{7,6},{8,9},{9,8},{10,11... | collective-permute-start | bytes 786440 | tf_op jit(solution)/shard_map/ppermute | solution.py:175
  9.2 0.1 collective-permute-start
  9.2 7.1 %collective-permute-done.2.got_ref = bf16[512,256]{1,0:T(8,128)(2,1)S(1)} collective-permute-done((bf16[512,256]{1,0:T(8,128)(2,1)S(1)}, bf16[512,256]{1,0:T(8,128)(2,1)S(1)}, u32[]{:S(2)}, u32[]{:S(2)}) %collective-permute-start.2) | collective-permute-done | bytes 262176 | tf_op jit(solution)/shard_map/ppermute | solution.py:175
  16.3 0.0 copy-done.2
  16.3 0.3 shard_map.100.part_ref
  16.7 0.1 collective-permute-start.3
  16.7 4.4 %collective-permute-done.got_ref = bf16[512,256]{1,0:T(8,128)(2,1)S(1)} collective-permute-done((bf16[512,256]{1,0:T(8,128)(2,1)S(1)}, bf16[512,256]{1,0:T(8,128)(2,1)S(1)}, u32[]{:S(2)}, u32[]{:S(2)}) %collective-permute-start) | collective-permute-done | bytes 262176 | tf_op jit(solution)/shard_map/ppermute | solution.py:175
  21.1 0.3 shard_map.97.part_ref
  21.4 0.1 collective-permute-start.1
  21.5 0.0 copy-start.1
  21.5 10.0 %shard_map.98 = (f32[2560,256]{1,0:T(8,128)S(1)}, f32[2560,256]{1,0:T(8,128)S(1)}) custom-call(bf16[2560,2560]{1,0:T(8,128)(2,1)} %bitcast.19, bf16[2560,512]{1,0:T(8,128)(2,1)S(1)} %get-tuple-element.38.masked_ref), custom_call_target="tpu_custom_call" | custom-call | flops 6710886400 | bytes 20971520 | tf_op jit(solution)/shard_map/pallas_call | solution.py:227
  31.5 0.0 collective-permute-done.3.got_ref
  31.5 0.0 copy-done.1
  31.5 1.5 %shard_map.101 = (bf16[384,256]{1,0:T(8,128)(2,1)S(1)}, bf16[384,256]{1,0:T(8,128)(2,1)S(1)}, bf16[768,256]{1,0:T(8,128)(2,1)S(1)}, bf16[768,256]{1,0:T(8,128)(2,1)S(1)}, bf16[256,256]{1,0:T(8,128)(2,1)S(1)}) custom-call(s32[20]{0:T(128)S(1)} %get-tuple-element.33.order_ref, f32[512,256]{1,0:T(8,128)S(1)} %shard_map.100.part_ref, ...), custom_call_target="tpu_custom_call" | custom-call | flops 671088640 | bytes 7602256 | tf_op jit(solution)/shard_map/pallas_call | solution.py:227
  33.0 1.8 %collective-permute-start.4 = (bf16[768,256]{1,0:T(8,128)(2,1)S(1)}, bf16[768,256]{1,0:T(8,128)(2,1)S(1)}, u32[]{:S(2)}, u32[]{:S(2)}) collective-permute-start(bf16[768,256]{1,0:T(8,128)(2,1)S(1)} %get-tuple-element.43), channel_id=1, source_target_pairs={{0,1},{1,0},{2,3},{3,2},{4,5},{5,4},{6,7},{7,6},{8,9},{9,8},{10,11... | collective-permute-start | bytes 1179656 | tf_op jit(solution)/shard_map/ppermute | solution.py:175
  34.8 0.3 collective-permute-start.6
  35.1 1.7 %collective-permute-start.10 = (bf16[768,256]{1,0:T(8,128)(2,1)S(1)}, bf16[768,256]{1,0:T(8,128)(2,1)S(1)}, u32[]{:S(2)}, u32[]{:S(2)}) collective-permute-start(bf16[768,256]{1,0:T(8,128)(2,1)S(1)} %get-tuple-element.51), channel_id=1, source_target_pairs={{0,1},{1,0},{2,3},{3,2},{4,5},{5,4},{6,7},{7,6},{8,9},{9,8},{10,11... | collective-permute-start | bytes 1179656 | tf_op jit(solution)/shard_map/ppermute | solution.py:175
  36.8 0.3 collective-permute-start.5
  37.1 0.0 collective-permute-done.1.got_ref
  37.1 1.7 %collective-permute-start.9 = (bf16[256,256]{1,0:T(8,128)(2,1)S(1)}, bf16[256,256]{1,0:T(8,128)(2,1)S(1)}, u32[]{:S(2)}, u32[]{:S(2)}) collective-permute-start(bf16[256,256]{1,0:T(8,128)(2,1)S(1)} %get-tuple-element.50), channel_id=1, source_target_pairs={{0,1},{1,0},{2,3},{3,2},{4,5},{5,4},{6,7},{7,6},{8,9},{9,8},{10,11... | collective-permute-start | bytes 393224 | tf_op jit(solution)/shard_map/ppermute | solution.py:175
  38.9 0.9 shard_map.99.own_ref
  39.7 9.5 %collective-permute-done.6.refs_0_ = bf16[384,256]{1,0:T(8,128)(2,1)S(1)} collective-permute-done((bf16[384,256]{1,0:T(8,128)(2,1)S(1)}, bf16[384,256]{1,0:T(8,128)(2,1)S(1)}, u32[]{:S(2)}, u32[]{:S(2)}) %collective-permute-start.6) | collective-permute-done | bytes 196640 | tf_op jit(solution)/shard_map/ppermute | solution.py:175
  49.3 0.6 shard_map.102
  49.9 12.0 %collective-permute-done.5.refs_0_ = bf16[384,256]{1,0:T(8,128)(2,1)S(1)} collective-permute-done((bf16[384,256]{1,0:T(8,128)(2,1)S(1)}, bf16[384,256]{1,0:T(8,128)(2,1)S(1)}, u32[]{:S(2)}, u32[]{:S(2)}) %collective-permute-start.5) | collective-permute-done | bytes 196640 | tf_op jit(solution)/shard_map/ppermute | solution.py:175
  61.9 0.6 shard_map.103
  62.5 3.9 %collective-permute-start.12 = (bf16[392,256]{1,0:T(8,128)(2,1)S(1)}, bf16[392,256]{1,0:T(8,128)(2,1)S(1)}, u32[]{:S(2)}, u32[]{:S(2)}) collective-permute-start(bf16[392,256]{1,0:T(8,128)(2,1)S(1)} %get-tuple-element.56), channel_id=1, source_target_pairs={{0,24},{4,28},{8,16},{12,20},{16,8},{20,12},{24,0},{28,4},{1,25},{... | collective-permute-start | bytes 602120 | tf_op jit(solution)/shard_map/ppermute | solution.py:175
  66.4 1.2 %collective-permute-start.11 = (bf16[392,256]{1,0:T(8,128)(2,1)S(1)}, bf16[392,256]{1,0:T(8,128)(2,1)S(1)}, u32[]{:S(2)}, u32[]{:S(2)}) collective-permute-start(bf16[392,256]{1,0:T(8,128)(2,1)S(1)} %get-tuple-element.55), channel_id=1, source_target_pairs={{0,28},{4,24},{8,20},{12,16},{16,12},{20,8},{24,4},{28,0},{1,29},{... | collective-permute-start | bytes 602120 | tf_op jit(solution)/shard_map/ppermute | solution.py:175
  67.6 0.0 collective-permute-done.4.refs_0_
  67.6 0.6 shard_map.104
  68.3 0.8 collective-permute-start.7
  69.1 0.0 collective-permute-done.10.refs_0_
  69.1 2.0 %collective-permute-start.8 = (bf16[392,256]{1,0:T(8,128)(2,1)S(1)}, bf16[392,256]{1,0:T(8,128)(2,1)S(1)}, u32[]{:S(2)}, u32[]{:S(2)}) collective-permute-start(bf16[392,256]{1,0:T(8,128)(2,1)S(1)} %get-tuple-element.49), channel_id=1, source_target_pairs={{0,16},{4,20},{8,24},{12,28},{16,0},{20,4},{24,8},{28,12},{1,17},{... | collective-permute-start | bytes 602120 | tf_op jit(solution)/shard_map/ppermute | solution.py:175
  71.1 0.6 shard_map.105
  71.7 0.0 copy-start
  71.7 0.0 collective-permute-done.9.refs_0_
  71.7 0.6 shard_map.106
  72.4 1.7 %collective-permute-start.15 = (bf16[392,256]{1,0:T(8,128)(2,1)S(1)}, bf16[392,256]{1,0:T(8,128)(2,1)S(1)}, u32[]{:S(2)}, u32[]{:S(2)}) collective-permute-start(bf16[392,256]{1,0:T(8,128)(2,1)S(1)} %get-tuple-element.59), channel_id=1, source_target_pairs={{0,4},{4,0},{8,12},{12,8},{16,20},{20,16},{24,28},{28,24},{1,5},{5... | collective-permute-start | bytes 602120 | tf_op jit(solution)/shard_map/ppermute | solution.py:175
  74.1 0.0 collective-permute-done.12.refs_2_
  74.1 15.4 %collective-permute-start.13 = (bf16[392,256]{1,0:T(8,128)(2,1)S(1)}, bf16[392,256]{1,0:T(8,128)(2,1)S(1)}, u32[]{:S(2)}, u32[]{:S(2)}) collective-permute-start(bf16[392,256]{1,0:T(8,128)(2,1)S(1)} %get-tuple-element.57), channel_id=1, source_target_pairs={{0,12},{4,8},{8,4},{12,0},{16,28},{20,24},{24,20},{28,16},{1,13},{... | collective-permute-start | bytes 602120 | tf_op jit(solution)/shard_map/ppermute | solution.py:175
  89.5 0.0 collective-permute-done.11.refs_1_
  89.5 6.0 %collective-permute-start.14 = (bf16[392,256]{1,0:T(8,128)(2,1)S(1)}, bf16[392,256]{1,0:T(8,128)(2,1)S(1)}, u32[]{:S(2)}, u32[]{:S(2)}) collective-permute-start(bf16[392,256]{1,0:T(8,128)(2,1)S(1)} %get-tuple-element.58), channel_id=1, source_target_pairs={{0,8},{4,12},{8,0},{12,4},{16,24},{20,28},{24,16},{28,20},{1,9},{5... | collective-permute-start | bytes 602120 | tf_op jit(solution)/shard_map/ppermute | solution.py:175
  95.5 0.0 copy-done
  95.5 0.9 shard_map.95.refs_0_
  96.4 1.3 %shard_map.107.refs_2_ = f32[3072,256]{1,0:T(8,128)S(1)} custom-call(bf16[392,256]{1,0:T(8,128)(2,1)S(1)} %get-tuple-element.54.refs_0_, bf16[392,256]{1,0:T(8,128)(2,1)S(1)} %collective-permute-done.11.refs_1_, bf16[392,256]{1,0:T(8,128)(2,1)S(1)} %collective-permute-done.12.refs_2_), custom_call_target="tpu_custom_call" | custom-call | flops 1000000000 | bytes 3747840 | tf_op jit(solution)/shard_map/pallas_call | solution.py:227
  97.8 0.6 collective-permute-done.7.refs_0_
  98.3 1.7 %collective-permute-done.8.refs_1_ = bf16[392,256]{1,0:T(8,128)(2,1)S(1)} collective-permute-done((bf16[392,256]{1,0:T(8,128)(2,1)S(1)}, bf16[392,256]{1,0:T(8,128)(2,1)S(1)}, u32[]{:S(2)}, u32[]{:S(2)}) %collective-permute-start.8) | collective-permute-done | bytes 200736 | tf_op jit(solution)/shard_map/ppermute | solution.py:175
  100.1 0.8 shard_map.108.refs_1_
  100.9 0.0 collective-permute-done.15.refs_4_
  100.9 1.6 %collective-permute-done.13.refs_2_ = bf16[392,256]{1,0:T(8,128)(2,1)S(1)} collective-permute-done((bf16[392,256]{1,0:T(8,128)(2,1)S(1)}, bf16[392,256]{1,0:T(8,128)(2,1)S(1)}, u32[]{:S(2)}, u32[]{:S(2)}) %collective-permute-start.13) | collective-permute-done | bytes 200736 | tf_op jit(solution)/shard_map/ppermute | solution.py:175
  102.5 2.7 %collective-permute-done.14.refs_3_ = bf16[392,256]{1,0:T(8,128)(2,1)S(1)} collective-permute-done((bf16[392,256]{1,0:T(8,128)(2,1)S(1)}, bf16[392,256]{1,0:T(8,128)(2,1)S(1)}, u32[]{:S(2)}, u32[]{:S(2)}) %collective-permute-start.14) | collective-permute-done | bytes 200736 | tf_op jit(solution)/shard_map/ppermute | solution.py:175
  105.2 2.2 %shard_map.109 = (f32[3072,256]{1,0:T(8,128)S(1)}, f32[512,256]{1,0:T(8,128)S(1)}) custom-call(bf16[512,3072]{1,0:T(8,128)(2,1)S(1)} %shard_map.95.refs_0_, f32[3072,256]{1,0:T(8,128)S(1)} %shard_map.108.refs_1_, bf16[392,256]{1,0:T(8,128)(2,1)S(1)} %collective-permute-done.13.refs_2_, ...), custom_call_target="tpu_custom_call", output_to_operand_aliasing={{0}: (1, {})} | custom-call | flops 805306368 | bytes 10563584 | tf_op jit(solution)/shard_map/pallas_call | solution.py:227
  107.4 0.1 collective-permute-start.16
  107.5 1.9 %collective-permute-done.16.got_ref = f32[512,256]{1,0:T(8,128)S(1)} collective-permute-done((f32[512,256]{1,0:T(8,128)S(1)}, f32[512,256]{1,0:T(8,128)S(1)}, u32[]{:S(2)}, u32[]{:S(2)}) %collective-permute-start.16) | collective-permute-done | bytes 524320 | tf_op jit(solution)/shard_map/ppermute | solution.py:175
  109.4 2.2 %shard_map.110 = (f32[512,256]{1,0:T(8,128)}, f32[3072,256]{1,0:T(8,128)}) custom-call(bf16[3072,512]{1,0:T(8,128)(2,1)S(1)} %bitcast.12, f32[3072,256]{1,0:T(8,128)S(1)} %get-tuple-element.60.parent_ref, f32[512,256]{1,0:T(8,128)S(1)} %get-tuple-element.61.part_ref, f32[512,256]{1,0:T(8,128)S(1)} %collective-permute-done.16.got_ref), custom_call_target="tpu_custom_call" | custom-call | flops 805306368 | bytes 11010048 | tf_op jit(solution)/shard_map/pallas_call | solution.py:227
Async XLA Ops:
  1.4 0.7 copy-start.3
  2.0 14.3 %copy-start.2 = (bf16[1,512,512]{2,1,0:T(8,128)(2,1)S(1)}, bf16[1,512,512]{2,1,0:T(8,128)(2,1)}, u32[]{:S(2)}) copy-start(bf16[1,512,512]{2,1,0:T(8,128)(2,1)} %param.10) | copy-start | bytes 1572868
  6.1 10.2 %collective-permute-start.2 = (bf16[512,256]{1,0:T(8,128)(2,1)S(1)}, bf16[512,256]{1,0:T(8,128)(2,1)S(1)}, u32[]{:S(2)}, u32[]{:S(2)}) collective-permute-start(bf16[512,256]{1,0:T(8,128)(2,1)S(1)} %get-tuple-element.41), channel_id=1, source_target_pairs={{0,1},{1,0},{2,3},{3,2},{4,5},{5,4},{6,7},{7,6},{8,9},{9,8},{10,11... | collective-permute-start | bytes 786440 | tf_op jit(solution)/shard_map/ppermute | solution.py:175
  9.2 11.9 %collective-permute-start = (bf16[512,256]{1,0:T(8,128)(2,1)S(1)}, bf16[512,256]{1,0:T(8,128)(2,1)S(1)}, u32[]{:S(2)}, u32[]{:S(2)}) collective-permute-start(bf16[512,256]{1,0:T(8,128)(2,1)S(1)} %get-tuple-element.37), channel_id=1, source_target_pairs={{0,1},{1,0},{2,3},{3,2},{4,5},{5,4},{6,7},{7,6},{8,9},{9,8},{10,11... | collective-permute-start | bytes 786440 | tf_op jit(solution)/shard_map/ppermute | solution.py:175
  16.7 14.8 %collective-permute-start.3 = (f32[512,256]{1,0:T(8,128)S(1)}, f32[512,256]{1,0:T(8,128)S(1)}, u32[]{:S(2)}, u32[]{:S(2)}) collective-permute-start(f32[512,256]{1,0:T(8,128)S(1)} %shard_map.100.part_ref), channel_id=1, source_target_pairs={{0,2},{2,0},{1,3},{3,1},{4,6},{6,4},{5,7},{7,5},{8,10},{10,8},{9,1... | collective-permute-start | bytes 1572872 | tf_op jit(solution)/shard_map/ppermute | solution.py:175
  21.4 15.7 %collective-permute-start.1 = (f32[512,256]{1,0:T(8,128)S(1)}, f32[512,256]{1,0:T(8,128)S(1)}, u32[]{:S(2)}, u32[]{:S(2)}) collective-permute-start(f32[512,256]{1,0:T(8,128)S(1)} %shard_map.97.part_ref), channel_id=1, source_target_pairs={{0,2},{2,0},{1,3},{3,1},{4,6},{6,4},{5,7},{7,5},{8,10},{10,8},{9,1... | collective-permute-start | bytes 1572872 | tf_op jit(solution)/shard_map/ppermute | solution.py:175
  21.5 10.0 %copy-start.1 = (bf16[1,2560,512]{2,1,0:T(8,128)(2,1)S(1)}, bf16[1,2560,512]{2,1,0:T(8,128)(2,1)}, u32[]{:S(2)}) copy-start(bf16[1,2560,512]{2,1,0:T(8,128)(2,1)} %param.12) | copy-start | bytes 7864324
  33.0 34.6 %collective-permute-start.4 = (bf16[768,256]{1,0:T(8,128)(2,1)S(1)}, bf16[768,256]{1,0:T(8,128)(2,1)S(1)}, u32[]{:S(2)}, u32[]{:S(2)}) collective-permute-start(bf16[768,256]{1,0:T(8,128)(2,1)S(1)} %get-tuple-element.43), channel_id=1, source_target_pairs={{0,1},{1,0},{2,3},{3,2},{4,5},{5,4},{6,7},{7,6},{8,9},{9,8},{10,11... | collective-permute-start | bytes 1179656 | tf_op jit(solution)/shard_map/ppermute | solution.py:175
  34.8 14.5 %collective-permute-start.6 = (bf16[384,256]{1,0:T(8,128)(2,1)S(1)}, bf16[384,256]{1,0:T(8,128)(2,1)S(1)}, u32[]{:S(2)}, u32[]{:S(2)}) collective-permute-start(bf16[384,256]{1,0:T(8,128)(2,1)S(1)} %get-tuple-element.45), channel_id=1, source_target_pairs={{0,1},{1,0},{2,3},{3,2},{4,5},{5,4},{6,7},{7,6},{8,9},{9,8},{10,11... | collective-permute-start | bytes 589832 | tf_op jit(solution)/shard_map/ppermute | solution.py:175
  35.1 34.0 %collective-permute-start.10 = (bf16[768,256]{1,0:T(8,128)(2,1)S(1)}, bf16[768,256]{1,0:T(8,128)(2,1)S(1)}, u32[]{:S(2)}, u32[]{:S(2)}) collective-permute-start(bf16[768,256]{1,0:T(8,128)(2,1)S(1)} %get-tuple-element.51), channel_id=1, source_target_pairs={{0,1},{1,0},{2,3},{3,2},{4,5},{5,4},{6,7},{7,6},{8,9},{9,8},{10,11... | collective-permute-start | bytes 1179656 | tf_op jit(solution)/shard_map/ppermute | solution.py:175
  36.8 25.1 %collective-permute-start.5 = (bf16[384,256]{1,0:T(8,128)(2,1)S(1)}, bf16[384,256]{1,0:T(8,128)(2,1)S(1)}, u32[]{:S(2)}, u32[]{:S(2)}) collective-permute-start(bf16[384,256]{1,0:T(8,128)(2,1)S(1)} %get-tuple-element.44), channel_id=1, source_target_pairs={{0,1},{1,0},{2,3},{3,2},{4,5},{5,4},{6,7},{7,6},{8,9},{9,8},{10,11... | collective-permute-start | bytes 589832 | tf_op jit(solution)/shard_map/ppermute | solution.py:175
  37.1 34.6 %collective-permute-start.9 = (bf16[256,256]{1,0:T(8,128)(2,1)S(1)}, bf16[256,256]{1,0:T(8,128)(2,1)S(1)}, u32[]{:S(2)}, u32[]{:S(2)}) collective-permute-start(bf16[256,256]{1,0:T(8,128)(2,1)S(1)} %get-tuple-element.50), channel_id=1, source_target_pairs={{0,1},{1,0},{2,3},{3,2},{4,5},{5,4},{6,7},{7,6},{8,9},{9,8},{10,11... | collective-permute-start | bytes 393224 | tf_op jit(solution)/shard_map/ppermute | solution.py:175
  62.5 11.6 %collective-permute-start.12 = (bf16[392,256]{1,0:T(8,128)(2,1)S(1)}, bf16[392,256]{1,0:T(8,128)(2,1)S(1)}, u32[]{:S(2)}, u32[]{:S(2)}) collective-permute-start(bf16[392,256]{1,0:T(8,128)(2,1)S(1)} %get-tuple-element.56), channel_id=1, source_target_pairs={{0,24},{4,28},{8,16},{12,20},{16,8},{20,12},{24,0},{28,4},{1,25},{... | collective-permute-start | bytes 602120 | tf_op jit(solution)/shard_map/ppermute | solution.py:175
  66.4 23.1 %collective-permute-start.11 = (bf16[392,256]{1,0:T(8,128)(2,1)S(1)}, bf16[392,256]{1,0:T(8,128)(2,1)S(1)}, u32[]{:S(2)}, u32[]{:S(2)}) collective-permute-start(bf16[392,256]{1,0:T(8,128)(2,1)S(1)} %get-tuple-element.55), channel_id=1, source_target_pairs={{0,28},{4,24},{8,20},{12,16},{16,12},{20,8},{24,4},{28,0},{1,29},{... | collective-permute-start | bytes 602120 | tf_op jit(solution)/shard_map/ppermute | solution.py:175
  68.3 30.1 %collective-permute-start.7 = (bf16[392,256]{1,0:T(8,128)(2,1)S(1)}, bf16[392,256]{1,0:T(8,128)(2,1)S(1)}, u32[]{:S(2)}, u32[]{:S(2)}) collective-permute-start(bf16[392,256]{1,0:T(8,128)(2,1)S(1)} %get-tuple-element.48), channel_id=1, source_target_pairs={{0,20},{4,16},{8,28},{12,24},{16,4},{20,0},{24,12},{28,8},{1,21},{... | collective-permute-start | bytes 602120 | tf_op jit(solution)/shard_map/ppermute | solution.py:175
  69.1 31.0 %collective-permute-start.8 = (bf16[392,256]{1,0:T(8,128)(2,1)S(1)}, bf16[392,256]{1,0:T(8,128)(2,1)S(1)}, u32[]{:S(2)}, u32[]{:S(2)}) collective-permute-start(bf16[392,256]{1,0:T(8,128)(2,1)S(1)} %get-tuple-element.49), channel_id=1, source_target_pairs={{0,16},{4,20},{8,24},{12,28},{16,0},{20,4},{24,8},{28,12},{1,17},{... | collective-permute-start | bytes 602120 | tf_op jit(solution)/shard_map/ppermute | solution.py:175
  71.7 23.8 %copy-start = (bf16[1,3072,512]{2,1,0:T(8,128)(2,1)S(1)}, bf16[1,3072,512]{2,1,0:T(8,128)(2,1)}, u32[]{:S(2)}) copy-start(bf16[1,3072,512]{2,1,0:T(8,128)(2,1)} %param.15) | copy-start | bytes 9437188
  72.4 28.5 %collective-permute-start.15 = (bf16[392,256]{1,0:T(8,128)(2,1)S(1)}, bf16[392,256]{1,0:T(8,128)(2,1)S(1)}, u32[]{:S(2)}, u32[]{:S(2)}) collective-permute-start(bf16[392,256]{1,0:T(8,128)(2,1)S(1)} %get-tuple-element.59), channel_id=1, source_target_pairs={{0,4},{4,0},{8,12},{12,8},{16,20},{20,16},{24,28},{28,24},{1,5},{5... | collective-permute-start | bytes 602120 | tf_op jit(solution)/shard_map/ppermute | solution.py:175
  74.1 28.4 %collective-permute-start.13 = (bf16[392,256]{1,0:T(8,128)(2,1)S(1)}, bf16[392,256]{1,0:T(8,128)(2,1)S(1)}, u32[]{:S(2)}, u32[]{:S(2)}) collective-permute-start(bf16[392,256]{1,0:T(8,128)(2,1)S(1)} %get-tuple-element.57), channel_id=1, source_target_pairs={{0,12},{4,8},{8,4},{12,0},{16,28},{20,24},{24,20},{28,16},{1,13},{... | collective-permute-start | bytes 602120 | tf_op jit(solution)/shard_map/ppermute | solution.py:175
  89.5 15.6 %collective-permute-start.14 = (bf16[392,256]{1,0:T(8,128)(2,1)S(1)}, bf16[392,256]{1,0:T(8,128)(2,1)S(1)}, u32[]{:S(2)}, u32[]{:S(2)}) collective-permute-start(bf16[392,256]{1,0:T(8,128)(2,1)S(1)} %get-tuple-element.58), channel_id=1, source_target_pairs={{0,8},{4,12},{8,0},{12,4},{16,24},{20,28},{24,16},{28,20},{1,9},{5... | collective-permute-start | bytes 602120 | tf_op jit(solution)/shard_map/ppermute | solution.py:175
  107.4 2.0 %collective-permute-start.16 = (f32[512,256]{1,0:T(8,128)S(1)}, f32[512,256]{1,0:T(8,128)S(1)}, u32[]{:S(2)}, u32[]{:S(2)}) collective-permute-start(f32[512,256]{1,0:T(8,128)S(1)} %get-tuple-element.61.part_ref), channel_id=1, source_target_pairs={{0,2},{2,0},{1,3},{3,1},{4,6},{6,4},{5,7},{7,5},{8,10},{10,8},{9,1... | collective-permute-start | bytes 1572872 | tf_op jit(solution)/shard_map/ppermute | solution.py:175

commit v3 on v2

v3 whole, which is shorter than its diff:
```python
import functools

import jax
import jax.numpy as jnp
from jax import lax
from jax.experimental import pallas as pl
from jax.experimental.pallas import tpu as pltpu
from jax.sharding import PartitionSpec as P


BLOCK = 128
TAG_ROWS = 8
F32 = jnp.float32
BF16 = jnp.bfloat16
VMEM = pl.BlockSpec(memory_space=pltpu.VMEM)
SMEM = pl.BlockSpec(memory_space=pltpu.SMEM)
MIB = 1024 * 1024
ANY = pl.BlockSpec(memory_space=pl.ANY)


def dot(a, b):
    return jnp.dot(a, b, preferred_element_type=F32)


def pivot_kernel(
    sizes, ids_ref, bound_ref, map_hbm, upper_hbm, sketch_hbm, trailing_hbm,
    own_ref, other_ref, kept_own_ref, kept_other_ref, masked_ref, head_ref, order_ref, offset_ref, tag_ref,
    upper_ref, sketch_ref, sum_ref, upper_sem, sketch_sem, head_sem, map_sem, map_ref, count_ref, rank_ref, key_ref,
):
    map_copy = pltpu.make_async_copy(map_hbm, map_ref, map_sem)
    map_copy.start()
    depth, width = sketch_ref.shape
    half = width // 2
    parts = upper_sem.shape[0]
    part = depth // parts
    copies = []
    for k in range(parts):
        at = pl.ds(k * part, part)
        copies.append(
            (
                pltpu.make_async_copy(upper_hbm.at[:, at], upper_ref.at[:, at], upper_sem.at[k]),
                pltpu.make_async_copy(sketch_hbm.at[at, :], sketch_ref.at[at, :], sketch_sem.at[k]),
            )
        )
        for copy in copies[-1]:
            copy.start()
    head_copy = pltpu.make_async_copy(trailing_hbm.at[pl.ds(0, head_ref.shape[0]), :], head_ref, head_sem)
    head_copy.start()
    map_copy.wait()
    plan(*sizes, ids_ref, bound_ref, map_ref, order_ref, offset_ref, tag_ref, count_ref, rank_ref, key_ref)
    col = ids_ref[2]
    for k in range(parts):
        for copy in copies[k]:
            copy.wait()
        for start in range(k * part, (k + 1) * part, BLOCK):
            rows = slice(start, start + BLOCK)
            keep = jnp.where(col * depth + start < bound_ref[0], 1.0, 0.0).astype(F32)
            keep = jnp.full((BLOCK, half), keep, F32).astype(BF16)
            for side in range(2):
                pick = col if side == 0 else 1 - col
                value = sketch_ref[rows, pl.ds(pl.multiple_of(pick * half, half), half)]
                masked_ref[rows, side * half : (side + 1) * half] = value * keep
        first = (parts + 1) // 2
        if k == first - 1:
            at = slice(0, first * part)
            sum_ref[...] = dot(upper_ref[:, at], masked_ref[at, :])
        if k == parts - 1 and parts > 1:
            at = slice(first * part, depth)
            sum_ref[...] += dot(upper_ref[:, at], masked_ref[at, :])
    kept_own_ref[...] = sum_ref[:, :half]
    own_ref[...] = sum_ref[:, :half].astype(BF16)
    kept_other_ref[...] = sum_ref[:, half:]
    other_ref[...] = sum_ref[:, half:].astype(BF16)
    head_copy.wait()


def trailing_kernel(tile, trailing_hbm, head_ref, masked_ref, own_ref, other_ref, rest_ref, rest_sem):
    height, half = own_ref.shape
    head = head_ref.shape[0]
    copies = []
    for i, start in enumerate(range(head, height, tile)):
        copies.append(
            pltpu.make_async_copy(
                trailing_hbm.at[pl.ds(start, tile), :], rest_ref.at[pl.ds(start - head, tile), :], rest_sem.at[i]
            )
        )
        copies[-1].start()
    for start in range(0, height, tile):
        rows = slice(start, start + tile)
        if start < head:
            value = dot(head_ref[rows, :], masked_ref[...])
        else:
            copies[(start - head) // tile].wait()
            value = dot(rest_ref[start - head : start - head + tile, :], masked_ref[...])
        own_ref[rows, :] = value[:, :half]
        other_ref[rows, :] = value[:, half:]


def solve_kernel(inverse_ref, kept_ref, got_ref, out_ref):
    rows = (kept_ref[...] + got_ref[...].astype(F32)).astype(BF16)
    out_ref[...] = dot(inverse_ref[...], rows)


def schur_kernel(part_ref, got_ref, lower_ref, trailing_ref, out_ref):
    solved = (part_ref[...] + got_ref[...]).astype(BF16)
    height = lower_ref.shape[0]
    step = 4 * BLOCK if height % (4 * BLOCK) == 0 else BLOCK
    for start in range(0, height, step):
        rows = slice(start, start + step)
        out_ref[rows, :] = (trailing_ref[rows, :] - dot(lower_ref[rows, :], solved)).astype(out_ref.dtype)


def first_schur_kernel(order_ref, part_ref, got_ref, lower_ref, trailing_ref, out_ref):
    solved = (part_ref[...] + got_ref[...]).astype(BF16)
    for p in range(out_ref.shape[0] // BLOCK):
        at = pl.ds(pl.multiple_of(order_ref[p] * BLOCK, BLOCK), BLOCK)
        value = trailing_ref[at, :] - dot(lower_ref[at, :], solved)
        out_ref[p * BLOCK : (p + 1) * BLOCK, :] = value.astype(BF16)


def packed_schur_kernel(cuts, order_ref, part_ref, got_ref, lower_ref, trailing_ref, *rest):
    outs, sum_ref = rest[:-1], rest[-1]
    schur_kernel(part_ref, got_ref, lower_ref, trailing_ref, sum_ref)
    for out, first in zip(outs, cuts):
        for p in range(out.shape[0] // BLOCK):
            at = pl.multiple_of(order_ref[first + p] * BLOCK, BLOCK)
            out[p * BLOCK : (p + 1) * BLOCK, :] = sum_ref[pl.ds(at, BLOCK), :]


def add_kernel(
    parts, cap, first, count, fresh, order_ref, offset_ref, tag_ref, part_ref, row_ref, lower_ref, trailing_ref, *refs
):
    refs = list(refs)
    got_ref = refs.pop(0) if count else None
    if not fresh:
        refs.pop(0)
    sum_ref, outs = refs[0], refs[1:]
    solved = (part_ref[...] + row_ref[...]).astype(BF16)
    for p in range(count):
        at = pl.ds(pl.multiple_of(order_ref[first + p] * BLOCK, BLOCK), BLOCK)
        value = trailing_ref[at, :] - dot(lower_ref[at, :], solved) + got_ref[p * BLOCK : (p + 1) * BLOCK, :].astype(F32)
        sum_ref[(first + p) * BLOCK : (first + p + 1) * BLOCK, :] = value.astype(BF16)
    last = sum_ref.shape[0] // BLOCK - 1
    index = lax.broadcasted_iota(jnp.int32, (TAG_ROWS, sum_ref.shape[1]), 0)
    for (key, low, high), out in zip(parts, outs):
        tags = jnp.zeros(index.shape, F32)
        for s in range(low, high):
            at = pl.multiple_of(jnp.minimum(offset_ref[key] + s, last) * BLOCK, BLOCK)
            out[(s - low) * BLOCK : (s - low + 1) * BLOCK, :] = sum_ref[pl.ds(at, BLOCK), :]
            tags = jnp.where(index == s - low, tag_ref[key * cap + s].astype(F32), tags)
        out[(high - low) * BLOCK :, :] = tags.astype(BF16)


def add_pieces(per_device, pieces, parent_ref):
    for piece in pieces:
        count = piece.shape[0] // BLOCK
        tile = piece[count * BLOCK : count * BLOCK + TAG_ROWS, :BLOCK].astype(F32)
        index = lax.broadcasted_iota(jnp.int32, tile.shape, 0)
        for s in range(count):
            tag = jnp.max(jnp.where(index == s, tile, 0.0)).astype(jnp.int32)

            @pl.when(tag < per_device)
            def _():
                at = pl.ds(pl.multiple_of(tag * BLOCK, BLOCK), BLOCK)
                parent_ref[at, :] += piece[s * BLOCK : (s + 1) * BLOCK, :].astype(F32)


def early_kernel(per_device, fresh, *refs):
    pieces, parent_ref = refs[: -1 if fresh else -2], refs[-1]
    if fresh:
        parent_ref[...] = jnp.zeros_like(parent_ref)
    add_pieces(per_device, pieces, parent_ref)


def late_kernel(per_device, *refs):
    flipped_ref, pieces, (parent_ref, coeff_ref) = refs[0], refs[2:-2], refs[-2:]
    add_pieces(per_device, pieces, parent_ref)
    coeff_ref[...] = dot(flipped_ref[...], parent_ref[...].astype(BF16))


def flip_kernel(basis_ref, out_ref):
    out_ref[...] = basis_ref[...].T


def residual_kernel(basis_ref, parent_ref, part_ref, got_ref, coeff_hbm, out_hbm, coeff_ref, out_ref, coeff_sem, out_sem):
    total = part_ref[...] + got_ref[...]
    coeff_ref[...] = total
    copies = [pltpu.make_async_copy(coeff_ref, coeff_hbm, coeff_sem)]
    copies[0].start()
    total = total.astype(BF16)
    parts = out_sem.shape[0]
    part = out_ref.shape[0] // parts
    for k in range(parts):
        rows = slice(k * part, (k + 1) * part)
        out_ref[rows, :] = parent_ref[rows, :] - dot(basis_ref[rows, :], total)
        at = pl.ds(k * part, part)
        copies.append(pltpu.make_async_copy(out_ref.at[at, :], out_hbm.at[at, :], out_sem.at[k]))
        copies[-1].start()
    for copy in copies:
        copy.wait()


def swap(x, axis):
    return lax.ppermute(x, axis, [(i, i ^ 1) for i in range(lax.axis_size(axis))])


def away(x, key, fronts):
    return lax.ppermute(
        x, "front", [(i, j) for i in range(fronts) for j in range(fronts) if key_of(j, i, fronts) == key]
    )


def groups_of(fronts, cap):
    total = fronts * cap
    cuts = [0, 1, total // 8, total // 4, 3 * total // 8, total // 2, 3 * total // 4, total]
    groups = []
    for a, b in zip(cuts, cuts[1:]):
        keys = range(a // cap, -(-b // cap))
        groups.append([(k, max(a - k * cap, 0), min(b - k * cap, cap)) for k in keys if b > a])
    return groups, cuts


LEGS = (2, 1, 3, 0)


def gray(x):
    return x ^ (x >> 1)


def key_of(owner, me, fronts):
    inner = fronts // 4
    leg = (gray(owner // inner) - gray(me // inner)) & 3 if isinstance(owner, int) else lax.bitwise_and(
        gray_of(lax.div(owner, inner)) - gray_of(lax.div(me, inner)) + 4, 3
    )
    rest = inner - 1 - ((owner ^ me) & (inner - 1))
    if isinstance(owner, int):
        return LEGS.index(leg) * inner + rest
    turn = jnp.where(leg == LEGS[0], 0, jnp.where(leg == LEGS[1], 1, jnp.where(leg == LEGS[2], 2, 3)))
    return turn * inner + rest


def gray_of(x):
    return lax.bitwise_xor(x, lax.shift_right_logical(x, jnp.int32(1)))


def divider(by, top):
    for shift in range(8, 31):
        factor = -(-(1 << shift) // by)
        if all(n * factor >> shift == n // by for n in range(top + 1)):
            assert top * factor < 1 << 31
            return factor, shift
    raise ValueError(by)


def plan(row_count, per_device, cap, fronts, ids_ref, bound_ref, map_ref, order_ref, offset_ref, tag_ref, count_ref, rank_ref, key_ref):
    me, row = ids_ref[0], ids_ref[1]
    blocks = map_ref.shape[0]
    factor, shift = divider(per_device, fronts * row_count * per_device)
    assert row_count & (row_count - 1) == 0
    inner = fronts // 4

    def zero(i, carry):
        count_ref[i] = 0
        return carry

    def no_tag(i, carry):
        tag_ref[i] = per_device
        return carry

    def rank_one(j, carry):
        value = map_ref[j]
        holder = lax.shift_right_logical(value * factor, jnp.int32(shift))
        owner = lax.shift_right_logical(holder, jnp.int32(row_count.bit_length() - 1))
        there, here = (lax.shift_right_logical(x, jnp.int32(inner.bit_length() - 1)) for x in (owner, me))
        there, here = (lax.bitwise_xor(x, lax.shift_right_logical(x, jnp.int32(1))) for x in (there, here))
        leg = lax.bitwise_and(there - here, jnp.int32(3))
        turn = jnp.where(leg == LEGS[0], 0, jnp.where(leg == LEGS[1], 1, jnp.where(leg == LEGS[2], 2, 3)))
        key = turn * inner + (inner - 1) - lax.bitwise_and(lax.bitwise_xor(owner, me), jnp.int32(inner - 1))
        key = jnp.where((row * blocks + j) * BLOCK < bound_ref[0], key, fronts)
        rank = count_ref[key]
        count_ref[key] = rank + 1
        rank_ref[j] = rank
        key_ref[j] = key
        tag_ref[key * cap + rank] = value - holder * per_device
        return carry

    def start(i, total):
        offset_ref[i] = total
        return total + count_ref[i]

    def place(j, carry):
        order_ref[offset_ref[key_ref[j]] + rank_ref[j]] = j
        return carry

    lax.fori_loop(0, fronts + 1, zero, 0)
    lax.fori_loop(0, fronts * cap, no_tag, 0)
    lax.fori_loop(0, blocks, rank_one, 0)
    lax.fori_loop(0, fronts + 1, start, jnp.int32(0))
    lax.fori_loop(0, blocks, place, 0)


def call(kernel, operands, specs, outs, out_specs, flops, scratch=(), limit=None, **kw):
    space = 0
    for x in (*operands, *outs, *scratch):
        space += x.size * x.dtype.itemsize if hasattr(x, "size") else 0
    moved = sum(x.size * x.dtype.itemsize for x in (*operands, *outs))
    semantics = {"dimension_semantics": ("arbitrary",)} if "grid" in kw else {}
    return pl.pallas_call(
        kernel,
        out_shape=tuple(outs),
        in_specs=specs,
        out_specs=tuple(out_specs),
        scratch_shapes=[pltpu.VMEM(x.shape, x.dtype) if isinstance(x, jax.ShapeDtypeStruct) else x for x in scratch],
        compiler_params=pltpu.CompilerParams(vmem_limit_bytes=int(limit or space + 3 * MIB), **semantics),
        cost_estimate=pl.CostEstimate(flops=int(flops), bytes_accessed=int(moved), transcendentals=0),
        **kw,
    )(*operands)


def in_hbm(x):
    return pltpu.with_memory_space_constraint(x, pltpu.HBM)


def shape(rows, columns, dtype):
    return jax.ShapeDtypeStruct((rows, columns), dtype)


def program(bounds, block_map, pivot_inverse, upper_block, lower_block, trailing_block, sketch, basis):
    fronts, row_count = lax.axis_size("front"), lax.axis_size("row")
    assert fronts % 4 == 0 and fronts & (fronts - 1) == 0
    blocks = block_map.shape[1]
    per_device = basis.shape[1] // BLOCK
    cap = -(-blocks // fronts)
    depth, width = sketch.shape
    half = width // 2
    ids = jnp.stack([lax.axis_index("front"), lax.axis_index("row"), lax.axis_index("col")]).astype(jnp.int32)
    inverse, upper, lower, trailing, basis = pivot_inverse[0], upper_block[0], lower_block[0], trailing_block[0], basis[0]
    height, _ = lower.shape
    tall = upper.shape[0]
    groups, cuts = groups_of(fronts, cap)

    steps = 5 if depth % (5 * BLOCK) == 0 else 1
    tile = 4 * BLOCK if height % (4 * BLOCK) == 0 else BLOCK
    head = max(height // tile * 2 // 5, 1) * tile
    send_own, send_other, kept_own, kept_other, masked, top, order, offset, tags = call(
        functools.partial(pivot_kernel, (row_count, per_device, cap, fronts)),
        (ids, bounds, in_hbm(block_map.reshape(-1)), in_hbm(upper), in_hbm(sketch), in_hbm(trailing)),
        [SMEM, SMEM, ANY, ANY, ANY, ANY],
        (shape(tall, half, BF16),) * 2
        + (shape(tall, half, F32),) * 2
        + (shape(depth, width, BF16), shape(head, depth, BF16))
        + tuple(jax.ShapeDtypeStruct((n,), jnp.int32) for n in (blocks, fronts + 1, fronts * cap + blocks)),
        [VMEM] * 6 + [SMEM] * 3,
        2 * upper.size * width,
        scratch=(
            shape(tall, depth, BF16),
            shape(depth, width, BF16),
            shape(tall, width, F32),
            pltpu.SemaphoreType.DMA((steps,)),
            pltpu.SemaphoreType.DMA((steps,)),
            pltpu.SemaphoreType.DMA,
            pltpu.SemaphoreType.DMA,
            pltpu.SMEM((blocks,), jnp.int32),
            pltpu.SMEM((fronts + 1,), jnp.int32),
            pltpu.SMEM((blocks,), jnp.int32),
            pltpu.SMEM((blocks,), jnp.int32),
        ),
    )
    got_other = swap(send_own, "col")
    got_own = swap(send_other, "col")

    trail_own, trail_other = call(
        functools.partial(trailing_kernel, tile),
        (in_hbm(trailing), top, masked),
        [ANY, VMEM, VMEM],
        (shape(height, half, F32),) * 2,
        [VMEM] * 2,
        2 * trailing.size * width,
        scratch=(shape(height - head, depth, BF16), pltpu.SemaphoreType.DMA(((height - head) // tile,))),
    )

    def solve(kept, got):
        return call(solve_kernel, (inverse, kept, got), [VMEM] * 3, (shape(inverse.shape[0], half, F32),), [VMEM], 2 * inverse.size * half)[0]

    part_other = solve(kept_other, got_other)
    row_other = swap(part_other, "row")
    cuts = [min(c, blocks) for c in cuts]
    counts = [b - a for a, b in zip(cuts, cuts[1:])]
    sums = call(
        first_schur_kernel,
        (order, part_other, row_other, lower, trail_other),
        [SMEM] + [VMEM] * 4,
        (shape(counts[0] * BLOCK, half, BF16),),
        [VMEM],
        2 * lower.size * half,
    )
    sums += call(
        functools.partial(packed_schur_kernel, [a for a, n in zip(cuts[1:], counts[1:]) if n]),
        (order, part_other, row_other, lower, trail_other),
        [SMEM] + [VMEM] * 4,
        tuple(shape(n * BLOCK, half, BF16) for n in counts[1:] if n),
        [VMEM] * sum(n > 0 for n in counts[1:]),
        2 * lower.size * half,
        scratch=(shape(height, half, BF16),),
    )
    arrived = [swap(x, "col") for x in sums]
    part_own = solve(kept_own, got_own)
    row_own = swap(part_own, "row")

    pieces = []
    total = None
    for g, parts in enumerate(groups):
        if not parts:
            continue
        operands = [order, offset, tags, part_own, row_own, lower, trail_own]
        if counts[g]:
            operands.append(arrived[g])
        if g:
            operands.append(total)
        total, *made = call(
            functools.partial(add_kernel, parts, cap, cuts[g], counts[g], g == 0),
            operands,
            [SMEM] * 3 + [VMEM] * (len(operands) - 3),
            (shape(blocks * BLOCK, half, BF16),)
            + tuple(shape((high - low) * BLOCK + TAG_ROWS, half, BF16) for _, low, high in parts),
            [VMEM] * (1 + len(parts)),
            1e9,
            **({"input_output_aliases": {len(operands) - 1: 0}} if g else {}),
        )
        for (key, _, _), piece in zip(parts, made):
            pieces.append(away(piece, key, fronts) if key < fronts - 1 else piece)

    rank = basis.shape[1]
    rows = per_device * BLOCK
    flipped = call(flip_kernel, (basis,), [VMEM], (shape(rank, rows, BF16),), [VMEM], 1e9)[0]
    counted = [len(g) for g in groups]
    far = sum(counted[:3])
    near = far + sum(counted[3:5])
    end = near + counted[5]
    late = [near - 1, end - 1]
    waves = [[len(pieces) - 1] + list(range(far))]
    waves += [[i for i in range(far, len(pieces) - 1) if i not in late], late]
    parent = None
    for w, keys in enumerate(waves[:-1]):
        parent = call(
            functools.partial(early_kernel, per_device, w == 0),
            [pieces[k] for k in keys] + ([parent] if w else []),
            [VMEM] * (len(keys) + (w > 0)),
            (shape(rows, half, F32),),
            [VMEM],
            1e9,
            **({"input_output_aliases": {len(keys): 0}} if w else {}),
        )[0]
    parent, coeff = call(
        functools.partial(late_kernel, per_device),
        [flipped, parent] + [pieces[k] for k in waves[-1]],
        [VMEM] * (2 + len(waves[-1])),
        (shape(rows, half, F32), shape(rank, half, F32)),
        [VMEM] * 2,
        2 * basis.size * half,
        input_output_aliases={1: 0},
    )
    got = swap(coeff, "row")
    steps = 6 if per_device % 6 == 0 else 1
    coefficients, residual = call(
        residual_kernel,
        (basis, parent, coeff, got),
        [VMEM] * 4,
        (shape(rank, half, F32), shape(rows, half, F32)),
        [ANY] * 2,
        2 * basis.size * half,
        scratch=(
            shape(rank, half, F32),
            shape(rows, half, F32),
            pltpu.SemaphoreType.DMA,
            pltpu.SemaphoreType.DMA((steps,)),
        ),
    )
    return coefficients[None], residual[None]


def solution(mesh):
    placed = (
        P("front"),
        P("front", "row"),
        P("front", "col", "row"),
        P("front", "row", "col"),
        P("front", "row", "col"),
        P("front", "row", "col"),
        P("col", None),
        P("front", "row", None),
    )

    def step(*args):
        sharded = jax.shard_map(
            program,
            mesh=mesh,
            in_specs=placed,
            out_specs=(P("front", None, "col"), P("front", "row", "col")),
            check_vma=False,
        )
        return sharded(*args)

    return step
```

time: 112 us -> 89.4 us (0.80)
  starting transfers between devices: 40.2 us -> 28.7 us
  waiting for transfers between devices: 41.5 us -> 30 us
  Pallas kernels: 27.6 us -> 29 us
    ppermute x17 -> x20, waiting for transfers between devices: 41.5 us -> 30 us  [the longest x12 21.4 us: swap(): lax.ppermute(x, axis, [(i, i ^ 1) for i in range(lax.axis_size(axis))])]
    ppermute x17 -> x20, starting transfers between devices: 40.2 us -> 28.7 us  [the longest x8 18.6 us: away(): lax.ppermute(x, 'front', [(i, j) for i in range(fronts) for j in range(fr...]
    pallas_call x16 -> x18, Pallas kernels: 27.6 us -> 29 us  [call(): pl.pallas_call(kernel, out_shape=tuple(outs), in_specs=specs, out_specs=t...]
  transfers between devices with their start and end apart: 17 -> 20, of which waited for: 9 -> 9; matrix products, arithmetic and copies ran while one was open for 0% -> 0% of each run, Pallas kernels for 17% -> 22%
where the time goes in v3:
time: 89.4 us; the launch traced here: 89.2 us
  waiting for transfers between devices  30 us (34%)
  Pallas kernels  29 us (32%)
  starting transfers between devices  28.7 us (32%)
  between operations  1.52 us (2%)
    pallas_call x18, Pallas kernels, call(): pl.pallas_call(kernel, out_shape=tuple(outs), in_specs=specs, out_specs=t...  29 us
    ppermute x12, waiting for transfers between devices, swap(): lax.ppermute(x, axis, [(i, i ^ 1) for i in range(lax.axis_size(axis))])  21.4 us
    ppermute x8, starting transfers between devices, away(): lax.ppermute(x, 'front', [(i, j) for i in range(fronts) for j in range(fr...  18.6 us
    ppermute x12, starting transfers between devices, swap(): lax.ppermute(x, axis, [(i, i ^ 1) for i in range(lax.axis_size(axis))])  10.1 us
    ppermute x8, waiting for transfers between devices, away(): lax.ppermute(x, 'front', [(i, j) for i in range(fronts) for j in range(fr...  8.56 us
  transfers between devices with their start and end apart: 20, of which 9 were waited for; matrix products, arithmetic and copies ran while one was open for 0% of the time, Pallas kernels for 22%

profile of v3, /device:TPU:0, one launch (start us, length us, event | category | flops | bytes accessed | tf_op | source)
XLA Modules:
  0.0 89.2 jit_solution(9379910988037687790)
XLA Ops:
  1.3 0.1 pad_add_fusion.ids_ref
  1.4 5.4 %shard_map.96 = (bf16[512,256]{1,0:T(8,128)(2,1)S(1)}, bf16[512,256]{1,0:T(8,128)(2,1)S(1)}, f32[512,256]{1,0:T(8,128)S(1)}, f32[512,256]{1,0:T(8,128)S(1)}, bf1...) custom-call(s32[3]{0:T(128)S(1)} %pad_add_fusion.ids_ref, ...), custom_call_target="tpu_custom_call" | custom-call | flops 1342177280 | bytes 27787652 | tf_op jit(solution)/shard_map/pallas_call | solution.py:308
  6.7 3.0 %collective-permute-start.2 = (bf16[512,256]{1,0:T(8,128)(2,1)S(1)}, bf16[512,256]{1,0:T(8,128)(2,1)S(1)}, u32[]{:S(2)}, u32[]{:S(2)}) collective-permute-start(bf16[512,256]{1,0:T(8,128)(2,1)S(1)} %get-tuple-element.47), channel_id=1, source_target_pairs={{0,1},{1,0},{2,3},{3,2},{4,5},{5,4},{6,7},{7,6},{8,9},{9,8},{10,11... | collective-permute-start | bytes 786440 | tf_op jit(solution)/shard_map/ppermute | solution.py:204
  9.8 0.1 collective-permute-start
  9.8 7.1 %collective-permute-done.2.got_ref = bf16[512,256]{1,0:T(8,128)(2,1)S(1)} collective-permute-done((bf16[512,256]{1,0:T(8,128)(2,1)S(1)}, bf16[512,256]{1,0:T(8,128)(2,1)S(1)}, u32[]{:S(2)}, u32[]{:S(2)}) %collective-permute-start.2) | collective-permute-done | bytes 262176 | tf_op jit(solution)/shard_map/ppermute | solution.py:204
  16.9 0.0 copy-done.2
  16.9 0.3 shard_map.99.part_ref
  17.3 0.1 collective-permute-start.3
  17.3 4.4 %collective-permute-done.got_ref = bf16[512,256]{1,0:T(8,128)(2,1)S(1)} collective-permute-done((bf16[512,256]{1,0:T(8,128)(2,1)S(1)}, bf16[512,256]{1,0:T(8,128)(2,1)S(1)}, u32[]{:S(2)}, u32[]{:S(2)}) %collective-permute-start) | collective-permute-done | bytes 262176 | tf_op jit(solution)/shard_map/ppermute | solution.py:204
  21.7 0.3 shard_map.97.part_ref
  22.0 0.1 collective-permute-start.1
  22.1 0.0 copy-start
  22.1 7.5 %shard_map.98 = (f32[2560,256]{1,0:T(8,128)S(1)}, f32[2560,256]{1,0:T(8,128)S(1)}) custom-call(bf16[2560,2560]{1,0:T(8,128)(2,1)} %bitcast.25, bf16[1024,2560]{1,0:T(8,128)(2,1)S(1)} %get-tuple-element.43.head_ref, bf16[2560,512]{1,0:T(8,128)(2,1)S(1)} %get-tuple-element.44.masked_ref), custom_call_target="tpu_custom_call" | custom-call | flops 6710886400 | bytes 26214400 | tf_op jit(solution)/shard_map/pallas_call | solution.py:308
  29.6 0.0 collective-permute-done.3.got_ref
  29.6 0.0 copy-done
  29.6 0.7 shard_map.101
  30.3 1.8 %collective-permute-start.7 = (bf16[128,256]{1,0:T(8,128)(2,1)S(1)}, bf16[128,256]{1,0:T(8,128)(2,1)S(1)}, u32[]{:S(2)}, u32[]{:S(2)}) collective-permute-start(bf16[128,256]{1,0:T(8,128)(2,1)S(1)} %shard_map.101), channel_id=1, source_target_pairs={{0,1},{1,0},{2,3},{3,2},{4,5},{5,4},{6,7},{7,6},{8,9},{9,8},{10,11... | collective-permute-start | bytes 196616 | tf_op jit(solution)/shard_map/ppermute | solution.py:204
  32.1 1.5 %shard_map.100 = (bf16[256,256]{1,0:T(8,128)(2,1)S(1)}, bf16[384,256]{1,0:T(8,128)(2,1)S(1)}, bf16[384,256]{1,0:T(8,128)(2,1)S(1)}, bf16[384,256]{1,0:T(8,128)(2...) custom-call(s32[20]{0:T(128)S(1)} %get-tuple-element.38.order_ref, ...), custom_call_target="tpu_custom_call" | custom-call | flops 671088640 | bytes 7536720 | tf_op jit(solution)/shard_map/pallas_call | solution.py:308
  33.6 0.3 collective-permute-start.6
  34.0 1.7 %collective-permute-start.5 = (bf16[384,256]{1,0:T(8,128)(2,1)S(1)}, bf16[384,256]{1,0:T(8,128)(2,1)S(1)}, u32[]{:S(2)}, u32[]{:S(2)}) collective-permute-start(bf16[384,256]{1,0:T(8,128)(2,1)S(1)} %get-tuple-element.50), channel_id=1, source_target_pairs={{0,1},{1,0},{2,3},{3,2},{4,5},{5,4},{6,7},{7,6},{8,9},{9,8},{10,11... | collective-permute-start | bytes 589832 | tf_op jit(solution)/shard_map/ppermute | solution.py:204
  35.7 0.3 collective-permute-start.4
  36.0 0.0 collective-permute-done.1.row_ref
  36.0 1.7 %collective-permute-start.10 = (bf16[384,256]{1,0:T(8,128)(2,1)S(1)}, bf16[384,256]{1,0:T(8,128)(2,1)S(1)}, u32[]{:S(2)}, u32[]{:S(2)}) collective-permute-start(bf16[384,256]{1,0:T(8,128)(2,1)S(1)} %get-tuple-element.57), channel_id=1, source_target_pairs={{0,1},{1,0},{2,3},{3,2},{4,5},{5,4},{6,7},{7,6},{8,9},{9,8},{10,11... | collective-permute-start | bytes 589832 | tf_op jit(solution)/shard_map/ppermute | solution.py:204
  37.8 0.0 collective-permute-done.7.refs_0_
  37.8 0.3 collective-permute-start.9
  38.1 0.8 shard_map.102
  38.8 1.3 %collective-permute-done.6.refs_0_ = bf16[256,256]{1,0:T(8,128)(2,1)S(1)} collective-permute-done((bf16[256,256]{1,0:T(8,128)(2,1)S(1)}, bf16[256,256]{1,0:T(8,128)(2,1)S(1)}, u32[]{:S(2)}, u32[]{:S(2)}) %collective-permute-start.6) | collective-permute-done | bytes 131104 | tf_op jit(solution)/shard_map/ppermute | solution.py:204
  40.1 0.6 collective-permute-start.12
  40.6 0.8 shard_map.103
  41.4 2.9 %collective-permute-done.5.refs_0_ = bf16[384,256]{1,0:T(8,128)(2,1)S(1)} collective-permute-done((bf16[384,256]{1,0:T(8,128)(2,1)S(1)}, bf16[384,256]{1,0:T(8,128)(2,1)S(1)}, u32[]{:S(2)}, u32[]{:S(2)}) %collective-permute-start.5) | collective-permute-done | bytes 196640 | tf_op jit(solution)/shard_map/ppermute | solution.py:204
  44.3 4.5 %collective-permute-start.14 = (bf16[136,256]{1,0:T(8,128)(2,1)S(1)}, bf16[136,256]{1,0:T(8,128)(2,1)S(1)}, u32[]{:S(2)}, u32[]{:S(2)}) collective-permute-start(bf16[136,256]{1,0:T(8,128)(2,1)S(1)} %get-tuple-element.65), channel_id=1, source_target_pairs={{0,28},{4,24},{8,20},{12,16},{16,12},{20,8},{24,4},{28,0},{1,29},{... | collective-permute-start | bytes 208904 | tf_op jit(solution)/shard_map/ppermute | solution.py:208
  48.8 0.9 shard_map.104
  49.7 0.0 collective-permute-done.4.refs_0_
  49.7 3.3 %collective-permute-start.15 = (bf16[264,256]{1,0:T(8,128)(2,1)S(1)}, bf16[264,256]{1,0:T(8,128)(2,1)S(1)}, u32[]{:S(2)}, u32[]{:S(2)}) collective-permute-start(bf16[264,256]{1,0:T(8,128)(2,1)S(1)} %get-tuple-element.66), channel_id=1, source_target_pairs={{0,28},{4,24},{8,20},{12,16},{16,12},{20,8},{24,4},{28,0},{1,29},{... | collective-permute-start | bytes 405512 | tf_op jit(solution)/shard_map/ppermute | solution.py:208
  53.0 0.9 shard_map.105
  53.9 0.0 collective-permute-done.10.refs_0_
  53.9 2.4 %collective-permute-start.16 = (bf16[392,256]{1,0:T(8,128)(2,1)S(1)}, bf16[392,256]{1,0:T(8,128)(2,1)S(1)}, u32[]{:S(2)}, u32[]{:S(2)}) collective-permute-start(bf16[392,256]{1,0:T(8,128)(2,1)S(1)} %get-tuple-element.67), channel_id=1, source_target_pairs={{0,24},{4,28},{8,16},{12,20},{16,8},{20,12},{24,0},{28,4},{1,25},{... | collective-permute-start | bytes 602120 | tf_op jit(solution)/shard_map/ppermute | solution.py:208
  56.3 0.9 shard_map.106
  57.2 4.0 %collective-permute-done.9.refs_0_ = bf16[768,256]{1,0:T(8,128)(2,1)S(1)} collective-permute-done((bf16[768,256]{1,0:T(8,128)(2,1)S(1)}, bf16[768,256]{1,0:T(8,128)(2,1)S(1)}, u32[]{:S(2)}, u32[]{:S(2)}) %collective-permute-start.9) | collective-permute-done | bytes 393248 | tf_op jit(solution)/shard_map/ppermute | solution.py:204
  61.1 2.5 %collective-permute-start.8 = (bf16[392,256]{1,0:T(8,128)(2,1)S(1)}, bf16[392,256]{1,0:T(8,128)(2,1)S(1)}, u32[]{:S(2)}, u32[]{:S(2)}) collective-permute-start(bf16[392,256]{1,0:T(8,128)(2,1)S(1)} %get-tuple-element.55), channel_id=1, source_target_pairs={{0,12},{4,8},{8,28},{12,24},{16,4},{20,0},{24,20},{28,16},{1,13},{... | collective-permute-start | bytes 602120 | tf_op jit(solution)/shard_map/ppermute | solution.py:208
  63.7 1.0 %shard_map.107 = (bf16[2560,256]{1,0:T(8,128)(2,1)S(1)}, bf16[392,256]{1,0:T(8,128)(2,1)S(1)}, bf16[392,256]{1,0:T(8,128)(2,1)S(1)}) custom-call(s32[20]{0:T(128)S(1)} %get-tuple-element.38.order_ref, s32[9]{0:T(128)S(1)} %get-tuple-element.39.offset_ref, s32[44]{0:T(128)S(1)} %get-tuple-element.40.tag_ref, ...), custom_call_target="tpu_custom_call", output_to_operand_aliasing={{0}: (8, {})} | custom-call | flops 1000000000 | bytes 9707812 | tf_op jit(solution)/shard_map/pallas_call | solution.py:308
  64.7 0.0 collective-permute-done.12.refs_0_
  64.7 0.0 copy-start.1
  64.7 0.8 shard_map.108
  65.5 0.6 collective-permute-start.13
  66.1 0.0 collective-permute-done.14.refs_1_
  66.1 2.3 %collective-permute-start.11 = (bf16[392,256]{1,0:T(8,128)(2,1)S(1)}, bf16[392,256]{1,0:T(8,128)(2,1)S(1)}, u32[]{:S(2)}, u32[]{:S(2)}) collective-permute-start(bf16[392,256]{1,0:T(8,128)(2,1)S(1)} %get-tuple-element.60), channel_id=1, source_target_pairs={{0,20},{4,16},{8,4},{12,0},{16,28},{20,24},{24,12},{28,8},{1,21},{... | collective-permute-start | bytes 602120 | tf_op jit(solution)/shard_map/ppermute | solution.py:208
  68.4 0.0 collective-permute-done.15.refs_2_
  68.4 0.7 collective-permute-start.17
  69.1 0.0 collective-permute-done.16.refs_3_
  69.1 2.2 %collective-permute-start.18 = (bf16[392,256]{1,0:T(8,128)(2,1)S(1)}, bf16[392,256]{1,0:T(8,128)(2,1)S(1)}, u32[]{:S(2)}, u32[]{:S(2)}) collective-permute-start(bf16[392,256]{1,0:T(8,128)(2,1)S(1)} %get-tuple-element.69), channel_id=1, source_target_pairs={{0,16},{4,20},{8,0},{12,4},{16,24},{20,28},{24,8},{28,12},{1,17},{... | collective-permute-start | bytes 602120 | tf_op jit(solution)/shard_map/ppermute | solution.py:208
  71.3 0.0 copy-done.1
  71.3 0.9 %shard_map.95.refs_0_ = bf16[512,3072]{1,0:T(8,128)(2,1)S(1)} custom-call(bf16[3072,512]{1,0:T(8,128)(2,1)S(1)} %bitcast.20), custom_call_target="tpu_custom_call" | custom-call | flops 1000000000 | bytes 6291456 | tf_op jit(solution)/shard_map/pallas_call | solution.py:308
  72.2 1.3 %shard_map.109.refs_3_ = f32[3072,256]{1,0:T(8,128)S(1)} custom-call(bf16[392,256]{1,0:T(8,128)(2,1)S(1)} %get-tuple-element.64.refs_0_, bf16[136,256]{1,0:T(8,128)(2,1)S(1)} %collective-permute-done.14.refs_1_, bf16[264,256]{1,0:T(8,128)(2,1)S(1)} %collective-permute-done.15.refs_2_, bf16[392,256]{1,0:T(8,128)(2,1)S(1)} %collective-permute-done.16.refs_3_), custom_call_target="tpu_custom_call" | custom-call | flops 1000000000 | bytes 3751936 | tf_op jit(solution)/shard_map/pallas_call | solution.py:308
  73.6 0.0 collective-permute-done.8.refs_0_
  73.6 5.5 %collective-permute-done.13.refs_2_ = bf16[392,256]{1,0:T(8,128)(2,1)S(1)} collective-permute-done((bf16[392,256]{1,0:T(8,128)(2,1)S(1)}, bf16[392,256]{1,0:T(8,128)(2,1)S(1)}, u32[]{:S(2)}, u32[]{:S(2)}) %collective-permute-start.13) | collective-permute-done | bytes 200736 | tf_op jit(solution)/shard_map/ppermute | solution.py:208
  79.1 0.0 collective-permute-done.11.refs_1_
  79.1 1.2 %shard_map.110.refs_1_ = f32[3072,256]{1,0:T(8,128)S(1)} custom-call(bf16[392,256]{1,0:T(8,128)(2,1)S(1)} %collective-permute-done.8.refs_0_, bf16[392,256]{1,0:T(8,128)(2,1)S(1)} %collective-permute-done.11.refs_1_, bf16[392,256]{1,0:T(8,128)(2,1)S(1)} %collective-permute-done.13.refs_2_, ...), custom_call_target="tpu_custom_call", output_to_operand_aliasing={{}: (3, {})} | custom-call | flops 1000000000 | bytes 6893568 | tf_op jit(solution)/shard_map/pallas_call | solution.py:308
  80.3 1.0 %collective-permute-done.17.refs_2_ = bf16[392,256]{1,0:T(8,128)(2,1)S(1)} collective-permute-done((bf16[392,256]{1,0:T(8,128)(2,1)S(1)}, bf16[392,256]{1,0:T(8,128)(2,1)S(1)}, u32[]{:S(2)}, u32[]{:S(2)}) %collective-permute-start.17) | collective-permute-done | bytes 200736 | tf_op jit(solution)/shard_map/ppermute | solution.py:208
  81.3 2.0 %collective-permute-done.18.refs_3_ = bf16[392,256]{1,0:T(8,128)(2,1)S(1)} collective-permute-done((bf16[392,256]{1,0:T(8,128)(2,1)S(1)}, bf16[392,256]{1,0:T(8,128)(2,1)S(1)}, u32[]{:S(2)}, u32[]{:S(2)}) %collective-permute-start.18) | collective-permute-done | bytes 200736 | tf_op jit(solution)/shard_map/ppermute | solution.py:208
  83.3 1.8 %shard_map.111 = (f32[3072,256]{1,0:T(8,128)S(1)}, f32[512,256]{1,0:T(8,128)S(1)}) custom-call(bf16[512,3072]{1,0:T(8,128)(2,1)S(1)} %shard_map.95.refs_0_, f32[3072,256]{1,0:T(8,128)S(1)} %shard_map.110.refs_1_, bf16[392,256]{1,0:T(8,128)(2,1)S(1)} %collective-permute-done.17.refs_2_, ...), custom_call_target="tpu_custom_call", output_to_operand_aliasing={{0}: (1, {})} | custom-call | flops 805306368 | bytes 10362880 | tf_op jit(solution)/shard_map/pallas_call | solution.py:308
  85.1 0.1 collective-permute-start.19
  85.2 1.9 %collective-permute-done.19.got_ref = f32[512,256]{1,0:T(8,128)S(1)} collective-permute-done((f32[512,256]{1,0:T(8,128)S(1)}, f32[512,256]{1,0:T(8,128)S(1)}, u32[]{:S(2)}, u32[]{:S(2)}) %collective-permute-start.19) | collective-permute-done | bytes 524320 | tf_op jit(solution)/shard_map/ppermute | solution.py:204
  87.1 2.2 %shard_map.112 = (f32[512,256]{1,0:T(8,128)}, f32[3072,256]{1,0:T(8,128)}) custom-call(bf16[3072,512]{1,0:T(8,128)(2,1)S(1)} %bitcast.21, f32[3072,256]{1,0:T(8,128)S(1)} %get-tuple-element.70.parent_ref, f32[512,256]{1,0:T(8,128)S(1)} %get-tuple-element.71.part_ref, f32[512,256]{1,0:T(8,128)S(1)} %collective-permute-done.19.got_ref), custom_call_target="tpu_custom_call" | custom-call | flops 805306368 | bytes 11010048 | tf_op jit(solution)/shard_map/pallas_call | solution.py:308
  (1 shorter events, 0.0 us)
Async XLA Ops:
  1.4 15.6 %copy-start.2 = (bf16[1,512,512]{2,1,0:T(8,128)(2,1)S(1)}, bf16[1,512,512]{2,1,0:T(8,128)(2,1)}, u32[]{:S(2)}) copy-start(bf16[1,512,512]{2,1,0:T(8,128)(2,1)} %param.10) | copy-start | bytes 1572868
  6.7 10.2 %collective-permute-start.2 = (bf16[512,256]{1,0:T(8,128)(2,1)S(1)}, bf16[512,256]{1,0:T(8,128)(2,1)S(1)}, u32[]{:S(2)}, u32[]{:S(2)}) collective-permute-start(bf16[512,256]{1,0:T(8,128)(2,1)S(1)} %get-tuple-element.47), channel_id=1, source_target_pairs={{0,1},{1,0},{2,3},{3,2},{4,5},{5,4},{6,7},{7,6},{8,9},{9,8},{10,11... | collective-permute-start | bytes 786440 | tf_op jit(solution)/shard_map/ppermute | solution.py:204
  9.8 11.9 %collective-permute-start = (bf16[512,256]{1,0:T(8,128)(2,1)S(1)}, bf16[512,256]{1,0:T(8,128)(2,1)S(1)}, u32[]{:S(2)}, u32[]{:S(2)}) collective-permute-start(bf16[512,256]{1,0:T(8,128)(2,1)S(1)} %get-tuple-element.42), channel_id=1, source_target_pairs={{0,1},{1,0},{2,3},{3,2},{4,5},{5,4},{6,7},{7,6},{8,9},{9,8},{10,11... | collective-permute-start | bytes 786440 | tf_op jit(solution)/shard_map/ppermute | solution.py:204
  17.3 12.3 %collective-permute-start.3 = (f32[512,256]{1,0:T(8,128)S(1)}, f32[512,256]{1,0:T(8,128)S(1)}, u32[]{:S(2)}, u32[]{:S(2)}) collective-permute-start(f32[512,256]{1,0:T(8,128)S(1)} %shard_map.99.part_ref), channel_id=1, source_target_pairs={{0,2},{2,0},{1,3},{3,1},{4,6},{6,4},{5,7},{7,5},{8,10},{10,8},{9,1... | collective-permute-start | bytes 1572872 | tf_op jit(solution)/shard_map/ppermute | solution.py:204
  22.0 14.0 %collective-permute-start.1 = (f32[512,256]{1,0:T(8,128)S(1)}, f32[512,256]{1,0:T(8,128)S(1)}, u32[]{:S(2)}, u32[]{:S(2)}) collective-permute-start(f32[512,256]{1,0:T(8,128)S(1)} %shard_map.97.part_ref), channel_id=1, source_target_pairs={{0,2},{2,0},{1,3},{3,1},{4,6},{6,4},{5,7},{7,5},{8,10},{10,8},{9,1... | collective-permute-start | bytes 1572872 | tf_op jit(solution)/shard_map/ppermute | solution.py:204
  22.1 7.5 %copy-start = (bf16[1,2560,512]{2,1,0:T(8,128)(2,1)S(1)}, bf16[1,2560,512]{2,1,0:T(8,128)(2,1)}, u32[]{:S(2)}) copy-start(bf16[1,2560,512]{2,1,0:T(8,128)(2,1)} %param.12) | copy-start | bytes 7864324
  30.3 7.4 %collective-permute-start.7 = (bf16[128,256]{1,0:T(8,128)(2,1)S(1)}, bf16[128,256]{1,0:T(8,128)(2,1)S(1)}, u32[]{:S(2)}, u32[]{:S(2)}) collective-permute-start(bf16[128,256]{1,0:T(8,128)(2,1)S(1)} %shard_map.101), channel_id=1, source_target_pairs={{0,1},{1,0},{2,3},{3,2},{4,5},{5,4},{6,7},{7,6},{8,9},{9,8},{10,11... | collective-permute-start | bytes 196616 | tf_op jit(solution)/shard_map/ppermute | solution.py:204
  33.6 6.4 %collective-permute-start.6 = (bf16[256,256]{1,0:T(8,128)(2,1)S(1)}, bf16[256,256]{1,0:T(8,128)(2,1)S(1)}, u32[]{:S(2)}, u32[]{:S(2)}) collective-permute-start(bf16[256,256]{1,0:T(8,128)(2,1)S(1)} %get-tuple-element.51), channel_id=1, source_target_pairs={{0,1},{1,0},{2,3},{3,2},{4,5},{5,4},{6,7},{7,6},{8,9},{9,8},{10,11... | collective-permute-start | bytes 393224 | tf_op jit(solution)/shard_map/ppermute | solution.py:204
  34.0 10.3 %collective-permute-start.5 = (bf16[384,256]{1,0:T(8,128)(2,1)S(1)}, bf16[384,256]{1,0:T(8,128)(2,1)S(1)}, u32[]{:S(2)}, u32[]{:S(2)}) collective-permute-start(bf16[384,256]{1,0:T(8,128)(2,1)S(1)} %get-tuple-element.50), channel_id=1, source_target_pairs={{0,1},{1,0},{2,3},{3,2},{4,5},{5,4},{6,7},{7,6},{8,9},{9,8},{10,11... | collective-permute-start | bytes 589832 | tf_op jit(solution)/shard_map/ppermute | solution.py:204
  35.7 14.0 %collective-permute-start.4 = (bf16[384,256]{1,0:T(8,128)(2,1)S(1)}, bf16[384,256]{1,0:T(8,128)(2,1)S(1)}, u32[]{:S(2)}, u32[]{:S(2)}) collective-permute-start(bf16[384,256]{1,0:T(8,128)(2,1)S(1)} %get-tuple-element.49), channel_id=1, source_target_pairs={{0,1},{1,0},{2,3},{3,2},{4,5},{5,4},{6,7},{7,6},{8,9},{9,8},{10,11... | collective-permute-start | bytes 589832 | tf_op jit(solution)/shard_map/ppermute | solution.py:204
  36.0 17.9 %collective-permute-start.10 = (bf16[384,256]{1,0:T(8,128)(2,1)S(1)}, bf16[384,256]{1,0:T(8,128)(2,1)S(1)}, u32[]{:S(2)}, u32[]{:S(2)}) collective-permute-start(bf16[384,256]{1,0:T(8,128)(2,1)S(1)} %get-tuple-element.57), channel_id=1, source_target_pairs={{0,1},{1,0},{2,3},{3,2},{4,5},{5,4},{6,7},{7,6},{8,9},{9,8},{10,11... | collective-permute-start | bytes 589832 | tf_op jit(solution)/shard_map/ppermute | solution.py:204
  37.8 23.4 %collective-permute-start.9 = (bf16[768,256]{1,0:T(8,128)(2,1)S(1)}, bf16[768,256]{1,0:T(8,128)(2,1)S(1)}, u32[]{:S(2)}, u32[]{:S(2)}) collective-permute-start(bf16[768,256]{1,0:T(8,128)(2,1)S(1)} %get-tuple-element.56), channel_id=1, source_target_pairs={{0,1},{1,0},{2,3},{3,2},{4,5},{5,4},{6,7},{7,6},{8,9},{9,8},{10,11... | collective-permute-start | bytes 1179656 | tf_op jit(solution)/shard_map/ppermute | solution.py:204
  40.1 24.6 %collective-permute-start.12 = (bf16[256,256]{1,0:T(8,128)(2,1)S(1)}, bf16[256,256]{1,0:T(8,128)(2,1)S(1)}, u32[]{:S(2)}, u32[]{:S(2)}) collective-permute-start(bf16[256,256]{1,0:T(8,128)(2,1)S(1)} %get-tuple-element.61), channel_id=1, source_target_pairs={{0,1},{1,0},{2,3},{3,2},{4,5},{5,4},{6,7},{7,6},{8,9},{9,8},{10,11... | collective-permute-start | bytes 393224 | tf_op jit(solution)/shard_map/ppermute | solution.py:204
  44.3 21.8 %collective-permute-start.14 = (bf16[136,256]{1,0:T(8,128)(2,1)S(1)}, bf16[136,256]{1,0:T(8,128)(2,1)S(1)}, u32[]{:S(2)}, u32[]{:S(2)}) collective-permute-start(bf16[136,256]{1,0:T(8,128)(2,1)S(1)} %get-tuple-element.65), channel_id=1, source_target_pairs={{0,28},{4,24},{8,20},{12,16},{16,12},{20,8},{24,4},{28,0},{1,29},{... | collective-permute-start | bytes 208904 | tf_op jit(solution)/shard_map/ppermute | solution.py:208
  49.7 18.7 %collective-permute-start.15 = (bf16[264,256]{1,0:T(8,128)(2,1)S(1)}, bf16[264,256]{1,0:T(8,128)(2,1)S(1)}, u32[]{:S(2)}, u32[]{:S(2)}) collective-permute-start(bf16[264,256]{1,0:T(8,128)(2,1)S(1)} %get-tuple-element.66), channel_id=1, source_target_pairs={{0,28},{4,24},{8,20},{12,16},{16,12},{20,8},{24,4},{28,0},{1,29},{... | collective-permute-start | bytes 405512 | tf_op jit(solution)/shard_map/ppermute | solution.py:208
  53.9 15.1 %collective-permute-start.16 = (bf16[392,256]{1,0:T(8,128)(2,1)S(1)}, bf16[392,256]{1,0:T(8,128)(2,1)S(1)}, u32[]{:S(2)}, u32[]{:S(2)}) collective-permute-start(bf16[392,256]{1,0:T(8,128)(2,1)S(1)} %get-tuple-element.67), channel_id=1, source_target_pairs={{0,24},{4,28},{8,16},{12,20},{16,8},{20,12},{24,0},{28,4},{1,25},{... | collective-permute-start | bytes 602120 | tf_op jit(solution)/shard_map/ppermute | solution.py:208
  61.1 12.4 %collective-permute-start.8 = (bf16[392,256]{1,0:T(8,128)(2,1)S(1)}, bf16[392,256]{1,0:T(8,128)(2,1)S(1)}, u32[]{:S(2)}, u32[]{:S(2)}) collective-permute-start(bf16[392,256]{1,0:T(8,128)(2,1)S(1)} %get-tuple-element.55), channel_id=1, source_target_pairs={{0,12},{4,8},{8,28},{12,24},{16,4},{20,0},{24,20},{28,16},{1,13},{... | collective-permute-start | bytes 602120 | tf_op jit(solution)/shard_map/ppermute | solution.py:208
  64.7 6.6 %copy-start.1 = (bf16[1,3072,512]{2,1,0:T(8,128)(2,1)S(1)}, bf16[1,3072,512]{2,1,0:T(8,128)(2,1)}, u32[]{:S(2)}) copy-start(bf16[1,3072,512]{2,1,0:T(8,128)(2,1)} %param.15) | copy-start | bytes 9437188
  65.5 13.6 %collective-permute-start.13 = (bf16[392,256]{1,0:T(8,128)(2,1)S(1)}, bf16[392,256]{1,0:T(8,128)(2,1)S(1)}, u32[]{:S(2)}, u32[]{:S(2)}) collective-permute-start(bf16[392,256]{1,0:T(8,128)(2,1)S(1)} %get-tuple-element.63), channel_id=1, source_target_pairs={{0,4},{4,0},{8,12},{12,8},{16,20},{20,16},{24,28},{28,24},{1,5},{5... | collective-permute-start | bytes 602120 | tf_op jit(solution)/shard_map/ppermute | solution.py:208
  66.1 13.0 %collective-permute-start.11 = (bf16[392,256]{1,0:T(8,128)(2,1)S(1)}, bf16[392,256]{1,0:T(8,128)(2,1)S(1)}, u32[]{:S(2)}, u32[]{:S(2)}) collective-permute-start(bf16[392,256]{1,0:T(8,128)(2,1)S(1)} %get-tuple-element.60), channel_id=1, source_target_pairs={{0,20},{4,16},{8,4},{12,0},{16,28},{20,24},{24,12},{28,8},{1,21},{... | collective-permute-start | bytes 602120 | tf_op jit(solution)/shard_map/ppermute | solution.py:208
  68.4 12.9 %collective-permute-start.17 = (bf16[392,256]{1,0:T(8,128)(2,1)S(1)}, bf16[392,256]{1,0:T(8,128)(2,1)S(1)}, u32[]{:S(2)}, u32[]{:S(2)}) collective-permute-start(bf16[392,256]{1,0:T(8,128)(2,1)S(1)} %get-tuple-element.68), channel_id=1, source_target_pairs={{0,8},{4,12},{8,24},{12,28},{16,0},{20,4},{24,16},{28,20},{1,9},{5... | collective-permute-start | bytes 602120 | tf_op jit(solution)/shard_map/ppermute | solution.py:208
  69.1 14.2 %collective-permute-start.18 = (bf16[392,256]{1,0:T(8,128)(2,1)S(1)}, bf16[392,256]{1,0:T(8,128)(2,1)S(1)}, u32[]{:S(2)}, u32[]{:S(2)}) collective-permute-start(bf16[392,256]{1,0:T(8,128)(2,1)S(1)} %get-tuple-element.69), channel_id=1, source_target_pairs={{0,16},{4,20},{8,0},{12,4},{16,24},{20,28},{24,8},{28,12},{1,17},{... | collective-permute-start | bytes 602120 | tf_op jit(solution)/shard_map/ppermute | solution.py:208
  85.1 2.0 %collective-permute-start.19 = (f32[512,256]{1,0:T(8,128)S(1)}, f32[512,256]{1,0:T(8,128)S(1)}, u32[]{:S(2)}, u32[]{:S(2)}) collective-permute-start(f32[512,256]{1,0:T(8,128)S(1)} %get-tuple-element.71.part_ref), channel_id=1, source_target_pairs={{0,2},{2,0},{1,3},{3,1},{4,6},{6,4},{5,7},{7,5},{8,10},{10,8},{9,1... | collective-permute-start | bytes 1572872 | tf_op jit(solution)/shard_map/ppermute | solution.py:204

commit v4 on v3

--- a/solution.py
+++ b/solution.py
@@ -212,7 +212,7 @@
 
 def groups_of(fronts, cap):
     total = fronts * cap
-    cuts = [0, 1, total // 8, total // 4, 3 * total // 8, total // 2, 3 * total // 4, total]
+    cuts = [0, 2, total // 8, total // 4, 3 * total // 8, total // 2, 3 * total // 4, total]
     groups = []
     for a, b in zip(cuts, cuts[1:]):
         keys = range(a // cap, -(-b // cap))
@@ -433,13 +433,11 @@
     rank = basis.shape[1]
     rows = per_device * BLOCK
     flipped = call(flip_kernel, (basis,), [VMEM], (shape(rank, rows, BF16),), [VMEM], 1e9)[0]
-    counted = [len(g) for g in groups]
-    far = sum(counted[:3])
-    near = far + sum(counted[3:5])
-    end = near + counted[5]
-    late = [near - 1, end - 1]
+    inner, extra = fronts // 4, int(cap > 1)
+    far = inner + extra
+    late, middle = 2 * inner - 1 + extra, [len(pieces) - 2, 3 * inner - 1 + extra]
     waves = [[len(pieces) - 1] + list(range(far))]
-    waves += [[i for i in range(far, len(pieces) - 1) if i not in late], late]
+    waves += [[i for i in range(far, len(pieces) - 2) if i not in (late, *middle)], middle, [late]]
     parent = None
     for w, keys in enumerate(waves[:-1]):
         parent = call(

time: 89.4 us -> 89.3 us (level)
  starting transfers between devices: 28.7 us -> 27.3 us
  waiting for transfers between devices: 30 us -> 31.3 us
    ppermute x8, starting transfers between devices: 18.6 us -> 16 us  [away(): lax.ppermute(x, 'front', [(i, j) for i in range(fronts) for j in range(fr...]
    ppermute x8, waiting for transfers between devices: 8.56 us -> 10.7 us  [away(): lax.ppermute(x, 'front', [(i, j) for i in range(fronts) for j in range(fr...]
    ppermute x12, starting transfers between devices: 10.1 us -> 11.3 us  [swap(): lax.ppermute(x, axis, [(i, i ^ 1) for i in range(lax.axis_size(axis))])]
    pallas_call x18 -> x19, Pallas kernels: 29 us -> 29 us  [call(): pl.pallas_call(kernel, out_shape=tuple(outs), in_specs=specs, out_specs=t...]
  transfers between devices with their start and end apart: 20 -> 20, of which waited for: 9 -> 7; matrix products, arithmetic and copies ran while one was open for 0% -> 0% of each run, Pallas kernels for 22% -> 22%
where the time goes in v4:
time: 89.3 us; the launch traced here: 89.2 us
  waiting for transfers between devices  31.3 us (35%)
  Pallas kernels  29 us (32%)
  starting transfers between devices  27.3 us (31%)
  between operations  1.54 us (2%)
    pallas_call x19, Pallas kernels, call(): pl.pallas_call(kernel, out_shape=tuple(outs), in_specs=specs, out_specs=t...  29 us
    ppermute x12, waiting for transfers between devices, swap(): lax.ppermute(x, axis, [(i, i ^ 1) for i in range(lax.axis_size(axis))])  20.6 us
    ppermute x8, starting transfers between devices, away(): lax.ppermute(x, 'front', [(i, j) for i in range(fronts) for j in range(fr...  16 us
    ppermute x12, starting transfers between devices, swap(): lax.ppermute(x, axis, [(i, i ^ 1) for i in range(lax.axis_size(axis))])  11.3 us
    ppermute x8, waiting for transfers between devices, away(): lax.ppermute(x, 'front', [(i, j) for i in range(fronts) for j in range(fr...  10.7 us
  transfers between devices with their start and end apart: 20, of which 7 were waited for; matrix products, arithmetic and copies ran while one was open for 0% of the time, Pallas kernels for 22%

profile of v4, /device:TPU:0, one launch (start us, length us, event | category | flops | bytes accessed | tf_op | source)
XLA Modules:
  0.0 89.2 jit_solution(12456402174222980148)
XLA Ops:
  1.3 0.1 pad_add_fusion.ids_ref
  1.4 5.4 %shard_map.96 = (bf16[512,256]{1,0:T(8,128)(2,1)S(1)}, bf16[512,256]{1,0:T(8,128)(2,1)S(1)}, f32[512,256]{1,0:T(8,128)S(1)}, f32[512,256]{1,0:T(8,128)S(1)}, bf1...) custom-call(s32[3]{0:T(128)S(1)} %pad_add_fusion.ids_ref, ...), custom_call_target="tpu_custom_call" | custom-call | flops 1342177280 | bytes 27787652 | tf_op jit(solution)/shard_map/pallas_call | solution.py:308
  6.7 3.0 %collective-permute-start.2 = (bf16[512,256]{1,0:T(8,128)(2,1)S(1)}, bf16[512,256]{1,0:T(8,128)(2,1)S(1)}, u32[]{:S(2)}, u32[]{:S(2)}) collective-permute-start(bf16[512,256]{1,0:T(8,128)(2,1)S(1)} %get-tuple-element.47), channel_id=1, source_target_pairs={{0,1},{1,0},{2,3},{3,2},{4,5},{5,4},{6,7},{7,6},{8,9},{9,8},{10,11... | collective-permute-start | bytes 786440 | tf_op jit(solution)/shard_map/ppermute | solution.py:204
  9.8 0.1 collective-permute-start
  9.8 7.1 %collective-permute-done.2.got_ref = bf16[512,256]{1,0:T(8,128)(2,1)S(1)} collective-permute-done((bf16[512,256]{1,0:T(8,128)(2,1)S(1)}, bf16[512,256]{1,0:T(8,128)(2,1)S(1)}, u32[]{:S(2)}, u32[]{:S(2)}) %collective-permute-start.2) | collective-permute-done | bytes 262176 | tf_op jit(solution)/shard_map/ppermute | solution.py:204
  16.9 0.0 copy-done.2
  16.9 0.3 shard_map.99.part_ref
  17.3 0.1 collective-permute-start.3
  17.3 4.4 %collective-permute-done.got_ref = bf16[512,256]{1,0:T(8,128)(2,1)S(1)} collective-permute-done((bf16[512,256]{1,0:T(8,128)(2,1)S(1)}, bf16[512,256]{1,0:T(8,128)(2,1)S(1)}, u32[]{:S(2)}, u32[]{:S(2)}) %collective-permute-start) | collective-permute-done | bytes 262176 | tf_op jit(solution)/shard_map/ppermute | solution.py:204
  21.7 0.3 shard_map.97.part_ref
  22.0 0.1 collective-permute-start.1
  22.1 0.0 copy-start
  22.1 7.5 %shard_map.98 = (f32[2560,256]{1,0:T(8,128)S(1)}, f32[2560,256]{1,0:T(8,128)S(1)}) custom-call(bf16[2560,2560]{1,0:T(8,128)(2,1)} %bitcast.25, bf16[1024,2560]{1,0:T(8,128)(2,1)S(1)} %get-tuple-element.43.head_ref, bf16[2560,512]{1,0:T(8,128)(2,1)S(1)} %get-tuple-element.44.masked_ref), custom_call_target="tpu_custom_call" | custom-call | flops 6710886400 | bytes 26214400 | tf_op jit(solution)/shard_map/pallas_call | solution.py:308
  29.6 0.0 collective-permute-done.3.got_ref
  29.6 0.0 copy-done
  29.6 0.8 shard_map.101
  30.4 1.8 %collective-permute-start.10 = (bf16[256,256]{1,0:T(8,128)(2,1)S(1)}, bf16[256,256]{1,0:T(8,128)(2,1)S(1)}, u32[]{:S(2)}, u32[]{:S(2)}) collective-permute-start(bf16[256,256]{1,0:T(8,128)(2,1)S(1)} %shard_map.101), channel_id=1, source_target_pairs={{0,1},{1,0},{2,3},{3,2},{4,5},{5,4},{6,7},{7,6},{8,9},{9,8},{10,11... | collective-permute-start | bytes 393224 | tf_op jit(solution)/shard_map/ppermute | solution.py:204
  32.2 1.5 %shard_map.100 = (bf16[128,256]{1,0:T(8,128)(2,1)S(1)}, bf16[384,256]{1,0:T(8,128)(2,1)S(1)}, bf16[384,256]{1,0:T(8,128)(2,1)S(1)}, bf16[384,256]{1,0:T(8,128)(2...) custom-call(s32[20]{0:T(128)S(1)} %get-tuple-element.38.order_ref, ...), custom_call_target="tpu_custom_call" | custom-call | flops 671088640 | bytes 7471184 | tf_op jit(solution)/shard_map/pallas_call | solution.py:308
  33.7 0.3 collective-permute-start.8
  34.0 1.7 %collective-permute-start.9 = (bf16[128,256]{1,0:T(8,128)(2,1)S(1)}, bf16[128,256]{1,0:T(8,128)(2,1)S(1)}, u32[]{:S(2)}, u32[]{:S(2)}) collective-permute-start(bf16[128,256]{1,0:T(8,128)(2,1)S(1)} %get-tuple-element.54), channel_id=1, source_target_pairs={{0,1},{1,0},{2,3},{3,2},{4,5},{5,4},{6,7},{7,6},{8,9},{9,8},{10,11... | collective-permute-start | bytes 196616 | tf_op jit(solution)/shard_map/ppermute | solution.py:204
  35.8 0.3 collective-permute-start.7
  36.0 0.0 collective-permute-done.1.row_ref
  36.0 1.7 %collective-permute-start.6 = (bf16[384,256]{1,0:T(8,128)(2,1)S(1)}, bf16[384,256]{1,0:T(8,128)(2,1)S(1)}, u32[]{:S(2)}, u32[]{:S(2)}) collective-permute-start(bf16[384,256]{1,0:T(8,128)(2,1)S(1)} %get-tuple-element.51), channel_id=1, source_target_pairs={{0,1},{1,0},{2,3},{3,2},{4,5},{5,4},{6,7},{7,6},{8,9},{9,8},{10,11... | collective-permute-start | bytes 589832 | tf_op jit(solution)/shard_map/ppermute | solution.py:204
  37.8 0.0 collective-permute-done.10.refs_0_
  37.8 0.8 collective-permute-start.5
  38.5 0.8 shard_map.102
  39.4 3.6 %collective-permute-done.9.refs_0_ = bf16[128,256]{1,0:T(8,128)(2,1)S(1)} collective-permute-done((bf16[128,256]{1,0:T(8,128)(2,1)S(1)}, bf16[128,256]{1,0:T(8,128)(2,1)S(1)}, u32[]{:S(2)}, u32[]{:S(2)}) %collective-permute-start.9) | collective-permute-done | bytes 65568 | tf_op jit(solution)/shard_map/ppermute | solution.py:204
  42.9 1.2 %collective-permute-start.4 = (bf16[256,256]{1,0:T(8,128)(2,1)S(1)}, bf16[256,256]{1,0:T(8,128)(2,1)S(1)}, u32[]{:S(2)}, u32[]{:S(2)}) collective-permute-start(bf16[256,256]{1,0:T(8,128)(2,1)S(1)} %get-tuple-element.49), channel_id=1, source_target_pairs={{0,1},{1,0},{2,3},{3,2},{4,5},{5,4},{6,7},{7,6},{8,9},{9,8},{10,11... | collective-permute-start | bytes 393224 | tf_op jit(solution)/shard_map/ppermute | solution.py:204
  44.2 0.8 shard_map.103
  44.9 0.0 collective-permute-done.8.refs_0_
  44.9 4.6 %collective-permute-start.16 = (bf16[136,256]{1,0:T(8,128)(2,1)S(1)}, bf16[136,256]{1,0:T(8,128)(2,1)S(1)}, u32[]{:S(2)}, u32[]{:S(2)}) collective-permute-start(bf16[136,256]{1,0:T(8,128)(2,1)S(1)} %get-tuple-element.67), channel_id=1, source_target_pairs={{0,28},{4,24},{8,20},{12,16},{16,12},{20,8},{24,4},{28,0},{1,29},{... | collective-permute-start | bytes 208904 | tf_op jit(solution)/shard_map/ppermute | solution.py:208
  49.6 0.9 shard_map.104
  50.4 0.0 collective-permute-done.7.refs_0_
  50.4 1.2 %collective-permute-start.15 = (bf16[264,256]{1,0:T(8,128)(2,1)S(1)}, bf16[264,256]{1,0:T(8,128)(2,1)S(1)}, u32[]{:S(2)}, u32[]{:S(2)}) collective-permute-start(bf16[264,256]{1,0:T(8,128)(2,1)S(1)} %get-tuple-element.66), channel_id=1, source_target_pairs={{0,28},{4,24},{8,20},{12,16},{16,12},{20,8},{24,4},{28,0},{1,29},{... | collective-permute-start | bytes 405512 | tf_op jit(solution)/shard_map/ppermute | solution.py:208
  51.7 0.9 shard_map.105
  52.5 0.0 collective-permute-done.6.refs_0_
  52.5 2.6 %collective-permute-start.17 = (bf16[392,256]{1,0:T(8,128)(2,1)S(1)}, bf16[392,256]{1,0:T(8,128)(2,1)S(1)}, u32[]{:S(2)}, u32[]{:S(2)}) collective-permute-start(bf16[392,256]{1,0:T(8,128)(2,1)S(1)} %get-tuple-element.68), channel_id=1, source_target_pairs={{0,24},{4,28},{8,16},{12,20},{16,8},{20,12},{24,0},{28,4},{1,25},{... | collective-permute-start | bytes 602120 | tf_op jit(solution)/shard_map/ppermute | solution.py:208
  55.2 0.9 shard_map.106
  56.1 3.7 %collective-permute-done.5.refs_0_ = bf16[768,256]{1,0:T(8,128)(2,1)S(1)} collective-permute-done((bf16[768,256]{1,0:T(8,128)(2,1)S(1)}, bf16[768,256]{1,0:T(8,128)(2,1)S(1)}, u32[]{:S(2)}, u32[]{:S(2)}) %collective-permute-start.5) | collective-permute-done | bytes 393248 | tf_op jit(solution)/shard_map/ppermute | solution.py:204
  59.8 2.5 %collective-permute-start.13 = (bf16[392,256]{1,0:T(8,128)(2,1)S(1)}, bf16[392,256]{1,0:T(8,128)(2,1)S(1)}, u32[]{:S(2)}, u32[]{:S(2)}) collective-permute-start(bf16[392,256]{1,0:T(8,128)(2,1)S(1)} %get-tuple-element.63), channel_id=1, source_target_pairs={{0,12},{4,8},{8,28},{12,24},{16,4},{20,0},{24,20},{28,16},{1,13},{... | collective-permute-start | bytes 602120 | tf_op jit(solution)/shard_map/ppermute | solution.py:208
  62.3 1.0 %shard_map.107 = (bf16[2560,256]{1,0:T(8,128)(2,1)S(1)}, bf16[392,256]{1,0:T(8,128)(2,1)S(1)}, bf16[392,256]{1,0:T(8,128)(2,1)S(1)}) custom-call(s32[20]{0:T(128)S(1)} %get-tuple-element.38.order_ref, s32[9]{0:T(128)S(1)} %get-tuple-element.39.offset_ref, s32[44]{0:T(128)S(1)} %get-tuple-element.40.tag_ref, ...), custom_call_target="tpu_custom_call", output_to_operand_aliasing={{0}: (8, {})} | custom-call | flops 1000000000 | bytes 9707812 | tf_op jit(solution)/shard_map/pallas_call | solution.py:308
  63.3 0.0 collective-permute-done.4.refs_0_
  63.3 2.1 %collective-permute-start.14 = (bf16[392,256]{1,0:T(8,128)(2,1)S(1)}, bf16[392,256]{1,0:T(8,128)(2,1)S(1)}, u32[]{:S(2)}, u32[]{:S(2)}) collective-permute-start(bf16[392,256]{1,0:T(8,128)(2,1)S(1)} %get-tuple-element.64), channel_id=1, source_target_pairs={{0,20},{4,16},{8,4},{12,0},{16,28},{20,24},{24,12},{28,8},{1,21},{... | collective-permute-start | bytes 602120 | tf_op jit(solution)/shard_map/ppermute | solution.py:208
  65.4 0.8 shard_map.108
  66.2 0.0 collective-permute-done.16.refs_2_
  66.2 0.8 collective-permute-start.11
  67.0 0.0 collective-permute-done.15.refs_1_
  67.0 1.7 %collective-permute-start.12 = (bf16[392,256]{1,0:T(8,128)(2,1)S(1)}, bf16[392,256]{1,0:T(8,128)(2,1)S(1)}, u32[]{:S(2)}, u32[]{:S(2)}) collective-permute-start(bf16[392,256]{1,0:T(8,128)(2,1)S(1)} %get-tuple-element.62), channel_id=1, source_target_pairs={{0,16},{4,20},{8,0},{12,4},{16,24},{20,28},{24,8},{28,12},{1,17},{... | collective-permute-start | bytes 602120 | tf_op jit(solution)/shard_map/ppermute | solution.py:208
  68.7 0.0 copy-done.1
  68.7 0.9 %shard_map.95.refs_0_ = bf16[512,3072]{1,0:T(8,128)(2,1)S(1)} custom-call(bf16[3072,512]{1,0:T(8,128)(2,1)S(1)} %bitcast.20), custom_call_target="tpu_custom_call" | custom-call | flops 1000000000 | bytes 6291456 | tf_op jit(solution)/shard_map/pallas_call | solution.py:308
  69.7 0.0 collective-permute-done.17.refs_3_
  69.7 0.4 collective-permute-start.18
  70.1 1.3 %shard_map.109.refs_2_ = f32[3072,256]{1,0:T(8,128)S(1)} custom-call(bf16[392,256]{1,0:T(8,128)(2,1)S(1)} %get-tuple-element.65.refs_0_, bf16[264,256]{1,0:T(8,128)(2,1)S(1)} %collective-permute-done.15.refs_1_, bf16[136,256]{1,0:T(8,128)(2,1)S(1)} %collective-permute-done.16.refs_2_, bf16[392,256]{1,0:T(8,128)(2,1)S(1)} %collective-permute-done.17.refs_3_), custom_call_target="tpu_custom_call" | custom-call | flops 1000000000 | bytes 3751936 | tf_op jit(solution)/shard_map/pallas_call | solution.py:308
  71.4 9.3 %collective-permute-done.13.refs_0_ = bf16[392,256]{1,0:T(8,128)(2,1)S(1)} collective-permute-done((bf16[392,256]{1,0:T(8,128)(2,1)S(1)}, bf16[392,256]{1,0:T(8,128)(2,1)S(1)}, u32[]{:S(2)}, u32[]{:S(2)}) %collective-permute-start.13) | collective-permute-done | bytes 200736 | tf_op jit(solution)/shard_map/ppermute | solution.py:208
  80.7 0.0 collective-permute-done.14.refs_1_
  80.7 0.8 shard_map.110.refs_2_
  81.5 0.0 collective-permute-done.11.refs_0_
  81.5 0.0 collective-permute-done.12.refs_1_
  81.5 0.8 shard_map.111.refs_1_
  82.3 1.3 %collective-permute-done.18.refs_2_ = bf16[392,256]{1,0:T(8,128)(2,1)S(1)} collective-permute-done((bf16[392,256]{1,0:T(8,128)(2,1)S(1)}, bf16[392,256]{1,0:T(8,128)(2,1)S(1)}, u32[]{:S(2)}, u32[]{:S(2)}) %collective-permute-start.18) | collective-permute-done | bytes 200736 | tf_op jit(solution)/shard_map/ppermute | solution.py:208
  83.6 1.4 %shard_map.112 = (f32[3072,256]{1,0:T(8,128)S(1)}, f32[512,256]{1,0:T(8,128)S(1)}) custom-call(bf16[512,3072]{1,0:T(8,128)(2,1)S(1)} %shard_map.95.refs_0_, f32[3072,256]{1,0:T(8,128)S(1)} %shard_map.111.refs_1_, bf16[392,256]{1,0:T(8,128)(2,1)S(1)} %collective-permute-done.18.refs_2_), custom_call_target="tpu_custom_call", output_to_operand_aliasing={{0}: (1, {})} | custom-call | flops 805306368 | bytes 10162176 | tf_op jit(solution)/shard_map/pallas_call | solution.py:308
  85.0 0.1 collective-permute-start.19
  85.1 1.9 %collective-permute-done.19.got_ref = f32[512,256]{1,0:T(8,128)S(1)} collective-permute-done((f32[512,256]{1,0:T(8,128)S(1)}, f32[512,256]{1,0:T(8,128)S(1)}, u32[]{:S(2)}, u32[]{:S(2)}) %collective-permute-start.19) | collective-permute-done | bytes 524320 | tf_op jit(solution)/shard_map/ppermute | solution.py:204
  87.0 2.2 %shard_map.113 = (f32[512,256]{1,0:T(8,128)}, f32[3072,256]{1,0:T(8,128)}) custom-call(bf16[3072,512]{1,0:T(8,128)(2,1)S(1)} %bitcast.21, f32[3072,256]{1,0:T(8,128)S(1)} %get-tuple-element.70.parent_ref, f32[512,256]{1,0:T(8,128)S(1)} %get-tuple-element.71.part_ref, f32[512,256]{1,0:T(8,128)S(1)} %collective-permute-done.19.got_ref), custom_call_target="tpu_custom_call" | custom-call | flops 805306368 | bytes 11010048 | tf_op jit(solution)/shard_map/pallas_call | solution.py:308
  (2 shorter events, 0.0 us)
Async XLA Ops:
  1.4 15.6 %copy-start.2 = (bf16[1,512,512]{2,1,0:T(8,128)(2,1)S(1)}, bf16[1,512,512]{2,1,0:T(8,128)(2,1)}, u32[]{:S(2)}) copy-start(bf16[1,512,512]{2,1,0:T(8,128)(2,1)} %param.10) | copy-start | bytes 1572868
  6.7 10.2 %collective-permute-start.2 = (bf16[512,256]{1,0:T(8,128)(2,1)S(1)}, bf16[512,256]{1,0:T(8,128)(2,1)S(1)}, u32[]{:S(2)}, u32[]{:S(2)}) collective-permute-start(bf16[512,256]{1,0:T(8,128)(2,1)S(1)} %get-tuple-element.47), channel_id=1, source_target_pairs={{0,1},{1,0},{2,3},{3,2},{4,5},{5,4},{6,7},{7,6},{8,9},{9,8},{10,11... | collective-permute-start | bytes 786440 | tf_op jit(solution)/shard_map/ppermute | solution.py:204
  9.8 11.9 %collective-permute-start = (bf16[512,256]{1,0:T(8,128)(2,1)S(1)}, bf16[512,256]{1,0:T(8,128)(2,1)S(1)}, u32[]{:S(2)}, u32[]{:S(2)}) collective-permute-start(bf16[512,256]{1,0:T(8,128)(2,1)S(1)} %get-tuple-element.42), channel_id=1, source_target_pairs={{0,1},{1,0},{2,3},{3,2},{4,5},{5,4},{6,7},{7,6},{8,9},{9,8},{10,11... | collective-permute-start | bytes 786440 | tf_op jit(solution)/shard_map/ppermute | solution.py:204
  17.3 12.3 %collective-permute-start.3 = (f32[512,256]{1,0:T(8,128)S(1)}, f32[512,256]{1,0:T(8,128)S(1)}, u32[]{:S(2)}, u32[]{:S(2)}) collective-permute-start(f32[512,256]{1,0:T(8,128)S(1)} %shard_map.99.part_ref), channel_id=1, source_target_pairs={{0,2},{2,0},{1,3},{3,1},{4,6},{6,4},{5,7},{7,5},{8,10},{10,8},{9,1... | collective-permute-start | bytes 1572872 | tf_op jit(solution)/shard_map/ppermute | solution.py:204
  22.0 14.0 %collective-permute-start.1 = (f32[512,256]{1,0:T(8,128)S(1)}, f32[512,256]{1,0:T(8,128)S(1)}, u32[]{:S(2)}, u32[]{:S(2)}) collective-permute-start(f32[512,256]{1,0:T(8,128)S(1)} %shard_map.97.part_ref), channel_id=1, source_target_pairs={{0,2},{2,0},{1,3},{3,1},{4,6},{6,4},{5,7},{7,5},{8,10},{10,8},{9,1... | collective-permute-start | bytes 1572872 | tf_op jit(solution)/shard_map/ppermute | solution.py:204
  22.1 7.5 %copy-start = (bf16[1,2560,512]{2,1,0:T(8,128)(2,1)S(1)}, bf16[1,2560,512]{2,1,0:T(8,128)(2,1)}, u32[]{:S(2)}) copy-start(bf16[1,2560,512]{2,1,0:T(8,128)(2,1)} %param.12) | copy-start | bytes 7864324
  30.4 7.4 %collective-permute-start.10 = (bf16[256,256]{1,0:T(8,128)(2,1)S(1)}, bf16[256,256]{1,0:T(8,128)(2,1)S(1)}, u32[]{:S(2)}, u32[]{:S(2)}) collective-permute-start(bf16[256,256]{1,0:T(8,128)(2,1)S(1)} %shard_map.101), channel_id=1, source_target_pairs={{0,1},{1,0},{2,3},{3,2},{4,5},{5,4},{6,7},{7,6},{8,9},{9,8},{10,11... | collective-permute-start | bytes 393224 | tf_op jit(solution)/shard_map/ppermute | solution.py:204
  33.7 11.3 %collective-permute-start.8 = (bf16[384,256]{1,0:T(8,128)(2,1)S(1)}, bf16[384,256]{1,0:T(8,128)(2,1)S(1)}, u32[]{:S(2)}, u32[]{:S(2)}) collective-permute-start(bf16[384,256]{1,0:T(8,128)(2,1)S(1)} %get-tuple-element.53), channel_id=1, source_target_pairs={{0,1},{1,0},{2,3},{3,2},{4,5},{5,4},{6,7},{7,6},{8,9},{9,8},{10,11... | collective-permute-start | bytes 589832 | tf_op jit(solution)/shard_map/ppermute | solution.py:204
  34.0 8.9 %collective-permute-start.9 = (bf16[128,256]{1,0:T(8,128)(2,1)S(1)}, bf16[128,256]{1,0:T(8,128)(2,1)S(1)}, u32[]{:S(2)}, u32[]{:S(2)}) collective-permute-start(bf16[128,256]{1,0:T(8,128)(2,1)S(1)} %get-tuple-element.54), channel_id=1, source_target_pairs={{0,1},{1,0},{2,3},{3,2},{4,5},{5,4},{6,7},{7,6},{8,9},{9,8},{10,11... | collective-permute-start | bytes 196616 | tf_op jit(solution)/shard_map/ppermute | solution.py:204
  35.8 14.7 %collective-permute-start.7 = (bf16[384,256]{1,0:T(8,128)(2,1)S(1)}, bf16[384,256]{1,0:T(8,128)(2,1)S(1)}, u32[]{:S(2)}, u32[]{:S(2)}) collective-permute-start(bf16[384,256]{1,0:T(8,128)(2,1)S(1)} %get-tuple-element.52), channel_id=1, source_target_pairs={{0,1},{1,0},{2,3},{3,2},{4,5},{5,4},{6,7},{7,6},{8,9},{9,8},{10,11... | collective-permute-start | bytes 589832 | tf_op jit(solution)/shard_map/ppermute | solution.py:204
  36.0 16.5 %collective-permute-start.6 = (bf16[384,256]{1,0:T(8,128)(2,1)S(1)}, bf16[384,256]{1,0:T(8,128)(2,1)S(1)}, u32[]{:S(2)}, u32[]{:S(2)}) collective-permute-start(bf16[384,256]{1,0:T(8,128)(2,1)S(1)} %get-tuple-element.51), channel_id=1, source_target_pairs={{0,1},{1,0},{2,3},{3,2},{4,5},{5,4},{6,7},{7,6},{8,9},{9,8},{10,11... | collective-permute-start | bytes 589832 | tf_op jit(solution)/shard_map/ppermute | solution.py:204
  37.8 22.0 %collective-permute-start.5 = (bf16[768,256]{1,0:T(8,128)(2,1)S(1)}, bf16[768,256]{1,0:T(8,128)(2,1)S(1)}, u32[]{:S(2)}, u32[]{:S(2)}) collective-permute-start(bf16[768,256]{1,0:T(8,128)(2,1)S(1)} %get-tuple-element.50), channel_id=1, source_target_pairs={{0,1},{1,0},{2,3},{3,2},{4,5},{5,4},{6,7},{7,6},{8,9},{9,8},{10,11... | collective-permute-start | bytes 1179656 | tf_op jit(solution)/shard_map/ppermute | solution.py:204
  42.9 20.4 %collective-permute-start.4 = (bf16[256,256]{1,0:T(8,128)(2,1)S(1)}, bf16[256,256]{1,0:T(8,128)(2,1)S(1)}, u32[]{:S(2)}, u32[]{:S(2)}) collective-permute-start(bf16[256,256]{1,0:T(8,128)(2,1)S(1)} %get-tuple-element.49), channel_id=1, source_target_pairs={{0,1},{1,0},{2,3},{3,2},{4,5},{5,4},{6,7},{7,6},{8,9},{9,8},{10,11... | collective-permute-start | bytes 393224 | tf_op jit(solution)/shard_map/ppermute | solution.py:204
  44.9 21.3 %collective-permute-start.16 = (bf16[136,256]{1,0:T(8,128)(2,1)S(1)}, bf16[136,256]{1,0:T(8,128)(2,1)S(1)}, u32[]{:S(2)}, u32[]{:S(2)}) collective-permute-start(bf16[136,256]{1,0:T(8,128)(2,1)S(1)} %get-tuple-element.67), channel_id=1, source_target_pairs={{0,28},{4,24},{8,20},{12,16},{16,12},{20,8},{24,4},{28,0},{1,29},{... | collective-permute-start | bytes 208904 | tf_op jit(solution)/shard_map/ppermute | solution.py:208
  50.4 16.6 %collective-permute-start.15 = (bf16[264,256]{1,0:T(8,128)(2,1)S(1)}, bf16[264,256]{1,0:T(8,128)(2,1)S(1)}, u32[]{:S(2)}, u32[]{:S(2)}) collective-permute-start(bf16[264,256]{1,0:T(8,128)(2,1)S(1)} %get-tuple-element.66), channel_id=1, source_target_pairs={{0,28},{4,24},{8,20},{12,16},{16,12},{20,8},{24,4},{28,0},{1,29},{... | collective-permute-start | bytes 405512 | tf_op jit(solution)/shard_map/ppermute | solution.py:208
  52.5 17.1 %collective-permute-start.17 = (bf16[392,256]{1,0:T(8,128)(2,1)S(1)}, bf16[392,256]{1,0:T(8,128)(2,1)S(1)}, u32[]{:S(2)}, u32[]{:S(2)}) collective-permute-start(bf16[392,256]{1,0:T(8,128)(2,1)S(1)} %get-tuple-element.68), channel_id=1, source_target_pairs={{0,24},{4,28},{8,16},{12,20},{16,8},{20,12},{24,0},{28,4},{1,25},{... | collective-permute-start | bytes 602120 | tf_op jit(solution)/shard_map/ppermute | solution.py:208
  59.8 21.0 %collective-permute-start.13 = (bf16[392,256]{1,0:T(8,128)(2,1)S(1)}, bf16[392,256]{1,0:T(8,128)(2,1)S(1)}, u32[]{:S(2)}, u32[]{:S(2)}) collective-permute-start(bf16[392,256]{1,0:T(8,128)(2,1)S(1)} %get-tuple-element.63), channel_id=1, source_target_pairs={{0,12},{4,8},{8,28},{12,24},{16,4},{20,0},{24,20},{28,16},{1,13},{... | collective-permute-start | bytes 602120 | tf_op jit(solution)/shard_map/ppermute | solution.py:208
  63.3 17.5 %collective-permute-start.14 = (bf16[392,256]{1,0:T(8,128)(2,1)S(1)}, bf16[392,256]{1,0:T(8,128)(2,1)S(1)}, u32[]{:S(2)}, u32[]{:S(2)}) collective-permute-start(bf16[392,256]{1,0:T(8,128)(2,1)S(1)} %get-tuple-element.64), channel_id=1, source_target_pairs={{0,20},{4,16},{8,4},{12,0},{16,28},{20,24},{24,12},{28,8},{1,21},{... | collective-permute-start | bytes 602120 | tf_op jit(solution)/shard_map/ppermute | solution.py:208
  65.4 3.3 %copy-start.1 = (bf16[1,3072,512]{2,1,0:T(8,128)(2,1)S(1)}, bf16[1,3072,512]{2,1,0:T(8,128)(2,1)}, u32[]{:S(2)}) copy-start(bf16[1,3072,512]{2,1,0:T(8,128)(2,1)} %param.15) | copy-start | bytes 9437188
  66.2 15.3 %collective-permute-start.11 = (bf16[392,256]{1,0:T(8,128)(2,1)S(1)}, bf16[392,256]{1,0:T(8,128)(2,1)S(1)}, u32[]{:S(2)}, u32[]{:S(2)}) collective-permute-start(bf16[392,256]{1,0:T(8,128)(2,1)S(1)} %get-tuple-element.61), channel_id=1, source_target_pairs={{0,4},{4,0},{8,12},{12,8},{16,20},{20,16},{24,28},{28,24},{1,5},{5... | collective-permute-start | bytes 602120 | tf_op jit(solution)/shard_map/ppermute | solution.py:208
  67.0 14.5 %collective-permute-start.12 = (bf16[392,256]{1,0:T(8,128)(2,1)S(1)}, bf16[392,256]{1,0:T(8,128)(2,1)S(1)}, u32[]{:S(2)}, u32[]{:S(2)}) collective-permute-start(bf16[392,256]{1,0:T(8,128)(2,1)S(1)} %get-tuple-element.62), channel_id=1, source_target_pairs={{0,16},{4,20},{8,0},{12,4},{16,24},{20,28},{24,8},{28,12},{1,17},{... | collective-permute-start | bytes 602120 | tf_op jit(solution)/shard_map/ppermute | solution.py:208
  69.7 14.0 %collective-permute-start.18 = (bf16[392,256]{1,0:T(8,128)(2,1)S(1)}, bf16[392,256]{1,0:T(8,128)(2,1)S(1)}, u32[]{:S(2)}, u32[]{:S(2)}) collective-permute-start(bf16[392,256]{1,0:T(8,128)(2,1)S(1)} %get-tuple-element.69), channel_id=1, source_target_pairs={{0,8},{4,12},{8,24},{12,28},{16,0},{20,4},{24,16},{28,20},{1,9},{5... | collective-permute-start | bytes 602120 | tf_op jit(solution)/shard_map/ppermute | solution.py:208
  85.0 2.0 %collective-permute-start.19 = (f32[512,256]{1,0:T(8,128)S(1)}, f32[512,256]{1,0:T(8,128)S(1)}, u32[]{:S(2)}, u32[]{:S(2)}) collective-permute-start(f32[512,256]{1,0:T(8,128)S(1)} %get-tuple-element.71.part_ref), channel_id=1, source_target_pairs={{0,2},{2,0},{1,3},{3,1},{4,6},{6,4},{5,7},{7,5},{8,10},{10,8},{9,1... | collective-permute-start | bytes 1572872 | tf_op jit(solution)/shard_map/ppermute | solution.py:204

commit v5 on v4

--- a/solution.py
+++ b/solution.py
@@ -151,7 +151,7 @@
         out[(high - low) * BLOCK :, :] = tags.astype(BF16)
 
 
-def add_pieces(per_device, pieces, parent_ref):
+def add_pieces(per_device, pieces, parent_ref, rounded_ref=None):
     for piece in pieces:
         count = piece.shape[0] // BLOCK
         tile = piece[count * BLOCK : count * BLOCK + TAG_ROWS, :BLOCK].astype(F32)
@@ -163,6 +163,8 @@
             def _():
                 at = pl.ds(pl.multiple_of(tag * BLOCK, BLOCK), BLOCK)
                 parent_ref[at, :] += piece[s * BLOCK : (s + 1) * BLOCK, :].astype(F32)
+                if rounded_ref is not None:
+                    rounded_ref[at, :] = parent_ref[at, :].astype(BF16)
 
 
 def early_kernel(per_device, fresh, *refs):
@@ -172,10 +174,16 @@
     add_pieces(per_device, pieces, parent_ref)
 
 
+def middle_kernel(per_device, *refs):
+    pieces, (parent_ref, rounded_ref) = refs[:-3], refs[-2:]
+    add_pieces(per_device, pieces, parent_ref)
+    rounded_ref[...] = parent_ref[...].astype(BF16)
+
+
 def late_kernel(per_device, *refs):
-    flipped_ref, pieces, (parent_ref, coeff_ref) = refs[0], refs[2:-2], refs[-2:]
-    add_pieces(per_device, pieces, parent_ref)
-    coeff_ref[...] = dot(flipped_ref[...], parent_ref[...].astype(BF16))
+    flipped_ref, pieces, (parent_ref, rounded_ref, coeff_ref) = refs[0], refs[3:-3], refs[-3:]
+    add_pieces(per_device, pieces, parent_ref, rounded_ref)
+    coeff_ref[...] = dot(flipped_ref[...], rounded_ref[...])
 
 
 def flip_kernel(basis_ref, out_ref):
@@ -186,7 +194,6 @@
     total = part_ref[...] + got_ref[...]
     coeff_ref[...] = total
     copies = [pltpu.make_async_copy(coeff_ref, coeff_hbm, coeff_sem)]
-    copies[0].start()
     total = total.astype(BF16)
     parts = out_sem.shape[0]
     part = out_ref.shape[0] // parts
@@ -196,6 +203,8 @@
         at = pl.ds(k * part, part)
         copies.append(pltpu.make_async_copy(out_ref.at[at, :], out_hbm.at[at, :], out_sem.at[k]))
         copies[-1].start()
+        if k == 0:
+            copies[0].start()
     for copy in copies:
         copy.wait()
 
@@ -439,7 +448,7 @@
     waves = [[len(pieces) - 1] + list(range(far))]
     waves += [[i for i in range(far, len(pieces) - 2) if i not in (late, *middle)], middle, [late]]
     parent = None
-    for w, keys in enumerate(waves[:-1]):
+    for w, keys in enumerate(waves[:-2]):
         parent = call(
             functools.partial(early_kernel, per_device, w == 0),
             [pieces[k] for k in keys] + ([parent] if w else []),
@@ -449,17 +458,26 @@
             1e9,
             **({"input_output_aliases": {len(keys): 0}} if w else {}),
         )[0]
-    parent, coeff = call(
+    parent, rounded = call(
+        functools.partial(middle_kernel, per_device),
+        [pieces[k] for k in waves[-2]] + [parent],
+        [VMEM] * (1 + len(waves[-2])),
+        (shape(rows, half, F32), shape(rows, half, BF16)),
+        [VMEM] * 2,
+        1e9,
+        input_output_aliases={len(waves[-2]): 0},
+    )
+    parent, _, coeff = call(
         functools.partial(late_kernel, per_device),
-        [flipped, parent] + [pieces[k] for k in waves[-1]],
-        [VMEM] * (2 + len(waves[-1])),
-        (shape(rows, half, F32), shape(rank, half, F32)),
-        [VMEM] * 2,
+        [flipped, parent, rounded] + [pieces[k] for k in waves[-1]],
+        [VMEM] * (3 + len(waves[-1])),
+        (shape(rows, half, F32), shape(rows, half, BF16), shape(rank, half, F32)),
+        [VMEM] * 3,
         2 * basis.size * half,
-        input_output_aliases={1: 0},
+        input_output_aliases={1: 0, 2: 1},
     )
     got = swap(coeff, "row")
-    steps = 6 if per_device % 6 == 0 else 1
+    steps = 8 if per_device % 8 == 0 else 1
     coefficients, residual = call(
         residual_kernel,
         (basis, parent, coeff, got),

time: 89.3 us -> 89.4 us (level)
  transfers between devices with their start and end apart: 20 -> 20, of which waited for: 7 -> 7; matrix products, arithmetic and copies ran while one was open for 0% -> 0% of each run, Pallas kernels for 22% -> 23%
where the time goes in v5:
time: 89.4 us; the launch traced here: 89.3 us
  waiting for transfers between devices  31.1 us (35%)
  Pallas kernels  29.2 us (33%)
  starting transfers between devices  27.3 us (31%)
  between operations  1.54 us (2%)
    pallas_call x19, Pallas kernels, call(): pl.pallas_call(kernel, out_shape=tuple(outs), in_specs=specs, out_specs=t...  29.2 us
    ppermute x12, waiting for transfers between devices, swap(): lax.ppermute(x, axis, [(i, i ^ 1) for i in range(lax.axis_size(axis))])  20.6 us
    ppermute x8, starting transfers between devices, away(): lax.ppermute(x, 'front', [(i, j) for i in range(fronts) for j in range(fr...  16 us
    ppermute x12, starting transfers between devices, swap(): lax.ppermute(x, axis, [(i, i ^ 1) for i in range(lax.axis_size(axis))])  11.3 us
    ppermute x8, waiting for transfers between devices, away(): lax.ppermute(x, 'front', [(i, j) for i in range(fronts) for j in range(fr...  10.5 us
  transfers between devices with their start and end apart: 20, of which 7 were waited for; matrix products, arithmetic and copies ran while one was open for 0% of the time, Pallas kernels for 23%

profile of v5, /device:TPU:0, one launch (start us, length us, event | category | flops | bytes accessed | tf_op | source)
XLA Modules:
  0.0 89.3 jit_solution(12451565179655750726)
XLA Ops:
  1.3 0.1 pad_add_fusion.ids_ref
  1.4 5.4 %shard_map.96 = (bf16[512,256]{1,0:T(8,128)(2,1)S(1)}, bf16[512,256]{1,0:T(8,128)(2,1)S(1)}, f32[512,256]{1,0:T(8,128)S(1)}, f32[512,256]{1,0:T(8,128)S(1)}, bf1...) custom-call(s32[3]{0:T(128)S(1)} %pad_add_fusion.ids_ref, ...), custom_call_target="tpu_custom_call" | custom-call | flops 1342177280 | bytes 27787652 | tf_op jit(solution)/shard_map/pallas_call | solution.py:317
  6.7 3.0 %collective-permute-start.2 = (bf16[512,256]{1,0:T(8,128)(2,1)S(1)}, bf16[512,256]{1,0:T(8,128)(2,1)S(1)}, u32[]{:S(2)}, u32[]{:S(2)}) collective-permute-start(bf16[512,256]{1,0:T(8,128)(2,1)S(1)} %get-tuple-element.49), channel_id=1, source_target_pairs={{0,1},{1,0},{2,3},{3,2},{4,5},{5,4},{6,7},{7,6},{8,9},{9,8},{10,11... | collective-permute-start | bytes 786440 | tf_op jit(solution)/shard_map/ppermute | solution.py:213
  9.8 0.1 collective-permute-start
  9.8 7.1 %collective-permute-done.2.got_ref = bf16[512,256]{1,0:T(8,128)(2,1)S(1)} collective-permute-done((bf16[512,256]{1,0:T(8,128)(2,1)S(1)}, bf16[512,256]{1,0:T(8,128)(2,1)S(1)}, u32[]{:S(2)}, u32[]{:S(2)}) %collective-permute-start.2) | collective-permute-done | bytes 262176 | tf_op jit(solution)/shard_map/ppermute | solution.py:213
  16.9 0.0 copy-done.2
  16.9 0.3 shard_map.99.part_ref
  17.3 0.1 collective-permute-start.3
  17.3 4.4 %collective-permute-done.got_ref = bf16[512,256]{1,0:T(8,128)(2,1)S(1)} collective-permute-done((bf16[512,256]{1,0:T(8,128)(2,1)S(1)}, bf16[512,256]{1,0:T(8,128)(2,1)S(1)}, u32[]{:S(2)}, u32[]{:S(2)}) %collective-permute-start) | collective-permute-done | bytes 262176 | tf_op jit(solution)/shard_map/ppermute | solution.py:213
  21.7 0.3 shard_map.97.part_ref
  22.0 0.1 collective-permute-start.1
  22.1 0.0 copy-start
  22.1 7.5 %shard_map.98 = (f32[2560,256]{1,0:T(8,128)S(1)}, f32[2560,256]{1,0:T(8,128)S(1)}) custom-call(bf16[2560,2560]{1,0:T(8,128)(2,1)} %bitcast.25, bf16[1024,2560]{1,0:T(8,128)(2,1)S(1)} %get-tuple-element.45.head_ref, bf16[2560,512]{1,0:T(8,128)(2,1)S(1)} %get-tuple-element.46.masked_ref), custom_call_target="tpu_custom_call" | custom-call | flops 6710886400 | bytes 26214400 | tf_op jit(solution)/shard_map/pallas_call | solution.py:317
  29.6 0.0 collective-permute-done.3.got_ref
  29.6 0.0 copy-done
  29.6 0.8 shard_map.101
  30.4 1.8 %collective-permute-start.10 = (bf16[256,256]{1,0:T(8,128)(2,1)S(1)}, bf16[256,256]{1,0:T(8,128)(2,1)S(1)}, u32[]{:S(2)}, u32[]{:S(2)}) collective-permute-start(bf16[256,256]{1,0:T(8,128)(2,1)S(1)} %shard_map.101), channel_id=1, source_target_pairs={{0,1},{1,0},{2,3},{3,2},{4,5},{5,4},{6,7},{7,6},{8,9},{9,8},{10,11... | collective-permute-start | bytes 393224 | tf_op jit(solution)/shard_map/ppermute | solution.py:213
  32.2 1.5 %shard_map.100 = (bf16[128,256]{1,0:T(8,128)(2,1)S(1)}, bf16[384,256]{1,0:T(8,128)(2,1)S(1)}, bf16[384,256]{1,0:T(8,128)(2,1)S(1)}, bf16[384,256]{1,0:T(8,128)(2...) custom-call(s32[20]{0:T(128)S(1)} %get-tuple-element.40.order_ref, ...), custom_call_target="tpu_custom_call" | custom-call | flops 671088640 | bytes 7471184 | tf_op jit(solution)/shard_map/pallas_call | solution.py:317
  33.7 0.3 collective-permute-start.8
  34.0 1.7 %collective-permute-start.9 = (bf16[128,256]{1,0:T(8,128)(2,1)S(1)}, bf16[128,256]{1,0:T(8,128)(2,1)S(1)}, u32[]{:S(2)}, u32[]{:S(2)}) collective-permute-start(bf16[128,256]{1,0:T(8,128)(2,1)S(1)} %get-tuple-element.56), channel_id=1, source_target_pairs={{0,1},{1,0},{2,3},{3,2},{4,5},{5,4},{6,7},{7,6},{8,9},{9,8},{10,11... | collective-permute-start | bytes 196616 | tf_op jit(solution)/shard_map/ppermute | solution.py:213
  35.8 0.3 collective-permute-start.7
  36.0 0.0 collective-permute-done.1.row_ref
  36.0 1.7 %collective-permute-start.6 = (bf16[384,256]{1,0:T(8,128)(2,1)S(1)}, bf16[384,256]{1,0:T(8,128)(2,1)S(1)}, u32[]{:S(2)}, u32[]{:S(2)}) collective-permute-start(bf16[384,256]{1,0:T(8,128)(2,1)S(1)} %get-tuple-element.53), channel_id=1, source_target_pairs={{0,1},{1,0},{2,3},{3,2},{4,5},{5,4},{6,7},{7,6},{8,9},{9,8},{10,11... | collective-permute-start | bytes 589832 | tf_op jit(solution)/shard_map/ppermute | solution.py:213
  37.8 0.0 collective-permute-done.10.refs_0_
  37.8 0.8 collective-permute-start.5
  38.5 0.8 shard_map.102
  39.3 3.6 %collective-permute-done.9.refs_0_ = bf16[128,256]{1,0:T(8,128)(2,1)S(1)} collective-permute-done((bf16[128,256]{1,0:T(8,128)(2,1)S(1)}, bf16[128,256]{1,0:T(8,128)(2,1)S(1)}, u32[]{:S(2)}, u32[]{:S(2)}) %collective-permute-start.9) | collective-permute-done | bytes 65568 | tf_op jit(solution)/shard_map/ppermute | solution.py:213
  42.9 1.2 %collective-permute-start.4 = (bf16[256,256]{1,0:T(8,128)(2,1)S(1)}, bf16[256,256]{1,0:T(8,128)(2,1)S(1)}, u32[]{:S(2)}, u32[]{:S(2)}) collective-permute-start(bf16[256,256]{1,0:T(8,128)(2,1)S(1)} %get-tuple-element.51), channel_id=1, source_target_pairs={{0,1},{1,0},{2,3},{3,2},{4,5},{5,4},{6,7},{7,6},{8,9},{9,8},{10,11... | collective-permute-start | bytes 393224 | tf_op jit(solution)/shard_map/ppermute | solution.py:213
  44.2 0.8 shard_map.103
  44.9 0.0 collective-permute-done.8.refs_0_
  44.9 4.6 %collective-permute-start.16 = (bf16[136,256]{1,0:T(8,128)(2,1)S(1)}, bf16[136,256]{1,0:T(8,128)(2,1)S(1)}, u32[]{:S(2)}, u32[]{:S(2)}) collective-permute-start(bf16[136,256]{1,0:T(8,128)(2,1)S(1)} %get-tuple-element.69), channel_id=1, source_target_pairs={{0,28},{4,24},{8,20},{12,16},{16,12},{20,8},{24,4},{28,0},{1,29},{... | collective-permute-start | bytes 208904 | tf_op jit(solution)/shard_map/ppermute | solution.py:217
  49.6 0.9 shard_map.104
  50.4 0.0 collective-permute-done.7.refs_0_
  50.4 1.2 %collective-permute-start.15 = (bf16[264,256]{1,0:T(8,128)(2,1)S(1)}, bf16[264,256]{1,0:T(8,128)(2,1)S(1)}, u32[]{:S(2)}, u32[]{:S(2)}) collective-permute-start(bf16[264,256]{1,0:T(8,128)(2,1)S(1)} %get-tuple-element.68), channel_id=1, source_target_pairs={{0,28},{4,24},{8,20},{12,16},{16,12},{20,8},{24,4},{28,0},{1,29},{... | collective-permute-start | bytes 405512 | tf_op jit(solution)/shard_map/ppermute | solution.py:217
  51.7 0.9 shard_map.105
  52.5 0.0 collective-permute-done.6.refs_0_
  52.5 2.6 %collective-permute-start.17 = (bf16[392,256]{1,0:T(8,128)(2,1)S(1)}, bf16[392,256]{1,0:T(8,128)(2,1)S(1)}, u32[]{:S(2)}, u32[]{:S(2)}) collective-permute-start(bf16[392,256]{1,0:T(8,128)(2,1)S(1)} %get-tuple-element.70), channel_id=1, source_target_pairs={{0,24},{4,28},{8,16},{12,20},{16,8},{20,12},{24,0},{28,4},{1,25},{... | collective-permute-start | bytes 602120 | tf_op jit(solution)/shard_map/ppermute | solution.py:217
  55.2 0.9 shard_map.106
  56.1 3.7 %collective-permute-done.5.refs_0_ = bf16[768,256]{1,0:T(8,128)(2,1)S(1)} collective-permute-done((bf16[768,256]{1,0:T(8,128)(2,1)S(1)}, bf16[768,256]{1,0:T(8,128)(2,1)S(1)}, u32[]{:S(2)}, u32[]{:S(2)}) %collective-permute-start.5) | collective-permute-done | bytes 393248 | tf_op jit(solution)/shard_map/ppermute | solution.py:213
  59.8 2.5 %collective-permute-start.13 = (bf16[392,256]{1,0:T(8,128)(2,1)S(1)}, bf16[392,256]{1,0:T(8,128)(2,1)S(1)}, u32[]{:S(2)}, u32[]{:S(2)}) collective-permute-start(bf16[392,256]{1,0:T(8,128)(2,1)S(1)} %get-tuple-element.65), channel_id=1, source_target_pairs={{0,12},{4,8},{8,28},{12,24},{16,4},{20,0},{24,20},{28,16},{1,13},{... | collective-permute-start | bytes 602120 | tf_op jit(solution)/shard_map/ppermute | solution.py:217
  62.3 1.0 %shard_map.107 = (bf16[2560,256]{1,0:T(8,128)(2,1)S(1)}, bf16[392,256]{1,0:T(8,128)(2,1)S(1)}, bf16[392,256]{1,0:T(8,128)(2,1)S(1)}) custom-call(s32[20]{0:T(128)S(1)} %get-tuple-element.40.order_ref, s32[9]{0:T(128)S(1)} %get-tuple-element.41.offset_ref, s32[44]{0:T(128)S(1)} %get-tuple-element.42.tag_ref, ...), custom_call_target="tpu_custom_call", output_to_operand_aliasing={{0}: (8, {})} | custom-call | flops 1000000000 | bytes 9707812 | tf_op jit(solution)/shard_map/pallas_call | solution.py:317
  63.3 0.0 collective-permute-done.4.refs_0_
  63.3 2.1 %collective-permute-start.14 = (bf16[392,256]{1,0:T(8,128)(2,1)S(1)}, bf16[392,256]{1,0:T(8,128)(2,1)S(1)}, u32[]{:S(2)}, u32[]{:S(2)}) collective-permute-start(bf16[392,256]{1,0:T(8,128)(2,1)S(1)} %get-tuple-element.66), channel_id=1, source_target_pairs={{0,20},{4,16},{8,4},{12,0},{16,28},{20,24},{24,12},{28,8},{1,21},{... | collective-permute-start | bytes 602120 | tf_op jit(solution)/shard_map/ppermute | solution.py:217
  65.4 0.8 shard_map.108
  66.2 0.0 collective-permute-done.16.refs_2_
  66.2 0.8 collective-permute-start.11
  67.0 0.0 collective-permute-done.15.refs_1_
  67.0 1.7 %collective-permute-start.12 = (bf16[392,256]{1,0:T(8,128)(2,1)S(1)}, bf16[392,256]{1,0:T(8,128)(2,1)S(1)}, u32[]{:S(2)}, u32[]{:S(2)}) collective-permute-start(bf16[392,256]{1,0:T(8,128)(2,1)S(1)} %get-tuple-element.64), channel_id=1, source_target_pairs={{0,16},{4,20},{8,0},{12,4},{16,24},{20,28},{24,8},{28,12},{1,17},{... | collective-permute-start | bytes 602120 | tf_op jit(solution)/shard_map/ppermute | solution.py:217
  68.7 0.0 copy-done.1
  68.7 0.9 %shard_map.95.refs_0_ = bf16[512,3072]{1,0:T(8,128)(2,1)S(1)} custom-call(bf16[3072,512]{1,0:T(8,128)(2,1)S(1)} %bitcast.20), custom_call_target="tpu_custom_call" | custom-call | flops 1000000000 | bytes 6291456 | tf_op jit(solution)/shard_map/pallas_call | solution.py:317
  69.7 0.0 collective-permute-done.17.refs_3_
  69.7 0.4 collective-permute-start.18
  70.1 1.3 %shard_map.109.refs_2_ = f32[3072,256]{1,0:T(8,128)S(1)} custom-call(bf16[392,256]{1,0:T(8,128)(2,1)S(1)} %get-tuple-element.67.refs_0_, bf16[264,256]{1,0:T(8,128)(2,1)S(1)} %collective-permute-done.15.refs_1_, bf16[136,256]{1,0:T(8,128)(2,1)S(1)} %collective-permute-done.16.refs_2_, bf16[392,256]{1,0:T(8,128)(2,1)S(1)} %collective-permute-done.17.refs_3_), custom_call_target="tpu_custom_call" | custom-call | flops 1000000000 | bytes 3751936 | tf_op jit(solution)/shard_map/pallas_call | solution.py:317
  71.4 9.3 %collective-permute-done.13.refs_0_ = bf16[392,256]{1,0:T(8,128)(2,1)S(1)} collective-permute-done((bf16[392,256]{1,0:T(8,128)(2,1)S(1)}, bf16[392,256]{1,0:T(8,128)(2,1)S(1)}, u32[]{:S(2)}, u32[]{:S(2)}) %collective-permute-start.13) | collective-permute-done | bytes 200736 | tf_op jit(solution)/shard_map/ppermute | solution.py:217
  80.7 0.0 collective-permute-done.14.refs_1_
  80.7 0.8 shard_map.110.refs_2_
  81.5 0.0 collective-permute-done.11.refs_0_
  81.5 0.0 collective-permute-done.12.refs_1_
  81.5 1.0 %shard_map.111 = (f32[3072,256]{1,0:T(8,128)S(1)}, bf16[3072,256]{1,0:T(8,128)(2,1)S(1)}) custom-call(bf16[392,256]{1,0:T(8,128)(2,1)S(1)} %collective-permute-done.11.refs_0_, bf16[392,256]{1,0:T(8,128)(2,1)S(1)} %collective-permute-done.12.refs_1_, f32[3072,256]{1,0:T(8,128)S(1)} %shard_map.110.refs_2_), custom_call_target="tpu_custom_call", output_to_operand_aliasing={{0}: (2, {})} | custom-call | flops 1000000000 | bytes 8265728 | tf_op jit(solution)/shard_map/pallas_call | solution.py:317
  82.5 1.1 %collective-permute-done.18.refs_3_ = bf16[392,256]{1,0:T(8,128)(2,1)S(1)} collective-permute-done((bf16[392,256]{1,0:T(8,128)(2,1)S(1)}, bf16[392,256]{1,0:T(8,128)(2,1)S(1)}, u32[]{:S(2)}, u32[]{:S(2)}) %collective-permute-start.18) | collective-permute-done | bytes 200736 | tf_op jit(solution)/shard_map/ppermute | solution.py:217
  83.6 1.4 %shard_map.112 = (f32[3072,256]{1,0:T(8,128)S(1)}, bf16[3072,256]{1,0:T(8,128)(2,1)S(1)}, f32[512,256]{1,0:T(8,128)S(1)}) custom-call(bf16[512,3072]{1,0:T(8,128)(2,1)S(1)} %shard_map.95.refs_0_, f32[3072,256]{1,0:T(8,128)S(1)} %get-tuple-element.71.refs_1_, ...), custom_call_target="tpu_custom_call", output_to_operand_aliasing={{0}: (1, {}), {1}: (2, {})} | custom-call | flops 805306368 | bytes 13307904 | tf_op jit(solution)/shard_map/pallas_call | solution.py:317
  85.0 0.1 collective-permute-start.19
  85.1 1.9 %collective-permute-done.19.got_ref = f32[512,256]{1,0:T(8,128)S(1)} collective-permute-done((f32[512,256]{1,0:T(8,128)S(1)}, f32[512,256]{1,0:T(8,128)S(1)}, u32[]{:S(2)}, u32[]{:S(2)}) %collective-permute-start.19) | collective-permute-done | bytes 524320 | tf_op jit(solution)/shard_map/ppermute | solution.py:213
  87.0 2.3 %shard_map.113 = (f32[512,256]{1,0:T(8,128)}, f32[3072,256]{1,0:T(8,128)}) custom-call(bf16[3072,512]{1,0:T(8,128)(2,1)S(1)} %bitcast.21, f32[3072,256]{1,0:T(8,128)S(1)} %get-tuple-element.74.parent_ref, f32[512,256]{1,0:T(8,128)S(1)} %get-tuple-element.75.part_ref, f32[512,256]{1,0:T(8,128)S(1)} %collective-permute-done.19.got_ref), custom_call_target="tpu_custom_call" | custom-call | flops 805306368 | bytes 11010048 | tf_op jit(solution)/shard_map/pallas_call | solution.py:317
  (2 shorter events, 0.0 us)
Async XLA Ops:
  1.4 15.6 %copy-start.2 = (bf16[1,512,512]{2,1,0:T(8,128)(2,1)S(1)}, bf16[1,512,512]{2,1,0:T(8,128)(2,1)}, u32[]{:S(2)}) copy-start(bf16[1,512,512]{2,1,0:T(8,128)(2,1)} %param.10) | copy-start | bytes 1572868
  6.7 10.2 %collective-permute-start.2 = (bf16[512,256]{1,0:T(8,128)(2,1)S(1)}, bf16[512,256]{1,0:T(8,128)(2,1)S(1)}, u32[]{:S(2)}, u32[]{:S(2)}) collective-permute-start(bf16[512,256]{1,0:T(8,128)(2,1)S(1)} %get-tuple-element.49), channel_id=1, source_target_pairs={{0,1},{1,0},{2,3},{3,2},{4,5},{5,4},{6,7},{7,6},{8,9},{9,8},{10,11... | collective-permute-start | bytes 786440 | tf_op jit(solution)/shard_map/ppermute | solution.py:213
  9.8 11.9 %collective-permute-start = (bf16[512,256]{1,0:T(8,128)(2,1)S(1)}, bf16[512,256]{1,0:T(8,128)(2,1)S(1)}, u32[]{:S(2)}, u32[]{:S(2)}) collective-permute-start(bf16[512,256]{1,0:T(8,128)(2,1)S(1)} %get-tuple-element.44), channel_id=1, source_target_pairs={{0,1},{1,0},{2,3},{3,2},{4,5},{5,4},{6,7},{7,6},{8,9},{9,8},{10,11... | collective-permute-start | bytes 786440 | tf_op jit(solution)/shard_map/ppermute | solution.py:213
  17.3 12.3 %collective-permute-start.3 = (f32[512,256]{1,0:T(8,128)S(1)}, f32[512,256]{1,0:T(8,128)S(1)}, u32[]{:S(2)}, u32[]{:S(2)}) collective-permute-start(f32[512,256]{1,0:T(8,128)S(1)} %shard_map.99.part_ref), channel_id=1, source_target_pairs={{0,2},{2,0},{1,3},{3,1},{4,6},{6,4},{5,7},{7,5},{8,10},{10,8},{9,1... | collective-permute-start | bytes 1572872 | tf_op jit(solution)/shard_map/ppermute | solution.py:213
  22.0 14.0 %collective-permute-start.1 = (f32[512,256]{1,0:T(8,128)S(1)}, f32[512,256]{1,0:T(8,128)S(1)}, u32[]{:S(2)}, u32[]{:S(2)}) collective-permute-start(f32[512,256]{1,0:T(8,128)S(1)} %shard_map.97.part_ref), channel_id=1, source_target_pairs={{0,2},{2,0},{1,3},{3,1},{4,6},{6,4},{5,7},{7,5},{8,10},{10,8},{9,1... | collective-permute-start | bytes 1572872 | tf_op jit(solution)/shard_map/ppermute | solution.py:213
  22.1 7.5 %copy-start = (bf16[1,2560,512]{2,1,0:T(8,128)(2,1)S(1)}, bf16[1,2560,512]{2,1,0:T(8,128)(2,1)}, u32[]{:S(2)}) copy-start(bf16[1,2560,512]{2,1,0:T(8,128)(2,1)} %param.12) | copy-start | bytes 7864324
  30.4 7.4 %collective-permute-start.10 = (bf16[256,256]{1,0:T(8,128)(2,1)S(1)}, bf16[256,256]{1,0:T(8,128)(2,1)S(1)}, u32[]{:S(2)}, u32[]{:S(2)}) collective-permute-start(bf16[256,256]{1,0:T(8,128)(2,1)S(1)} %shard_map.101), channel_id=1, source_target_pairs={{0,1},{1,0},{2,3},{3,2},{4,5},{5,4},{6,7},{7,6},{8,9},{9,8},{10,11... | collective-permute-start | bytes 393224 | tf_op jit(solution)/shard_map/ppermute | solution.py:213
  33.7 11.3 %collective-permute-start.8 = (bf16[384,256]{1,0:T(8,128)(2,1)S(1)}, bf16[384,256]{1,0:T(8,128)(2,1)S(1)}, u32[]{:S(2)}, u32[]{:S(2)}) collective-permute-start(bf16[384,256]{1,0:T(8,128)(2,1)S(1)} %get-tuple-element.55), channel_id=1, source_target_pairs={{0,1},{1,0},{2,3},{3,2},{4,5},{5,4},{6,7},{7,6},{8,9},{9,8},{10,11... | collective-permute-start | bytes 589832 | tf_op jit(solution)/shard_map/ppermute | solution.py:213
  34.0 8.9 %collective-permute-start.9 = (bf16[128,256]{1,0:T(8,128)(2,1)S(1)}, bf16[128,256]{1,0:T(8,128)(2,1)S(1)}, u32[]{:S(2)}, u32[]{:S(2)}) collective-permute-start(bf16[128,256]{1,0:T(8,128)(2,1)S(1)} %get-tuple-element.56), channel_id=1, source_target_pairs={{0,1},{1,0},{2,3},{3,2},{4,5},{5,4},{6,7},{7,6},{8,9},{9,8},{10,11... | collective-permute-start | bytes 196616 | tf_op jit(solution)/shard_map/ppermute | solution.py:213
  35.8 14.7 %collective-permute-start.7 = (bf16[384,256]{1,0:T(8,128)(2,1)S(1)}, bf16[384,256]{1,0:T(8,128)(2,1)S(1)}, u32[]{:S(2)}, u32[]{:S(2)}) collective-permute-start(bf16[384,256]{1,0:T(8,128)(2,1)S(1)} %get-tuple-element.54), channel_id=1, source_target_pairs={{0,1},{1,0},{2,3},{3,2},{4,5},{5,4},{6,7},{7,6},{8,9},{9,8},{10,11... | collective-permute-start | bytes 589832 | tf_op jit(solution)/shard_map/ppermute | solution.py:213
  36.0 16.5 %collective-permute-start.6 = (bf16[384,256]{1,0:T(8,128)(2,1)S(1)}, bf16[384,256]{1,0:T(8,128)(2,1)S(1)}, u32[]{:S(2)}, u32[]{:S(2)}) collective-permute-start(bf16[384,256]{1,0:T(8,128)(2,1)S(1)} %get-tuple-element.53), channel_id=1, source_target_pairs={{0,1},{1,0},{2,3},{3,2},{4,5},{5,4},{6,7},{7,6},{8,9},{9,8},{10,11... | collective-permute-start | bytes 589832 | tf_op jit(solution)/shard_map/ppermute | solution.py:213
  37.8 22.0 %collective-permute-start.5 = (bf16[768,256]{1,0:T(8,128)(2,1)S(1)}, bf16[768,256]{1,0:T(8,128)(2,1)S(1)}, u32[]{:S(2)}, u32[]{:S(2)}) collective-permute-start(bf16[768,256]{1,0:T(8,128)(2,1)S(1)} %get-tuple-element.52), channel_id=1, source_target_pairs={{0,1},{1,0},{2,3},{3,2},{4,5},{5,4},{6,7},{7,6},{8,9},{9,8},{10,11... | collective-permute-start | bytes 1179656 | tf_op jit(solution)/shard_map/ppermute | solution.py:213
  42.9 20.4 %collective-permute-start.4 = (bf16[256,256]{1,0:T(8,128)(2,1)S(1)}, bf16[256,256]{1,0:T(8,128)(2,1)S(1)}, u32[]{:S(2)}, u32[]{:S(2)}) collective-permute-start(bf16[256,256]{1,0:T(8,128)(2,1)S(1)} %get-tuple-element.51), channel_id=1, source_target_pairs={{0,1},{1,0},{2,3},{3,2},{4,5},{5,4},{6,7},{7,6},{8,9},{9,8},{10,11... | collective-permute-start | bytes 393224 | tf_op jit(solution)/shard_map/ppermute | solution.py:213
  44.9 21.3 %collective-permute-start.16 = (bf16[136,256]{1,0:T(8,128)(2,1)S(1)}, bf16[136,256]{1,0:T(8,128)(2,1)S(1)}, u32[]{:S(2)}, u32[]{:S(2)}) collective-permute-start(bf16[136,256]{1,0:T(8,128)(2,1)S(1)} %get-tuple-element.69), channel_id=1, source_target_pairs={{0,28},{4,24},{8,20},{12,16},{16,12},{20,8},{24,4},{28,0},{1,29},{... | collective-permute-start | bytes 208904 | tf_op jit(solution)/shard_map/ppermute | solution.py:217
  50.4 16.6 %collective-permute-start.15 = (bf16[264,256]{1,0:T(8,128)(2,1)S(1)}, bf16[264,256]{1,0:T(8,128)(2,1)S(1)}, u32[]{:S(2)}, u32[]{:S(2)}) collective-permute-start(bf16[264,256]{1,0:T(8,128)(2,1)S(1)} %get-tuple-element.68), channel_id=1, source_target_pairs={{0,28},{4,24},{8,20},{12,16},{16,12},{20,8},{24,4},{28,0},{1,29},{... | collective-permute-start | bytes 405512 | tf_op jit(solution)/shard_map/ppermute | solution.py:217
  52.5 17.1 %collective-permute-start.17 = (bf16[392,256]{1,0:T(8,128)(2,1)S(1)}, bf16[392,256]{1,0:T(8,128)(2,1)S(1)}, u32[]{:S(2)}, u32[]{:S(2)}) collective-permute-start(bf16[392,256]{1,0:T(8,128)(2,1)S(1)} %get-tuple-element.70), channel_id=1, source_target_pairs={{0,24},{4,28},{8,16},{12,20},{16,8},{20,12},{24,0},{28,4},{1,25},{... | collective-permute-start | bytes 602120 | tf_op jit(solution)/shard_map/ppermute | solution.py:217
  59.8 21.0 %collective-permute-start.13 = (bf16[392,256]{1,0:T(8,128)(2,1)S(1)}, bf16[392,256]{1,0:T(8,128)(2,1)S(1)}, u32[]{:S(2)}, u32[]{:S(2)}) collective-permute-start(bf16[392,256]{1,0:T(8,128)(2,1)S(1)} %get-tuple-element.65), channel_id=1, source_target_pairs={{0,12},{4,8},{8,28},{12,24},{16,4},{20,0},{24,20},{28,16},{1,13},{... | collective-permute-start | bytes 602120 | tf_op jit(solution)/shard_map/ppermute | solution.py:217
  63.3 17.5 %collective-permute-start.14 = (bf16[392,256]{1,0:T(8,128)(2,1)S(1)}, bf16[392,256]{1,0:T(8,128)(2,1)S(1)}, u32[]{:S(2)}, u32[]{:S(2)}) collective-permute-start(bf16[392,256]{1,0:T(8,128)(2,1)S(1)} %get-tuple-element.66), channel_id=1, source_target_pairs={{0,20},{4,16},{8,4},{12,0},{16,28},{20,24},{24,12},{28,8},{1,21},{... | collective-permute-start | bytes 602120 | tf_op jit(solution)/shard_map/ppermute | solution.py:217
  65.4 3.3 %copy-start.1 = (bf16[1,3072,512]{2,1,0:T(8,128)(2,1)S(1)}, bf16[1,3072,512]{2,1,0:T(8,128)(2,1)}, u32[]{:S(2)}) copy-start(bf16[1,3072,512]{2,1,0:T(8,128)(2,1)} %param.15) | copy-start | bytes 9437188
  66.2 15.3 %collective-permute-start.11 = (bf16[392,256]{1,0:T(8,128)(2,1)S(1)}, bf16[392,256]{1,0:T(8,128)(2,1)S(1)}, u32[]{:S(2)}, u32[]{:S(2)}) collective-permute-start(bf16[392,256]{1,0:T(8,128)(2,1)S(1)} %get-tuple-element.63), channel_id=1, source_target_pairs={{0,4},{4,0},{8,12},{12,8},{16,20},{20,16},{24,28},{28,24},{1,5},{5... | collective-permute-start | bytes 602120 | tf_op jit(solution)/shard_map/ppermute | solution.py:217
  67.0 14.5 %collective-permute-start.12 = (bf16[392,256]{1,0:T(8,128)(2,1)S(1)}, bf16[392,256]{1,0:T(8,128)(2,1)S(1)}, u32[]{:S(2)}, u32[]{:S(2)}) collective-permute-start(bf16[392,256]{1,0:T(8,128)(2,1)S(1)} %get-tuple-element.64), channel_id=1, source_target_pairs={{0,16},{4,20},{8,0},{12,4},{16,24},{20,28},{24,8},{28,12},{1,17},{... | collective-permute-start | bytes 602120 | tf_op jit(solution)/shard_map/ppermute | solution.py:217
  69.7 14.0 %collective-permute-start.18 = (bf16[392,256]{1,0:T(8,128)(2,1)S(1)}, bf16[392,256]{1,0:T(8,128)(2,1)S(1)}, u32[]{:S(2)}, u32[]{:S(2)}) collective-permute-start(bf16[392,256]{1,0:T(8,128)(2,1)S(1)} %get-tuple-element.73), channel_id=1, source_target_pairs={{0,8},{4,12},{8,24},{12,28},{16,0},{20,4},{24,16},{28,20},{1,9},{5... | collective-permute-start | bytes 602120 | tf_op jit(solution)/shard_map/ppermute | solution.py:217
  85.0 2.0 %collective-permute-start.19 = (f32[512,256]{1,0:T(8,128)S(1)}, f32[512,256]{1,0:T(8,128)S(1)}, u32[]{:S(2)}, u32[]{:S(2)}) collective-permute-start(f32[512,256]{1,0:T(8,128)S(1)} %get-tuple-element.75.part_ref), channel_id=1, source_target_pairs={{0,2},{2,0},{1,3},{3,1},{4,6},{6,4},{5,7},{7,5},{8,10},{10,8},{9,1... | collective-permute-start | bytes 1572872 | tf_op jit(solution)/shard_map/ppermute | solution.py:213
